TPU v7x, 128 devices: a whole 4x4x4 slice. The times are simulated.
128 devices in a mesh: dp: 1, wy: 16 (over z, y), wx: 8 (over x, core).
Axes of the slice: x: 4, y: 4, z: 4, core: 2. Of those that a mesh axis runs over, the one named last changes fastest.
Arguments:
- x_tokens: bfloat16 [128, 256, 2048], P(('dp', 'wy', 'wx'))
- gamma_ln: float32 [2, 2048], replicated
- w_q: bfloat16 [2, 2048, 2048], P(None, 'wx', 'wy')
- w_kv: bfloat16 [2, 2048, 2, 128], P(None, 'wx')
- w_gu: bfloat16 [2, 2048, 2, 8192], P(None, 'wx', None, 'wy')
- w_o: bfloat16 [2, 2048, 2048], P(None, 'wy', 'wx')
- w_d: bfloat16 [2, 8192, 2048], P(None, 'wy', 'wx')
Outputs:
- output 1: bfloat16 [128, 256, 2048], P(('dp', 'wy', 'wx'))
- output 2: bfloat16 [2, 128, 256, 128], P(None, ('dp', 'wy', 'wx'))
- output 3: bfloat16 [2, 128, 256, 128], P(None, ('dp', 'wy', 'wx'))
All inputs are finite; a program needn't handle non-finite values.
Results may differ from a plain program's by a relative error of at most 0.0150521.
Values are sent between devices in bfloat16 or wider.
A program may use at most 1 GiB of HBM per device.

v0:
```python
import jax
import jax.numpy as jnp
from jax import lax
from jax.sharding import PartitionSpec as P

LN_EPS = 1e-6
ROPE_BASE = 10000.0


def rope_tables(seq_len, head_dim):
    half_dim = head_dim // 2
    inv_freq = ROPE_BASE ** (-2.0 * jnp.arange(half_dim, dtype=jnp.float32) / head_dim)
    angles = jnp.arange(seq_len, dtype=jnp.float32)[:, None] * inv_freq[None, :]
    return jnp.cos(angles), jnp.sin(angles)


def rotate(values_in, cos_tab, sin_tab):
    half_dim = values_in.shape[-1] // 2
    first_half = values_in[..., :half_dim].astype(jnp.float32)
    second_half = values_in[..., half_dim:].astype(jnp.float32)
    rotated = jnp.concatenate([first_half * cos_tab - second_half * sin_tab, second_half * cos_tab + first_half * sin_tab], axis=-1)
    return rotated.astype(jnp.bfloat16)


def layer_norm(resid, g_scale):
    resid_f = resid.astype(jnp.float32)
    centered = resid_f - jnp.mean(resid_f, axis=-1, keepdims=True)
    variance = jnp.mean(centered * centered, axis=-1, keepdims=True)
    return (centered * lax.rsqrt(variance + LN_EPS) * g_scale).astype(jnp.bfloat16)


def causal_attention(q_rot, k_rot, v_val):
    seq_len = q_rot.shape[1]
    score_scale = q_rot.shape[-1] ** -0.5
    scores = jnp.einsum('bshe,bte->bhst', q_rot, k_rot, preferred_element_type=jnp.float32) * score_scale
    allowed = jnp.arange(seq_len)[:, None] >= jnp.arange(seq_len)[None, :]
    scores = jnp.where(allowed, scores, -jnp.inf)
    attn_probs = jax.nn.softmax(scores, axis=-1).astype(jnp.bfloat16)
    attended = jnp.einsum('bhst,bte->bshe', attn_probs, v_val, preferred_element_type=jnp.float32)
    return attended.astype(jnp.bfloat16)


def decoder_layer(resid, g_scale, w_q, w_kv, w_gu, w_o, w_d, cos_tab, sin_tab):
    batch_loc, seq_len = resid.shape[0], resid.shape[1]
    head_dim = w_kv.shape[-1]
    normed = layer_norm(resid, g_scale)
    q_proj = jnp.einsum('bsd,dn->bsn', normed, w_q, preferred_element_type=jnp.float32).astype(jnp.bfloat16)
    kv_proj = jnp.einsum('bsd,dce->bsce', normed, w_kv, preferred_element_type=jnp.float32).astype(jnp.bfloat16)
    gu_proj = jnp.einsum('bsd,dcf->bscf', normed, w_gu, preferred_element_type=jnp.float32).astype(jnp.bfloat16)
    q_rot = rotate(q_proj.reshape(batch_loc, seq_len, -1, head_dim), cos_tab[:, None, :], sin_tab[:, None, :])
    k_rot = rotate(kv_proj[:, :, 0], cos_tab, sin_tab)
    v_val = kv_proj[:, :, 1]
    attended = causal_attention(q_rot, k_rot, v_val).reshape(batch_loc, seq_len, -1)
    hidden = (jax.nn.silu(gu_proj[:, :, 0].astype(jnp.float32)) * gu_proj[:, :, 1].astype(jnp.float32)).astype(jnp.bfloat16)
    mixed = jnp.einsum('bsn,nd->bsd', attended, w_o, preferred_element_type=jnp.float32) + jnp.einsum('bsf,fd->bsd', hidden, w_d, preferred_element_type=jnp.float32)
    return (resid.astype(jnp.float32) + mixed).astype(jnp.bfloat16), k_rot, v_val


def solution(mesh):
    batch_axes = ('dp', 'wy', 'wx')
    in_specs = (P(batch_axes), P(), P(None, 'wx', 'wy'), P(None, 'wx'), P(None, 'wx', None, 'wy'), P(None, 'wy', 'wx'), P(None, 'wy', 'wx'))
    out_specs = (P(batch_axes), P(None, batch_axes), P(None, batch_axes))

    def device_step(x_tokens, gamma_ln, w_q, w_kv, w_gu, w_o, w_d):
        cos_tab, sin_tab = rope_tables(x_tokens.shape[1], w_kv.shape[-1])
        resid = x_tokens
        key_list = []
        value_list = []
        for layer_idx in range(w_q.shape[0]):
            full_q = lax.all_gather(lax.all_gather(w_q[layer_idx], 'wy', axis=1, tiled=True), 'wx', axis=0, tiled=True)
            full_kv = lax.all_gather(w_kv[layer_idx], 'wx', axis=0, tiled=True)
            full_gu = lax.all_gather(lax.all_gather(w_gu[layer_idx], 'wy', axis=2, tiled=True), 'wx', axis=0, tiled=True)
            full_o = lax.all_gather(lax.all_gather(w_o[layer_idx], 'wy', axis=0, tiled=True), 'wx', axis=1, tiled=True)
            full_d = lax.all_gather(lax.all_gather(w_d[layer_idx], 'wy', axis=0, tiled=True), 'wx', axis=1, tiled=True)
            resid, k_rot, v_val = decoder_layer(resid, gamma_ln[layer_idx], full_q, full_kv, full_gu, full_o, full_d, cos_tab, sin_tab)
            key_list.append(k_rot)
            value_list.append(v_val)
        return resid, jnp.stack(key_list), jnp.stack(value_list)

    return jax.shard_map(device_step, mesh=mesh, in_specs=in_specs, out_specs=out_specs, check_vma=False)
```

profile of v0, /device:TPU:1, one launch (start us, length us, event | category | flops | bytes accessed | tf_op | source)
XLA Modules:
  0.0 1672.9 jit_solution(16598142725286699807)
XLA Ops:
  7.2 1.6 fusion.183
  8.9 1.5 fusion.182
  10.5 1.9 fusion.177
  12.4 0.8 copy.46
  13.4 0.8 fusion.180
  15.4 0.8 copy.50
  17.3 0.8 copy.43
  18.1 37.2 %all-gather.39.cloned.1.call-done = bf16[1,256,2048]{2,1,0:T(8,128)(2,1)} async-done(((bf16[1,256,128]{2,1,0:T(8,128)(2,1)}), bf16[1,256,2048]{2,1,0:T(8,128)(2,1)}) %all-gather.39.cloned.1.call-update) | async-done | bytes 1048592 | tf_op jit(solution)/shard_map/all_gather | solution.py:70
  55.4 43.7 %all-gather.43.cloned.1.call-done = bf16[1,2048,256]{2,1,0:T(8,128)(2,1)} async-done(((bf16[1,128,256]{2,1,0:T(8,128)(2,1)}), bf16[1,2048,256]{2,1,0:T(8,128)(2,1)}) %all-gather.43.cloned.1.call-update) | async-done | bytes 1048592 | tf_op jit(solution)/shard_map/all_gather | solution.py:73
  99.2 78.8 %all-gather.47.cloned.1.call-done = bf16[1,256,2,8192]{3,1,2,0:T(8,128)(2,1)} async-done(((bf16[1,256,2,512]{3,1,2,0:T(8,128)(2,1)}), bf16[1,256,2,8192]{3,1,2,0:T(8,128)(2,1)}) %all-gather.47.cloned.1.call-update) | async-done | bytes 8388624 | tf_op jit(solution)/shard_map/all_gather | solution.py:72
  178.0 53.5 %all-gather.51.cloned.1.call-done = bf16[1,8192,256]{2,1,0:T(8,128)(2,1)} async-done(((bf16[1,512,256]{2,1,0:T(8,128)(2,1)}), bf16[1,8192,256]{2,1,0:T(8,128)(2,1)}) %all-gather.51.cloned.1.call-update) | async-done | bytes 4194320 | tf_op jit(solution)/shard_map/all_gather | solution.py:74
  231.6 0.8 copy.47
  232.5 42.3 %all-gather.57.cloned.1.call-done = bf16[1,256,2048]{2,1,0:T(8,128)(2,1)} async-done(((bf16[1,256,128]{2,1,0:T(8,128)(2,1)}), bf16[1,256,2048]{2,1,0:T(8,128)(2,1)}) %all-gather.57.cloned.1.call-update) | async-done | bytes 1048592 | tf_op jit(solution)/shard_map/all_gather | solution.py:70
  274.9 43.5 %all-gather.61.cloned.1.call-done = bf16[1,2048,256]{2,1,0:T(8,128)(2,1)} async-done(((bf16[1,128,256]{2,1,0:T(8,128)(2,1)}), bf16[1,2048,256]{2,1,0:T(8,128)(2,1)}) %all-gather.61.cloned.1.call-update) | async-done | bytes 1048592 | tf_op jit(solution)/shard_map/all_gather | solution.py:73
  318.5 78.2 %all-gather.65.cloned.1.call-done = bf16[1,256,2,8192]{3,1,2,0:T(8,128)(2,1)} async-done(((bf16[1,256,2,512]{3,1,2,0:T(8,128)(2,1)}), bf16[1,256,2,8192]{3,1,2,0:T(8,128)(2,1)}) %all-gather.65.cloned.1.call-update) | async-done | bytes 8388624 | tf_op jit(solution)/shard_map/all_gather | solution.py:72
  397.3 53.1 %all-gather.69.cloned.1.call-done = bf16[1,8192,256]{2,1,0:T(8,128)(2,1)} async-done(((bf16[1,512,256]{2,1,0:T(8,128)(2,1)}), bf16[1,8192,256]{2,1,0:T(8,128)(2,1)}) %all-gather.69.cloned.1.call-update) | async-done | bytes 4194320 | tf_op jit(solution)/shard_map/all_gather | solution.py:74
  451.7 24.3 %all-gather.37.cloned.1.call-done = bf16[1,2048,2,128]{1,3,2,0:T(8,128)(2,1)} async-done(((bf16[1,256,2,128]{1,3,2,0:T(8,128)(2,1)}), bf16[1,2048,2,128]{1,3,2,0:T(8,128)(2,1)}) %all-gather.37.cloned.1.call-update) | async-done | bytes 1048592 | tf_op jit(solution)/shard_map/all_gather | solution.py:71
  476.0 1.8 fusion.141
  478.9 49.2 %all-gather.41.cloned.1.call-done = bf16[1,2048,2048]{2,1,0:T(8,128)(2,1)} async-done(((bf16[1,256,2048]{2,1,0:T(8,128)(2,1)}), bf16[1,2048,2048]{2,1,0:T(8,128)(2,1)}) %all-gather.41.cloned.1.call-update) | async-done | bytes 8388624 | tf_op jit(solution)/shard_map/all_gather | solution.py:70
  528.1 5.8 fusion.120
  534.6 0.8 fusion.126
  535.3 1.3 fusion.44
  536.7 0.9 fusion.42
  537.5 1.3 fusion.114
  538.9 44.0 %all-gather.45.cloned.1.call-done = bf16[1,2048,2048]{2,1,0:T(8,128)(2,1)} async-done(((bf16[1,2048,256]{2,1,0:T(8,128)(2,1)}), bf16[1,2048,2048]{2,1,0:T(8,128)(2,1)}) %all-gather.45.cloned.1.call-update) | async-done | bytes 8388624 | tf_op jit(solution)/shard_map/all_gather | solution.py:73
  582.9 7.1 fusion.32
  589.9 292.8 %all-gather.49.cloned.1.call-done = bf16[1,2048,2,8192]{3,1,2,0:T(8,128)(2,1)} async-done(((bf16[1,256,2,8192]{3,1,2,0:T(8,128)(2,1)}), bf16[1,2048,2,8192]{3,1,2,0:T(8,128)(2,1)}) %all-gather.49.cloned.1.call-update) | async-done | bytes 67108880 | tf_op jit(solution)/shard_map/all_gather | solution.py:72
  882.7 30.6 %fusion.17 = bf16[1,256,2,8192]{3,1,2,0:T(8,128)(2,1)} fusion(bf16[1,2048,2,8192]{3,1,2,0:T(8,128)(2,1)} %all-gather.49.cloned.1.call-done, bf16[1,256,2048]{2,1,0:T(8,128)(2,1)S(1)} %copy-done, f32[2048]{0:T(1024)S(1)} %bitcast.274, f32[256]{0:T(256)S(1)} %add_rsqrt_fusion.1, f32[256]{0:T(256)S(1)} %broadcast_multiply_fusion.1), kind=kOutput, calls=%fused_computation.11 | convolution fusion | flops 17186684928 | bytes 76556288 | tf_op jit(solution)/shard_map/bsd,dcf->bscf/dot_general | solution.py:49
  913.3 134.8 %all-gather.53.cloned.1.call-done = bf16[1,8192,2048]{2,1,0:T(8,128)(2,1)} async-done(((bf16[1,8192,256]{2,1,0:T(8,128)(2,1)}), bf16[1,8192,2048]{2,1,0:T(8,128)(2,1)}) %all-gather.53.cloned.1.call-update) | async-done | bytes 33554448 | tf_op jit(solution)/shard_map/all_gather | solution.py:74
  1048.1 19.5 %convert_reduce_fusion = (f32[256]{0:T(256)S(1)}, bf16[1,256,2048]{2,1,0:T(8,128)(2,1)S(1)}) fusion(f32[256,2048]{1,0:T(8,128)} %fusion.32, bf16[1,8192,2048]{2,1,0:T(8,128)(2,1)} %all-gather.53.cloned.1.call-done, bf16[1,256,2,8192]{3,1,2,0:T(8,128)(2,1)} %fusion.17, bf16[1,256,2048]{2,1,0:T(8,128)(2,1)S(1)} %copy-done), kind=kOutput, calls=%fused_computation.52 | convolution fusion | flops 8609857536 | bytes 46138368 | tf_op jit(solution)/shard_map/bsf,fd->bsd/dot_general | solution.py:55
  1068.0 6.2 all-gather.55.cloned.1.call-done
  1074.2 1.8 fusion.137
  1077.1 0.8 copy.35
  1077.9 48.4 %all-gather.59.cloned.1.call-done = bf16[1,2048,2048]{2,1,0:T(8,128)(2,1)} async-done(((bf16[1,256,2048]{2,1,0:T(8,128)(2,1)}), bf16[1,2048,2048]{2,1,0:T(8,128)(2,1)}) %all-gather.59.cloned.1.call-update) | async-done | bytes 8388624 | tf_op jit(solution)/shard_map/all_gather | solution.py:70
  1126.3 5.8 fusion.77
  1132.6 0.9 fusion.178
  1133.9 1.5 copy.49
  1135.5 1.5 pad_maximum_fusion
  1137.0 1.7 copy.36
  1139.4 1.3 fusion.45
  1140.7 0.9 fusion.43
  1141.6 1.3 fusion.117
  1142.9 38.0 %all-gather.63.cloned.1.call-done = bf16[1,2048,2048]{2,1,0:T(8,128)(2,1)} async-done(((bf16[1,2048,256]{2,1,0:T(8,128)(2,1)}), bf16[1,2048,2048]{2,1,0:T(8,128)(2,1)}) %all-gather.63.cloned.1.call-update) | async-done | bytes 8388624 | tf_op jit(solution)/shard_map/all_gather | solution.py:73
  1180.9 7.0 fusion.28
  1188.0 292.8 %all-gather.67.cloned.1.call-done = bf16[1,2048,2,8192]{3,1,2,0:T(8,128)(2,1)} async-done(((bf16[1,256,2,8192]{3,1,2,0:T(8,128)(2,1)}), bf16[1,2048,2,8192]{3,1,2,0:T(8,128)(2,1)}) %all-gather.67.cloned.1.call-update) | async-done | bytes 67108880 | tf_op jit(solution)/shard_map/all_gather | solution.py:72
  1480.7 30.7 %fusion.14 = bf16[1,256,2,8192]{3,1,2,0:T(8,128)(2,1)} fusion(bf16[1,2048,2,8192]{3,1,2,0:T(8,128)(2,1)} %all-gather.67.cloned.1.call-done, bf16[1,256,2048]{2,1,0:T(8,128)(2,1)S(1)} %get-tuple-element.42, f32[2048]{0:T(1024)S(1)} %bitcast.271, f32[256]{0:T(256)S(1)} %add_rsqrt_fusion, f32[256]{0:T(256)S(1)} %broadcast_multiply_fusion), kind=kOutput, calls=%fused_computation.10 | convolution fusion | flops 17186684928 | bytes 76556288 | tf_op jit(solution)/shard_map/bsd,dcf->bscf/dot_general | solution.py:49
  1511.5 134.5 %all-gather.71.cloned.1.call-done = bf16[1,8192,2048]{2,1,0:T(8,128)(2,1)} async-done(((bf16[1,8192,256]{2,1,0:T(8,128)(2,1)}), bf16[1,8192,2048]{2,1,0:T(8,128)(2,1)}) %all-gather.71.cloned.1.call-update) | async-done | bytes 33554448 | tf_op jit(solution)/shard_map/all_gather | solution.py:74
  1646.0 19.8 %fusion.85 = bf16[1,256,2048]{2,1,0:T(8,128)(2,1)} fusion(f32[256,2048]{1,0:T(8,128)} %fusion.28, bf16[1,8192,2048]{2,1,0:T(8,128)(2,1)} %all-gather.71.cloned.1.call-done, bf16[1,256,2,8192]{3,1,2,0:T(8,128)(2,1)} %fusion.14, bf16[1,256,2048]{2,1,0:T(8,128)(2,1)S(1)} %get-tuple-element.42), kind=kOutput, calls=%fused_computation.71 | convolution fusion | flops 8608808960 | bytes 46137344 | tf_op jit(solution)/shard_map/bsf,fd->bsd/dot_general | solution.py:55
  (72 shorter events, 9.5 us)
Async XLA Ops:
  7.2 6.2 copy-start.3
  7.2 9.9 copy-start.4
  7.2 48.2 %all-gather.39.cloned.1.call-start = ((), (), s32[]{:S(2)}) async-start(), calls=%async_computation.1 | async-start | bytes 1114112 | tf_op jit(solution)/shard_map/all_gather | solution.py:70
  8.8 90.3 %all-gather.43.cloned.1.call-start = ((), (), s32[]{:S(2)}) async-start(), calls=%async_computation.3 | async-start | bytes 1114112 | tf_op jit(solution)/shard_map/all_gather | solution.py:73
  10.5 167.5 %all-gather.47.cloned.1.call-start = ((), (), s32[]{:S(2)}) async-start(), calls=%async_computation.5 | async-start | bytes 8912896 | tf_op jit(solution)/shard_map/all_gather | solution.py:72
  13.3 218.3 %all-gather.51.cloned.1.call-start = ((), (), s32[]{:S(2)}) async-start(), calls=%async_computation.7 | async-start | bytes 4456448 | tf_op jit(solution)/shard_map/all_gather | solution.py:74
  14.2 260.6 %all-gather.57.cloned.1.call-start = ((), (), s32[]{:S(2)}) async-start(), calls=%async_computation.10 | async-start | bytes 1114112 | tf_op jit(solution)/shard_map/all_gather | solution.py:70
  14.8 303.6 %all-gather.61.cloned.1.call-start = ((), (), s32[]{:S(2)}) async-start(), calls=%async_computation.12 | async-start | bytes 1114112 | tf_op jit(solution)/shard_map/all_gather | solution.py:73
  15.4 381.3 %all-gather.65.cloned.1.call-start = ((), (), s32[]{:S(2)}) async-start(), calls=%async_computation.14 | async-start | bytes 8912896 | tf_op jit(solution)/shard_map/all_gather | solution.py:72
  16.3 434.2 %all-gather.69.cloned.1.call-start = ((), (), s32[]{:S(2)}) async-start(), calls=%async_computation.16 | async-start | bytes 4456448 | tf_op jit(solution)/shard_map/all_gather | solution.py:74
  17.1 459.0 %all-gather.37.cloned.1.call-start = ((), (), s32[]{:S(2)}) async-start(), calls=%async_computation | async-start | bytes 1179648 | tf_op jit(solution)/shard_map/all_gather | solution.py:71
  18.1 510.0 %all-gather.41.cloned.1.call-start = ((), (), s32[]{:S(2)}) async-start(), calls=%async_computation.2 | async-start | bytes 9437184 | tf_op jit(solution)/shard_map/all_gather | solution.py:70
  55.4 527.5 %all-gather.45.cloned.1.call-start = ((), (), s32[]{:S(2)}) async-start(), calls=%async_computation.4 | async-start | bytes 9437184 | tf_op jit(solution)/shard_map/all_gather | solution.py:73
  99.1 783.6 %all-gather.49.cloned.1.call-start = ((), (), s32[]{:S(2)}) async-start(), calls=%async_computation.6 | async-start | bytes 75497472 | tf_op jit(solution)/shard_map/all_gather | solution.py:72
  178.0 870.1 %all-gather.53.cloned.1.call-start = ((), (), s32[]{:S(2)}) async-start(), calls=%async_computation.8 | async-start | bytes 37748736 | tf_op jit(solution)/shard_map/all_gather | solution.py:74
  231.6 842.6 %all-gather.55.cloned.1.call-start = ((), (), s32[]{:S(2)}) async-start(), calls=%async_computation.9 | async-start | bytes 1179648 | tf_op jit(solution)/shard_map/all_gather | solution.py:71
  232.4 893.8 %all-gather.59.cloned.1.call-start = ((), (), s32[]{:S(2)}) async-start(), calls=%async_computation.11 | async-start | bytes 9437184 | tf_op jit(solution)/shard_map/all_gather | solution.py:70
  274.9 906.1 %all-gather.63.cloned.1.call-start = ((), (), s32[]{:S(2)}) async-start(), calls=%async_computation.13 | async-start | bytes 9437184 | tf_op jit(solution)/shard_map/all_gather | solution.py:73
  318.5 1162.3 %all-gather.67.cloned.1.call-start = ((), (), s32[]{:S(2)}) async-start(), calls=%async_computation.15 | async-start | bytes 75497472 | tf_op jit(solution)/shard_map/all_gather | solution.py:72
  396.7 53.8 %copy-start = (bf16[1,256,2048]{2,1,0:T(8,128)(2,1)S(1)}, bf16[1,256,2048]{2,1,0:T(8,128)(2,1)}, u32[]{:S(2)}) copy-start(bf16[1,256,2048]{2,1,0:T(8,128)(2,1)} %param.7) | copy-start | bytes 3145732
  396.7 55.0 %copy-start.5 = (f32[2,2048]{1,0:T(2,128)S(1)}, f32[2,2048]{1,0:T(2,128)}, u32[]{:S(2)}) copy-start(f32[2,2048]{1,0:T(2,128)} %param.8) | copy-start | bytes 49156
  396.8 1249.2 %all-gather.71.cloned.1.call-start = ((), (), s32[]{:S(2)}) async-start(), calls=%async_computation.17 | async-start | bytes 37748736 | tf_op jit(solution)/shard_map/all_gather | solution.py:74
  1076.1 1.8 copy-start.1
  1139.3 2.2 copy-start.2
Sparse Core Ops, SparseCore 0:
  10.7 44.6 all-gather.38
  57.5 41.5 all-gather.42
  101.8 76.1 all-gather.46
  180.0 51.5 all-gather.50
  233.5 41.2 all-gather.56
  276.8 41.5 all-gather.60
  320.5 76.1 all-gather.64
  398.8 51.5 all-gather.68
  452.7 23.2 all-gather.36
  477.6 50.4 all-gather.40
  529.7 53.0 all-gather.44
  584.4 298.2 all-gather.48
  884.4 163.6 all-gather.52
  1050.2 24.0 all-gather.54
  1075.8 50.4 all-gather.58
  1127.8 53.0 all-gather.62
  1182.5 298.2 all-gather.66
  1482.3 163.6 all-gather.70
where the time goes:
time: 1680 us; the launch traced here: 1670 us
  waiting for transfers between devices  1500 us (89%)
  matrix products  135 us (8%)
  local copies, waits for them, and re-layouts  17.2 us (1%)
    all_gather x2, waiting for transfers between devices, device_step(): lax.all_gather(lax.all_gather(w_gu[layer_idx], 'wy', axis=2, tiled=True),...  586 us
    all_gather x2, waiting for transfers between devices, device_step(): lax.all_gather(lax.all_gather(w_d[layer_idx], 'wy', axis=0, tiled=True),...  269 us
    all_gather x2, waiting for transfers between devices, device_step(): lax.all_gather(w_gu[layer_idx], 'wy', axis=2, tiled=True)  157 us
    all_gather x2, waiting for transfers between devices, device_step(): lax.all_gather(w_d[layer_idx], 'wy', axis=0, tiled=True)  107 us
    all_gather x2, waiting for transfers between devices, device_step(): lax.all_gather(lax.all_gather(w_q[layer_idx], 'wy', axis=1, tiled=True),...  97.5 us
    all_gather x2, waiting for transfers between devices, device_step(): lax.all_gather(w_o[layer_idx], 'wy', axis=0, tiled=True)  87.2 us
    all_gather x2, waiting for transfers between devices, device_step(): lax.all_gather(lax.all_gather(w_o[layer_idx], 'wy', axis=0, tiled=True),...  82 us
    all_gather x2, waiting for transfers between devices, device_step(): lax.all_gather(w_q[layer_idx], 'wy', axis=1, tiled=True)  79.6 us
  transfers between devices with their start and end apart: 18, of which 18 were waited for; matrix products, arithmetic and copies ran while one was open for 8% of the time, Pallas kernels for 0%

commit v1 on v0

v1 whole, which is shorter than its diff:
```python
import jax
import jax.numpy as jnp
from jax import lax
from jax.sharding import PartitionSpec as P

LN_EPS = 1e-6
ROPE_BASE = 10000.0


def rope_tables(seq_len, head_dim):
    half_dim = head_dim // 2
    inv_freq = ROPE_BASE ** (-2.0 * jnp.arange(half_dim, dtype=jnp.float32) / head_dim)
    angles = jnp.arange(seq_len, dtype=jnp.float32)[:, None] * inv_freq[None, :]
    return jnp.cos(angles), jnp.sin(angles)


def rotate(values_in, cos_tab, sin_tab):
    half_dim = values_in.shape[-1] // 2
    first_half = values_in[..., :half_dim].astype(jnp.float32)
    second_half = values_in[..., half_dim:].astype(jnp.float32)
    rotated = jnp.concatenate([first_half * cos_tab - second_half * sin_tab, second_half * cos_tab + first_half * sin_tab], axis=-1)
    return rotated.astype(jnp.bfloat16)


def layer_norm(resid, g_scale):
    resid_f = resid.astype(jnp.float32)
    centered = resid_f - jnp.mean(resid_f, axis=-1, keepdims=True)
    variance = jnp.mean(centered * centered, axis=-1, keepdims=True)
    return (centered * lax.rsqrt(variance + LN_EPS) * g_scale).astype(jnp.bfloat16)


def causal_attention(q_rot, k_rot, v_val):
    seq_len = q_rot.shape[1]
    score_scale = q_rot.shape[-1] ** -0.5
    scores = jnp.einsum('bshe,bte->bhst', q_rot, k_rot, preferred_element_type=jnp.float32) * score_scale
    allowed = jnp.arange(seq_len)[:, None] >= jnp.arange(seq_len)[None, :]
    scores = jnp.where(allowed, scores, -jnp.inf)
    attn_probs = jax.nn.softmax(scores, axis=-1).astype(jnp.bfloat16)
    attended = jnp.einsum('bhst,bte->bshe', attn_probs, v_val, preferred_element_type=jnp.float32)
    return attended.astype(jnp.bfloat16)


def solution(mesh):
    batch_axes = ('dp', 'wy', 'wx')
    in_specs = (P(batch_axes), P(), P(None, 'wx', 'wy'), P(None, 'wx'), P(None, 'wx', None, 'wy'), P(None, 'wy', 'wx'), P(None, 'wy', 'wx'))
    out_specs = (P(batch_axes), P(None, batch_axes), P(None, batch_axes))
    n_wy, n_wx = mesh.shape['wy'], mesh.shape['wx']
    per = n_wy // n_wx
    perm = []
    for iy in range(n_wy):
        for ix in range(n_wx):
            perm.append((iy * n_wx + ix, ((iy % per) * n_wx + ix) * n_wx + iy // per))

    def device_step(x_tokens, gamma_ln, w_q, w_kv, w_gu, w_o, w_d):
        seq_len, d_model = x_tokens.shape[1], x_tokens.shape[2]
        head_dim = w_kv.shape[-1]
        d_loc = w_q.shape[1]
        f_loc = w_gu.shape[-1]
        n_layers = w_q.shape[0]
        cos_tab, sin_tab = rope_tables(seq_len, head_dim)
        iy = lax.axis_index('wy')
        ix = lax.axis_index('wx')
        weights_a, weights_b = [], []
        for layer_idx in range(n_layers):
            kv_half = lax.dynamic_index_in_dim(w_kv[layer_idx], lax.rem(iy, per), axis=1, keepdims=False)
            pack_a = jnp.concatenate([w_gu[layer_idx].reshape(d_loc, 2 * f_loc), w_q[layer_idx], kv_half], axis=1)
            pack_b = jnp.concatenate([w_d[layer_idx], w_o[layer_idx]], axis=0)
            pack_a = lax.ppermute(pack_a, ('wy', 'wx'), perm)
            pack_b = lax.ppermute(pack_b, ('wy', 'wx'), perm)
            full_a = lax.all_gather(pack_a, 'wy', axis=0, tiled=True)
            full_b = lax.all_gather(pack_b, 'wy', axis=0, tiled=True)
            weights_a.append(full_a.reshape(per, d_model, 2 * f_loc + 2 * head_dim))
            weights_b.append(full_b.reshape(per, n_wx, f_loc + head_dim, d_loc))
        resid = x_tokens[0]
        key_list = []
        value_list = []
        for layer_idx in range(n_layers):
            wa, wb = weights_a[layer_idx], weights_b[layer_idx]
            normed = layer_norm(resid, gamma_ln[layer_idx])
            h_all = lax.all_gather(normed, 'wx', axis=0, tiled=True)
            proj = [jnp.dot(h_all, wa[hh], preferred_element_type=jnp.float32).astype(jnp.bfloat16) for hh in range(per)]
            q_all = jnp.stack([p[:, 2 * f_loc:2 * f_loc + head_dim] for p in proj], axis=1).reshape(n_wx, seq_len, per, head_dim)
            k_all = proj[0][:, 2 * f_loc + head_dim:].reshape(n_wx, seq_len, head_dim)
            v_all = proj[1][:, 2 * f_loc + head_dim:].reshape(n_wx, seq_len, head_dim)
            q_rot = rotate(q_all, cos_tab[:, None, :], sin_tab[:, None, :])
            k_rot = rotate(k_all, cos_tab, sin_tab)
            attended = causal_attention(q_rot, k_rot, v_all)
            total = None
            for hh in range(per):
                g_f = proj[hh][:, :f_loc].astype(jnp.float32)
                u_f = proj[hh][:, f_loc:2 * f_loc].astype(jnp.float32)
                hidden = (jax.nn.silu(g_f) * u_f).astype(jnp.bfloat16)
                lhs = jnp.concatenate([hidden, attended[:, :, hh].reshape(n_wx * seq_len, head_dim)], axis=1)
                rhs = jnp.transpose(wb[hh], (1, 0, 2)).reshape(f_loc + head_dim, d_model)
                part = jnp.dot(lhs, rhs, preferred_element_type=jnp.float32)
                total = part if total is None else total + part
            mixed = lax.psum_scatter(total, 'wx', scatter_dimension=0, tiled=True)
            resid = (resid.astype(jnp.float32) + mixed).astype(jnp.bfloat16)
            key_list.append(lax.dynamic_index_in_dim(k_rot, ix, axis=0, keepdims=True))
            value_list.append(lax.dynamic_index_in_dim(v_all, ix, axis=0, keepdims=True))
        return resid[None], jnp.stack(key_list), jnp.stack(value_list)

    return jax.shard_map(device_step, mesh=mesh, in_specs=in_specs, out_specs=out_specs, check_vma=False)
```

time: 1680 us -> 815 us (0.49)
  waiting for transfers between devices: 1500 us -> 586 us
  local copies, waits for them, and re-layouts: 17.2 us -> 47.5 us
  other arithmetic: 7.06 us -> 30.9 us
  matrix products: 135 us -> 113 us
  starting transfers between devices: 1.24 us -> 18.4 us
    all_gather x18 -> x6, waiting for transfers between devices: 1500 us -> 337 us  [the longest x2 150 us: device_step(): full_a = lax.all_gather(pack_a, 'wy', axis=0, tiled=True)]
    reduce_scatter x0 -> x2, waiting for transfers between devices: none -> 164 us  [device_step(): mixed = lax.psum_scatter(total, 'wx', scatter_dimension=0, tiled=True)]
    ppermute x0 -> x4, waiting for transfers between devices: none -> 84.9 us  [the longest x2 54 us: device_step(): pack_a = lax.ppermute(pack_a, ('wy', 'wx'), perm)]
    transpose x0 -> x4, local copies, waits for them, and re-layouts: none -> 18.2 us  [device_step(): rhs = jnp.transpose(wb[hh], (1, 0, 2)).reshape(f_loc + head_dim, d_model)]
    ppermute x0 -> x4, starting transfers between devices: none -> 18 us  [the longest x2 9.51 us: device_step(): pack_a = lax.ppermute(pack_a, ('wy', 'wx'), perm)]
  transfers between devices with their start and end apart: 18 -> 12, of which waited for: 18 -> 12; matrix products, arithmetic and copies ran while one was open for 8% -> 6% of each run, Pallas kernels for 0% -> 0%
where the time goes in v1:
time: 815 us; the launch traced here: 811 us
  waiting for transfers between devices  586 us (72%)
  matrix products  113 us (14%)
  local copies, waits for them, and re-layouts  47.5 us (6%)
  other arithmetic  30.9 us (4%)
  starting transfers between devices  18.4 us (2%)
  between operations  14.8 us (2%)
    reduce_scatter x2, waiting for transfers between devices, device_step(): mixed = lax.psum_scatter(total, 'wx', scatter_dimension=0, tiled=True)  164 us
    all_gather x2, waiting for transfers between devices, device_step(): full_a = lax.all_gather(pack_a, 'wy', axis=0, tiled=True)  150 us
    all_gather x2, waiting for transfers between devices, device_step(): full_b = lax.all_gather(pack_b, 'wy', axis=0, tiled=True)  97.5 us
    all_gather x2, waiting for transfers between devices, device_step(): h_all = lax.all_gather(normed, 'wx', axis=0, tiled=True)  89.9 us
    dot_general x4, matrix products, device_step(): jnp.dot(h_all, wa[hh], preferred_element_type=jnp.float32)  57.1 us
    ppermute x2, waiting for transfers between devices, device_step(): pack_a = lax.ppermute(pack_a, ('wy', 'wx'), perm)  54 us
    dot_general x4, matrix products, device_step(): part = jnp.dot(lhs, rhs, preferred_element_type=jnp.float32)  52.6 us
    ppermute x2, waiting for transfers between devices, device_step(): pack_b = lax.ppermute(pack_b, ('wy', 'wx'), perm)  30.9 us
  transfers between devices with their start and end apart: 12, of which 12 were waited for; matrix products, arithmetic and copies ran while one was open for 6% of the time, Pallas kernels for 0%

profile of v1, /device:TPU:1, one launch (start us, length us, event | category | flops | bytes accessed | tf_op | source)
XLA Modules:
  0.0 810.7 jit_solution(3576563985063768932)
XLA Ops:
  7.3 1.9 slice_bitcast_fusion.1
  9.2 1.5 slice_bitcast_fusion.4
  10.7 4.6 collective-permute-start.1
  15.3 15.2 %collective-permute-done.1 = bf16[640,256]{1,0:T(8,128)(2,1)S(1)} collective-permute-done((bf16[640,256]{1,0:T(8,128)(2,1)S(1)}, bf16[640,256]{1,0:T(8,128)(2,1)S(1)}, u32[]{:S(2)}, u32[]{:S(2)}) %collective-permute-start.1) | collective-permute-done | bytes 327712 | tf_op jit(solution)/shard_map/ppermute | solution.py:69
  31.4 1.4 convert_reduce_fusion.1
  32.8 1.7 fusion.51
  34.5 1.4 fusion.53
  36.5 1.5 fusion.121
  38.8 5.5 collective-permute-start
  44.3 30.8 %collective-permute-done = bf16[256,1280]{1,0:T(8,128)(2,1)S(1)} collective-permute-done((bf16[256,1280]{1,0:T(8,128)(2,1)S(1)}, bf16[256,1280]{1,0:T(8,128)(2,1)S(1)}, u32[]{:S(2)}, u32[]{:S(2)}) %collective-permute-start) | collective-permute-done | bytes 655392 | tf_op jit(solution)/shard_map/ppermute | solution.py:68
  77.2 41.2 %all-gather.11.cloned.1.call-done = bf16[10240,256]{1,0:T(8,128)(2,1)} async-done(((bf16[640,256]{1,0:T(8,128)(2,1)}), bf16[10240,256]{1,0:T(8,128)(2,1)}) %all-gather.11.cloned.1.call-update) | async-done | bytes 5242896 | tf_op jit(solution)/shard_map/all_gather | solution.py:71
  118.4 5.2 fusion.117
  123.6 4.5 copy.42
  128.1 4.4 copy.44
  132.6 37.8 %all-gather.7.cloned.1.call-done = bf16[2048,2048]{1,0:T(8,128)(2,1)} async-done(((bf16[256,2048]{1,0:T(8,128)(2,1)}), bf16[2048,2048]{1,0:T(8,128)(2,1)}) %all-gather.7.cloned.1.call-update) | async-done | bytes 8388624 | tf_op jit(solution)/shard_map/all_gather | solution.py:80
  170.4 82.2 %all-gather.9.cloned.1.call-done = bf16[4096,1280]{1,0:T(8,128)(2,1)} async-done(((bf16[256,1280]{1,0:T(8,128)(2,1)}), bf16[4096,1280]{1,0:T(8,128)(2,1)}) %all-gather.9.cloned.1.call-update) | async-done | bytes 10485776 | tf_op jit(solution)/shard_map/all_gather | solution.py:70
  252.6 15.3 %convolution_convert_fusion.3 = bf16[2048,1280]{1,0:T(8,128)(2,1)S(1)} fusion(bf16[2048,2048]{1,0:T(8,128)(2,1)} %all-gather.7.cloned.1.call-done, bf16[4096,1280]{1,0:T(8,128)(2,1)} %all-gather.9.cloned.1.call-done), kind=kOutput, calls=%fused_computation.7 | convolution fusion | flops 10740039680 | bytes 18874368 | tf_op jit(solution)/shard_map/dot_general | solution.py:81
  268.0 2.6 fusion.25
  270.7 13.2 %convolution_convert_fusion.2 = bf16[2048,1280]{1,0:T(8,128)(2,1)S(1)} fusion(bf16[2048,2048]{1,0:T(8,128)(2,1)} %all-gather.7.cloned.1.call-done, bf16[4096,1280]{1,0:T(8,128)(2,1)S(1)} %copy-done.22), kind=kOutput, calls=%fused_computation.6 | convolution fusion | flops 10740039680 | bytes 18874368 | tf_op jit(solution)/shard_map/dot_general | solution.py:81
  284.0 2.6 fusion.24
  288.1 1.1 fusion.85
  289.1 1.4 fusion.125
  292.5 12.6 %fusion.30 = f32[2048,2048]{1,0:T(8,128)} fusion(bf16[640,2048]{0,1:T(8,128)(2,1)} %bitcast.154, bf16[2048,128]{1,0:T(8,128)(2,1)} %bitcast.169, bf16[2048,512]{1,0:T(8,128)(2,1)} %fusion.25), kind=kOutput, calls=%fused_computation.63 | convolution fusion | flops 5373952000 | bytes 22020096 | tf_op jit(solution)/shard_map/dot_general | solution.py:95
  305.1 13.7 %convolution_add_fusion.1 = f32[2048,2048]{1,0:T(8,128)} fusion(f32[2048,2048]{1,0:T(8,128)} %fusion.30, bf16[640,2048]{0,1:T(8,128)(2,1)S(1)} %bitcast.153, bf16[2048,128]{1,0:T(8,128)(2,1)S(1)} %bitcast.167, bf16[2048,512]{1,0:T(8,128)(2,1)S(1)} %copy-done.4), kind=kOutput, calls=%fused_computation.3 | convolution fusion | flops 5378146304 | bytes 38797312 | tf_op jit(solution)/shard_map/dot_general | solution.py:95
  319.8 3.9 collective-permute-start.3
  323.7 15.6 %collective-permute-done.3 = bf16[640,256]{1,0:T(8,128)(2,1)S(1)} collective-permute-done((bf16[640,256]{1,0:T(8,128)(2,1)S(1)}, bf16[640,256]{1,0:T(8,128)(2,1)S(1)}, u32[]{:S(2)}, u32[]{:S(2)}) %collective-permute-start.3) | collective-permute-done | bytes 327712 | tf_op jit(solution)/shard_map/ppermute | solution.py:69
  341.1 4.0 collective-permute-start.2
  345.1 23.3 %collective-permute-done.2 = bf16[256,1280]{1,0:T(8,128)(2,1)S(1)} collective-permute-done((bf16[256,1280]{1,0:T(8,128)(2,1)S(1)}, bf16[256,1280]{1,0:T(8,128)(2,1)S(1)}, u32[]{:S(2)}, u32[]{:S(2)}) %collective-permute-start.2) | collective-permute-done | bytes 655392 | tf_op jit(solution)/shard_map/ppermute | solution.py:68
  369.3 76.0 %reduce-scatter.3.cloned.1.call-done = f32[256,2048]{1,0:T(8,128)} async-done(((f32[2048,2048]{1,0:T(8,128)}), f32[256,2048]{1,0:T(8,128)}) %reduce-scatter.3.cloned.1.call-update) | async-done | bytes 2097168 | tf_op jit(solution)/shard_map/reduce_scatter | solution.py:97
  445.3 1.9 convert_reduce_fusion
  447.7 1.4 fusion.50
  449.1 56.3 %all-gather.17.cloned.1.call-done = bf16[10240,256]{1,0:T(8,128)(2,1)} async-done(((bf16[640,256]{1,0:T(8,128)(2,1)}), bf16[10240,256]{1,0:T(8,128)(2,1)}) %all-gather.17.cloned.1.call-update) | async-done | bytes 5242896 | tf_op jit(solution)/shard_map/all_gather | solution.py:71
  505.4 5.3 fusion.114
  510.7 4.8 copy.51
  515.5 4.4 copy.53
  519.9 67.5 %all-gather.15.cloned.1.call-done = bf16[4096,1280]{1,0:T(8,128)(2,1)} async-done(((bf16[256,1280]{1,0:T(8,128)(2,1)}), bf16[4096,1280]{1,0:T(8,128)(2,1)}) %all-gather.15.cloned.1.call-update) | async-done | bytes 10485776 | tf_op jit(solution)/shard_map/all_gather | solution.py:70
  587.5 52.0 %all-gather.13.cloned.1.call-done = bf16[2048,2048]{1,0:T(8,128)(2,1)} async-done(((bf16[256,2048]{1,0:T(8,128)(2,1)}), bf16[2048,2048]{1,0:T(8,128)(2,1)}) %all-gather.13.cloned.1.call-update) | async-done | bytes 8388624 | tf_op jit(solution)/shard_map/all_gather | solution.py:80
  639.5 15.4 %convolution_convert_fusion.1 = bf16[2048,1280]{1,0:T(8,128)(2,1)S(1)} fusion(bf16[2048,2048]{1,0:T(8,128)(2,1)} %all-gather.13.cloned.1.call-done, bf16[4096,1280]{1,0:T(8,128)(2,1)} %all-gather.15.cloned.1.call-done), kind=kOutput, calls=%fused_computation.5 | convolution fusion | flops 10740039680 | bytes 18874368 | tf_op jit(solution)/shard_map/dot_general | solution.py:81
  654.9 2.6 fusion.23
  657.5 13.2 %convolution_convert_fusion = bf16[2048,1280]{1,0:T(8,128)(2,1)S(1)} fusion(bf16[2048,2048]{1,0:T(8,128)(2,1)} %all-gather.13.cloned.1.call-done, bf16[4096,1280]{1,0:T(8,128)(2,1)S(1)} %copy-done.21), kind=kOutput, calls=%fused_computation.4 | convolution fusion | flops 10740039680 | bytes 18874368 | tf_op jit(solution)/shard_map/dot_general | solution.py:81
  670.8 2.6 fusion.22
  676.0 1.4 fusion.126
  679.0 2.1 copy.50
  681.0 2.1 copy.52
  683.1 12.6 %fusion.37 = f32[2048,2048]{1,0:T(8,128)} fusion(bf16[640,2048]{0,1:T(8,128)(2,1)} %bitcast.152, bf16[2048,128]{1,0:T(8,128)(2,1)} %bitcast.170, bf16[2048,512]{1,0:T(8,128)(2,1)} %fusion.23), kind=kOutput, calls=%fused_computation.70 | convolution fusion | flops 5373952000 | bytes 22020096 | tf_op jit(solution)/shard_map/dot_general | solution.py:95
  695.7 13.7 %convolution_add_fusion = f32[2048,2048]{1,0:T(8,128)} fusion(f32[2048,2048]{1,0:T(8,128)} %fusion.37, bf16[640,2048]{0,1:T(8,128)(2,1)S(1)} %bitcast.151, bf16[2048,128]{1,0:T(8,128)(2,1)S(1)} %bitcast.168, bf16[2048,512]{1,0:T(8,128)(2,1)S(1)} %copy-done.3), kind=kOutput, calls=%fused_computation.2 | convolution fusion | flops 5378146304 | bytes 38797312 | tf_op jit(solution)/shard_map/dot_general | solution.py:95
  712.7 88.1 %reduce-scatter.5.cloned.1.call-done = f32[256,2048]{1,0:T(8,128)} async-done(((f32[2048,2048]{1,0:T(8,128)}), f32[256,2048]{1,0:T(8,128)}) %reduce-scatter.5.cloned.1.call-update) | async-done | bytes 2097168 | tf_op jit(solution)/shard_map/reduce_scatter | solution.py:97
  800.8 2.8 fusion.84
  (103 shorter events, 19.4 us)
Async XLA Ops:
  7.2 27.4 %copy-start = (bf16[1,256,2048]{2,1,0:T(8,128)(2,1)S(1)}, bf16[1,256,2048]{2,1,0:T(8,128)(2,1)}, u32[]{:S(2)}) copy-start(bf16[1,256,2048]{2,1,0:T(8,128)(2,1)} %param.7) | copy-start | bytes 3145732
  7.2 27.3 %copy-start.20 = (f32[2,2048]{1,0:T(2,128)S(1)}, f32[2,2048]{1,0:T(2,128)}, u32[]{:S(2)}) copy-start(f32[2,2048]{1,0:T(2,128)} %param.8) | copy-start | bytes 49156
  7.2 28.8 %copy-start.15 = (bf16[2,256,2,128]{3,2,1,0:T(2,128)(2,1)S(1)}, bf16[2,256,2,128]{3,2,1,0:T(2,128)(2,1)}, u32[]{:S(2)}) copy-start(bf16[2,256,2,128]{3,2,1,0:T(2,128)(2,1)} %param.10) | copy-start | bytes 786436
  7.2 29.3 %copy-start.6 = (bf16[2,256,2,512]{3,2,1,0:T(2,128)(2,1)S(1)}, bf16[2,256,2,512]{3,2,1,0:T(2,128)(2,1)}, u32[]{:S(2)}) copy-start(bf16[2,256,2,512]{3,2,1,0:T(2,128)(2,1)} %param.11) | copy-start | bytes 3145732
  7.2 111.2 %all-gather.11.cloned.1.call-start = ((), (), s32[]{:S(2)}) async-start(), calls=%async_computation.4 | async-start | bytes 5570560 | tf_op jit(solution)/shard_map/all_gather | solution.py:71
  10.7 19.8 %collective-permute-start.1 = (bf16[640,256]{1,0:T(8,128)(2,1)S(1)}, bf16[640,256]{1,0:T(8,128)(2,1)S(1)}, u32[]{:S(2)}, u32[]{:S(2)}) collective-permute-start(bf16[640,256]{1,0:T(8,128)(2,1)S(1)} %pad_maximum_fusion.4), channel_id=1, source_target_pairs={{0,0},{1,8},{2,16},{3,24},{4,32},{5,40},{6,48},{7,56},{8,64},{9,72... | collective-permute-start | bytes 983048 | tf_op jit(solution)/shard_map/ppermute | solution.py:69
  30.5 0.7 copy-start.13
  31.3 139.1 %all-gather.7.cloned.1.call-start = ((), (), s32[]{:S(2)}) async-start(), calls=%async_computation.2 | async-start | bytes 9437184 | tf_op jit(solution)/shard_map/all_gather | solution.py:80
  32.8 5.3 copy-start.17
  35.9 216.7 %all-gather.9.cloned.1.call-start = ((), (), s32[]{:S(2)}) async-start(), calls=%async_computation.3 | async-start | bytes 11141120 | tf_op jit(solution)/shard_map/all_gather | solution.py:70
  38.8 36.3 %collective-permute-start = (bf16[256,1280]{1,0:T(8,128)(2,1)S(1)}, bf16[256,1280]{1,0:T(8,128)(2,1)S(1)}, u32[]{:S(2)}, u32[]{:S(2)}) collective-permute-start(bf16[256,1280]{1,0:T(8,128)(2,1)S(1)} %pad_maximum_fusion.2), channel_id=1, source_target_pairs={{0,0},{1,8},{2,16},{3,24},{4,32},{5,40},{6,48},{7,56},{8,64},{9,72... | collective-permute-start | bytes 1966088 | tf_op jit(solution)/shard_map/ppermute | solution.py:68
  75.1 0.9 copy-start.11
  76.0 369.4 %reduce-scatter.3.cloned.1.call-start = ((), (), s32[]{:S(2)}) async-start(), calls=%async_computation.5 | async-start | bytes 18874368 | tf_op jit(solution)/shard_map/reduce_scatter | solution.py:97
  252.6 18.0 %copy-start.22 = (bf16[4096,1280]{1,0:T(8,128)(2,1)S(1)}, bf16[4096,1280]{1,0:T(8,128)(2,1)}, u32[]{:S(2)}) copy-start(bf16[4096,1280]{1,0:T(8,128)(2,1)} %all-gather.9.cloned.1.call-done) | copy-start | bytes 31457284
  284.0 6.6 copy-start.8
  288.1 1.1 copy-start.18
  292.5 12.6 %copy-start.2 = (bf16[640,8,256]{0,2,1:T(8,128)(2,1)S(1)}, bf16[640,8,256]{0,2,1:T(8,128)(2,1)}, u32[]{:S(2)}) copy-start(bf16[640,8,256]{0,2,1:T(8,128)(2,1)} %copy.44) | copy-start | bytes 7864324
  292.5 12.6 %copy-start.4 = (bf16[2048,512]{1,0:T(8,128)(2,1)S(1)}, bf16[2048,512]{1,0:T(8,128)(2,1)}, u32[]{:S(2)}) copy-start(bf16[2048,512]{1,0:T(8,128)(2,1)} %fusion.24) | copy-start | bytes 6291460
  318.8 1.0 copy-start.7
  318.8 1.0 copy-start.16
  318.8 21.3 %copy-start.5 = (bf16[1,256,2,512]{3,2,1,0:T(2,128)(2,1)S(1)}, bf16[1,256,2,512]{3,2,1,0:T(2,128)(2,1)}, u32[]{:S(2)}) copy-start(bf16[1,256,2,512]{3,2,1,0:T(2,128)(2,1)} %get-tuple-element.23) | copy-start | bytes 1572868
  318.8 186.6 %all-gather.17.cloned.1.call-start = ((), (), s32[]{:S(2)}) async-start(), calls=%async_computation.8 | async-start | bytes 5570560 | tf_op jit(solution)/shard_map/all_gather | solution.py:71
  319.8 19.6 %collective-permute-start.3 = (bf16[640,256]{1,0:T(8,128)(2,1)S(1)}, bf16[640,256]{1,0:T(8,128)(2,1)S(1)}, u32[]{:S(2)}, u32[]{:S(2)}) collective-permute-start(bf16[640,256]{1,0:T(8,128)(2,1)S(1)} %pad_maximum_fusion.5), channel_id=1, source_target_pairs={{0,0},{1,8},{2,16},{3,24},{4,32},{5,40},{6,48},{7,56},{8,64},{9,72... | collective-permute-start | bytes 983048 | tf_op jit(solution)/shard_map/ppermute | solution.py:69
  339.4 0.7 copy-start.14
  340.1 247.4 %all-gather.15.cloned.1.call-start = ((), (), s32[]{:S(2)}) async-start(), calls=%async_computation.7 | async-start | bytes 11141120 | tf_op jit(solution)/shard_map/all_gather | solution.py:70
  341.1 27.3 %collective-permute-start.2 = (bf16[256,1280]{1,0:T(8,128)(2,1)S(1)}, bf16[256,1280]{1,0:T(8,128)(2,1)S(1)}, u32[]{:S(2)}, u32[]{:S(2)}) collective-permute-start(bf16[256,1280]{1,0:T(8,128)(2,1)S(1)} %pad_maximum_fusion.3), channel_id=1, source_target_pairs={{0,0},{1,8},{2,16},{3,24},{4,32},{5,40},{6,48},{7,56},{8,64},{9,72... | collective-permute-start | bytes 1966088 | tf_op jit(solution)/shard_map/ppermute | solution.py:68
  368.4 0.8 copy-start.10
  369.3 270.2 %all-gather.13.cloned.1.call-start = ((), (), s32[]{:S(2)}) async-start(), calls=%async_computation.6 | async-start | bytes 9437184 | tf_op jit(solution)/shard_map/all_gather | solution.py:80
  449.1 351.8 %reduce-scatter.5.cloned.1.call-start = ((), (), s32[]{:S(2)}) async-start(), calls=%async_computation.9 | async-start | bytes 18874368 | tf_op jit(solution)/shard_map/reduce_scatter | solution.py:97
  639.5 18.0 %copy-start.21 = (bf16[4096,1280]{1,0:T(8,128)(2,1)S(1)}, bf16[4096,1280]{1,0:T(8,128)(2,1)}, u32[]{:S(2)}) copy-start(bf16[4096,1280]{1,0:T(8,128)(2,1)} %all-gather.15.cloned.1.call-done) | copy-start | bytes 31457284
  670.8 6.6 copy-start.9
  674.9 1.1 copy-start.19
  683.1 12.6 %copy-start.1 = (bf16[640,8,256]{0,2,1:T(8,128)(2,1)S(1)}, bf16[640,8,256]{0,2,1:T(8,128)(2,1)}, u32[]{:S(2)}) copy-start(bf16[640,8,256]{0,2,1:T(8,128)(2,1)} %copy.53) | copy-start | bytes 7864324
  683.1 12.6 %copy-start.3 = (bf16[2048,512]{1,0:T(8,128)(2,1)S(1)}, bf16[2048,512]{1,0:T(8,128)(2,1)}, u32[]{:S(2)}) copy-start(bf16[2048,512]{1,0:T(8,128)(2,1)} %fusion.22) | copy-start | bytes 6291460
  683.1 12.6 %copy-start.12 = (bf16[8,256,1,128]{3,1,0,2:T(8,128)(2,1)S(1)}, bf16[8,256,1,128]{3,1,0,2:T(8,128)(2,1)}, u32[]{:S(2)}) copy-start(bf16[8,256,1,128]{3,1,0,2:T(8,128)(2,1)} %copy.52) | copy-start | bytes 1572868
Sparse Core Ops, SparseCore 0:
  31.4 86.9 all-gather.10
  120.7 49.6 all-gather.6
  172.5 80.0 all-gather.8
  319.0 126.3 reduce-scatter.2
  447.3 58.0 all-gather.16
  507.4 80.0 all-gather.14
  589.7 49.6 all-gather.12
  709.6 91.2 reduce-scatter.4

commit v2 on v1

v2 whole, which is shorter than its diff:
```python
import functools

import jax
import jax.numpy as jnp
from jax import lax
from jax.experimental import pallas as pl
from jax.experimental.pallas import tpu as pltpu
from jax.sharding import PartitionSpec as P

LN_EPS = 1e-6
ROPE_BASE = 10000.0
MESH = pl.DeviceIdType.MESH
VMEM_LIMIT = 60 * 1024 * 1024


def rope_tables(seq_len, head_dim):
    half_dim = head_dim // 2
    inv_freq = ROPE_BASE ** (-2.0 * jnp.arange(half_dim, dtype=jnp.float32) / head_dim)
    angles = jnp.arange(seq_len, dtype=jnp.float32)[:, None] * inv_freq[None, :]
    cos, sin = jnp.cos(angles), jnp.sin(angles)
    return jnp.concatenate([cos, cos], axis=1), jnp.concatenate([-sin, sin], axis=1)


def layer_norm(resid, g_scale):
    resid_f = resid.astype(jnp.float32)
    centered = resid_f - jnp.mean(resid_f, axis=-1, keepdims=True)
    variance = jnp.mean(centered * centered, axis=-1, keepdims=True)
    return (centered * lax.rsqrt(variance + LN_EPS) * g_scale).astype(jnp.bfloat16)


def ring_ids(n_wx):
    me = lax.axis_index('wx')
    chip, core = lax.div(me, 2), lax.rem(me, 2)
    n_chip = n_wx // 2

    def at(step, other=0):
        return lax.rem(chip + step, n_chip) * 2 + (lax.rem(core + other, 2))

    return me, chip, core, at


def entry_barrier(peers):
    barrier = pltpu.get_barrier_semaphore()
    for peer in peers:
        pl.semaphore_signal(barrier, inc=1, device_id={'wx': peer}, device_id_type=MESH)
    pl.semaphore_wait(barrier, len(peers))


def gather_copies(n_wx, hall, send_sem, recv_sem):
    me, chip, core, at = ring_ids(n_wx)
    half = hall.shape[1] // 2
    right, left, partner = at(1), at(3), at(0, 1)
    top, bottom, whole = pl.ds(0, half), pl.ds(half, half), pl.ds(0, 2 * half)

    def copy(num, block, rows, target):
        ref = hall.at[block, rows]
        return pltpu.make_async_remote_copy(
            src_ref=ref, dst_ref=ref, send_sem=send_sem.at[num], recv_sem=recv_sem.at[num],
            device_id={'wx': target}, device_id_type=MESH)

    return [
        copy(0, me, whole, partner),
        copy(1, me, top, right), copy(2, me, bottom, left),
        copy(3, me, bottom, right), copy(4, me, top, left),
        copy(5, left, top, right), copy(6, right, bottom, left),
        copy(7, left, whole, partner), copy(8, right, whole, partner),
        copy(9, at(2), top, partner), copy(10, at(2), bottom, partner),
    ]


def arrivals(n_wx, hall, send_sem, recv_sem):
    me, chip, core, at = ring_ids(n_wx)
    half = hall.shape[1] // 2
    top, bottom, whole = pl.ds(0, half), pl.ds(half, half), pl.ds(0, 2 * half)

    def copy(num, block, rows):
        ref = hall.at[block, rows]
        return pltpu.make_async_remote_copy(
            src_ref=ref, dst_ref=ref, send_sem=send_sem.at[num], recv_sem=recv_sem.at[num],
            device_id={'wx': at(0, 1)}, device_id_type=MESH)

    return [
        copy(0, at(0, 1), whole),
        copy(1, at(3), top), copy(2, at(1), bottom), copy(3, at(3), bottom), copy(4, at(1), top),
        copy(5, at(2), top), copy(6, at(2), bottom),
        copy(7, at(3, 1), whole), copy(8, at(1, 1), whole),
        copy(9, at(2, 1), top), copy(10, at(2, 1), bottom),
    ]


def gather_kernel(n_wx, h_ref, out_ref, hall, send_sem, recv_sem, local_sem, out_sem):
    me, chip, core, at = ring_ids(n_wx)
    load = pltpu.make_async_copy(h_ref, hall.at[me], local_sem)
    load.start()
    entry_barrier([at(1), at(3), at(0, 1)])
    sends = gather_copies(n_wx, hall, send_sem, recv_sem)
    lands = arrivals(n_wx, hall, send_sem, recv_sem)
    outs = []

    def put(block):
        out = pltpu.make_async_copy(hall.at[block], out_ref.at[block], out_sem.at[len(outs)])
        out.start()
        outs.append(out)

    load.wait()
    for num in range(5):
        sends[num].start()
    put(me)
    lands[0].wait_recv()
    put(at(0, 1))
    lands[1].wait_recv()
    sends[5].start()
    lands[2].wait_recv()
    sends[6].start()
    lands[3].wait_recv()
    sends[7].start()
    put(at(3))
    lands[4].wait_recv()
    sends[8].start()
    put(at(1))
    lands[7].wait_recv()
    put(at(3, 1))
    lands[8].wait_recv()
    put(at(1, 1))
    lands[5].wait_recv()
    sends[9].start()
    lands[6].wait_recv()
    sends[10].start()
    put(at(2))
    lands[9].wait_recv()
    lands[10].wait_recv()
    put(at(2, 1))
    for num in range(11):
        sends[num].wait_send()
    for out in outs:
        out.wait()


def gather_h(h, n_wx):
    seq, d_model = h.shape
    return pl.pallas_call(
        functools.partial(gather_kernel, n_wx),
        out_shape=jax.ShapeDtypeStruct((n_wx, seq, d_model), h.dtype),
        in_specs=[pl.BlockSpec(memory_space=pl.ANY)],
        out_specs=pl.BlockSpec(memory_space=pl.ANY),
        scratch_shapes=[
            pltpu.VMEM((n_wx, seq, d_model), h.dtype),
            pltpu.SemaphoreType.DMA((11,)), pltpu.SemaphoreType.DMA((11,)),
            pltpu.SemaphoreType.DMA, pltpu.SemaphoreType.DMA((n_wx,)),
        ],
        compiler_params=pltpu.CompilerParams(collective_id=0, has_side_effects=True, vmem_limit_bytes=VMEM_LIMIT),
        cost_estimate=pl.CostEstimate(flops=20_000_000_000, bytes_accessed=16 * 2**20, transcendentals=0),
        name='gather_h',
    )(h)


def up_step(hall, wa, mo, kv_out, xt, cos, sin, f_loc, head_dim):
    seq, d_model = hall.shape[1], hall.shape[2]
    rows = pl.ds(pl.multiple_of(xt * 2 * seq, 2 * seq), 2 * seq)
    h = hall[pl.ds(xt * 2, 2)].reshape(2 * seq, d_model)
    width = f_loc + head_dim
    narrow = []
    for hh in range(2):
        qkv = jnp.dot(h, wa[hh, :, 2 * f_loc:], preferred_element_type=jnp.float32)
        narrow.append(qkv.astype(jnp.bfloat16))
    for hh in range(2):
        g_f = jnp.dot(h, wa[hh, :, :f_loc], preferred_element_type=jnp.float32).astype(jnp.bfloat16).astype(jnp.float32)
        u_f = jnp.dot(h, wa[hh, :, f_loc:2 * f_loc], preferred_element_type=jnp.float32).astype(jnp.bfloat16).astype(jnp.float32)
        hidden = g_f * (1.0 / (1.0 + jnp.exp(-g_f))) * u_f
        mo[rows, hh * width:hh * width + f_loc] = hidden.astype(jnp.bfloat16)

    def rot(val):
        val_f = val.astype(jnp.float32)
        return (val_f * cos + pltpu.roll(val_f, head_dim // 2, 1) * sin).astype(jnp.bfloat16)

    allowed = lax.broadcasted_iota(jnp.int32, (seq, seq), 0) >= lax.broadcasted_iota(jnp.int32, (seq, seq), 1)
    for b in range(2):
        part = slice(b * seq, (b + 1) * seq)
        k_rot = rot(narrow[0][part, head_dim:])
        v_val = narrow[1][part, head_dim:]
        kv_out[b, 0] = k_rot
        kv_out[b, 1] = v_val
        for hh in range(2):
            q_rot = rot(narrow[hh][part, :head_dim])
            scores = lax.dot_general(q_rot, k_rot, (((1,), (1,)), ((), ())), preferred_element_type=jnp.float32) * head_dim ** -0.5
            scores = jnp.where(allowed, scores, -jnp.inf)
            top = jnp.max(scores, axis=-1, keepdims=True)
            expd = jnp.exp(scores - top)
            probs = (expd / jnp.sum(expd, axis=-1, keepdims=True)).astype(jnp.bfloat16)
            att = jnp.dot(probs, v_val, preferred_element_type=jnp.float32)
            mo[pl.ds(pl.multiple_of(xt * 2 * seq, 2 * seq) + b * seq, seq), hh * width + f_loc:(hh + 1) * width] = att.astype(jnp.bfloat16)


def up_kernel(n_wx, f_loc, head_dim, hall_ref, wa_ref, cos_ref, sin_ref, mo_ref, k_ref, v_ref, hall, wa, mo, kv, h_sem, w_sem, out_sem, kv_sem):
    me, chip, core, at = ring_ids(n_wx)
    n_chip = n_wx // 2
    seq = hall.shape[1]
    w_loads = [pltpu.make_async_copy(wa_ref.at[hh], wa.at[hh], w_sem.at[hh]) for hh in range(2)]

    def h_load(xt):
        return pltpu.make_async_copy(hall_ref.at[pl.ds(xt * 2, 2)], hall.at[pl.ds(xt * 2, 2)], h_sem.at[xt])

    def out_copy(xt):
        rows = pl.ds(pl.multiple_of(xt * 2 * seq, 2 * seq), 2 * seq)
        return pltpu.make_async_copy(mo.at[rows], mo_ref.at[rows], out_sem.at[xt])

    h_load(0).start()
    for load in w_loads:
        load.start()
    for xt in range(1, n_chip):
        h_load(xt).start()
    for load in w_loads:
        load.wait()

    def body(xt, carry):
        h_load(xt).wait()
        up_step(hall, wa, mo, kv.at[xt], xt, cos_ref[...], sin_ref[...], f_loc, head_dim)
        out_copy(xt).start()
        return carry

    lax.fori_loop(0, n_chip, body, 0)
    k_copy = pltpu.make_async_copy(kv.at[chip, core, 0], k_ref, kv_sem.at[0])
    v_copy = pltpu.make_async_copy(kv.at[chip, core, 1], v_ref, kv_sem.at[1])
    k_copy.start()
    v_copy.start()
    for xt in range(n_chip):
        out_copy(xt).wait()
    k_copy.wait()
    v_copy.wait()


def up_project(h_all, wa, cos, sin, f_loc, head_dim):
    n_wx, seq, d_model = h_all.shape
    n_chip = n_wx // 2
    width = 2 * (f_loc + head_dim)
    return pl.pallas_call(
        functools.partial(up_kernel, n_wx, f_loc, head_dim),
        out_shape=(
            jax.ShapeDtypeStruct((n_wx * seq, width), jnp.bfloat16),
            jax.ShapeDtypeStruct((seq, head_dim), jnp.bfloat16),
            jax.ShapeDtypeStruct((seq, head_dim), jnp.bfloat16),
        ),
        in_specs=[pl.BlockSpec(memory_space=pl.ANY), pl.BlockSpec(memory_space=pl.ANY),
                  pl.BlockSpec(memory_space=pltpu.VMEM), pl.BlockSpec(memory_space=pltpu.VMEM)],
        out_specs=[pl.BlockSpec(memory_space=pl.ANY)] * 3,
        scratch_shapes=[
            pltpu.VMEM((n_wx, seq, d_model), jnp.bfloat16),
            pltpu.VMEM(wa.shape, jnp.bfloat16),
            pltpu.VMEM((n_wx * seq, width), jnp.bfloat16),
            pltpu.VMEM((n_chip, 2, 2, seq, head_dim), jnp.bfloat16),
            pltpu.SemaphoreType.DMA((n_chip,)), pltpu.SemaphoreType.DMA((2,)),
            pltpu.SemaphoreType.DMA((n_chip,)), pltpu.SemaphoreType.DMA((2,)),
        ],
        compiler_params=pltpu.CompilerParams(vmem_limit_bytes=VMEM_LIMIT),
        cost_estimate=pl.CostEstimate(flops=22_000_000_000, bytes_accessed=24 * 2**20, transcendentals=0),
        name='up_project',
    )(h_all, wa, cos, sin)


N_COL = 4


def down_kernel(n_wx, mo_ref, wb_ref, resid_ref, out_ref, mo, wb, given, taken, acc, landed,
                mo_sem, wb_sem, pair_send, pair_recv, ring_send, ring_recv):
    me, chip, core, at = ring_ids(n_wx)
    n_chip = n_wx // 2
    right, left, partner = at(1), at(3), at(0, 1)
    seq = resid_ref.shape[0]
    n_hh, n_w, k_loc, col_w = wb_ref.shape
    col = wb.shape[1] // N_COL

    def step_of(i):
        phase, j = lax.div(i, 4), lax.rem(i, 4)
        odd, slot = lax.rem(j, 2), lax.div(j, 2)
        off = jnp.where(phase == 0, 2, jnp.where(phase == 3, 0, 1 + 2 * odd))
        q = jnp.where(phase == 3, j, jnp.where(phase == 1, (1 - odd) * 2 + slot, odd * 2 + slot))
        return lax.rem(chip + off, n_chip), q, odd

    def mo_load(off):
        rows = pl.ds(pl.multiple_of(lax.rem(chip + off, n_chip) * 2 * seq, 2 * seq), 2 * seq)
        return pltpu.make_async_copy(mo_ref.at[rows], mo.at[rows], mo_sem.at[off])

    def wb_load(hh, w):
        return pltpu.make_async_copy(
            wb_ref.at[hh, w], wb.at[pl.ds(hh * k_loc, k_loc), pl.ds(w * col_w, col_w)], wb_sem.at[hh * n_w + w])

    def pair_copy(i):
        return pltpu.make_async_remote_copy(
            src_ref=given.at[i], dst_ref=taken.at[i], send_sem=pair_send.at[i], recv_sem=pair_recv.at[i],
            device_id={'wx': partner}, device_id_type=MESH)

    def ring_copy(k, odd):
        return pltpu.make_async_remote_copy(
            src_ref=acc.at[k], dst_ref=landed.at[k], send_sem=ring_send.at[k], recv_sem=ring_recv.at[k],
            device_id={'wx': jnp.where(odd == 0, right, left)}, device_id_type=MESH)

    mo_load(2).start()
    for hh in range(n_hh):
        for w in range(n_w):
            wb_load(hh, w).start()
    for off in (1, 3, 0):
        mo_load(off).start()
    entry_barrier([right, left, partner])
    mo_load(2).wait()
    for hh in range(n_hh):
        for w in range(n_w):
            wb_load(hh, w).wait()
    for off in (1, 3, 0):
        mo_load(off).wait()

    def dot_of(i, which):
        xt, q, _ = step_of(i)
        rows = pl.ds(pl.multiple_of((xt * 2 + which) * seq, seq), seq)
        cols = pl.ds(pl.multiple_of(q * col, col), col)
        return jnp.dot(mo[rows, :], wb[:, cols], preferred_element_type=jnp.float32)

    def body(i, carry):
        given[i] = dot_of(i, 1 - core)

        @pl.when(i > 0)
        def _():
            pair_copy(i - 1).wait_recv()
            acc[i - 1] = acc[i - 1] + taken[i - 1]

        acc[i] = dot_of(i, core)
        pair_copy(i).start()

        @pl.when((i > 0) & (i <= 8))
        def _():
            ring_copy(i - 1, lax.rem(i - 1, 2)).start()

        return carry

    n_step = 4 * N_COL
    lax.fori_loop(0, n_step, body, 0)
    pair_copy(n_step - 1).wait_recv()
    acc[n_step - 1] = acc[n_step - 1] + taken[n_step - 1]
    for pair in range(2):
        for odd in range(2):
            k = 8 + pair * 2 + odd
            ring_copy(k - 8, odd).wait_recv()
            acc[k] = acc[k] + landed[k - 8]
        for q in (pair, pair + 2):
            cols = slice(q * col, (q + 1) * col)
            acc[12 + q] = acc[12 + q] + resid_ref[:, cols].astype(jnp.float32)
        for odd in range(2):
            ring_copy(8 + pair * 2 + odd, odd).start()
    for q, (raw, comb) in ((0, (5, 8)), (2, (4, 9)), (1, (7, 10)), (3, (6, 11))):
        ring_copy(raw, raw % 2).wait_recv()
        ring_copy(comb, comb % 2).wait_recv()
        cols = slice(q * col, (q + 1) * col)
        out_ref[:, cols] = (acc[12 + q] + (landed[raw] + landed[comb])).astype(jnp.bfloat16)
    for i in range(n_step):
        pair_copy(i).wait_send()
    for k in range(12):
        ring_copy(k, k % 2).wait_send()


def down_project(mo, wb, resid, n_wx):
    seq, d_model = resid.shape
    col = d_model // N_COL
    n_hh, n_w, k_loc, col_w = wb.shape
    n_step = 4 * N_COL
    return pl.pallas_call(
        functools.partial(down_kernel, n_wx),
        out_shape=jax.ShapeDtypeStruct((seq, d_model), jnp.bfloat16),
        in_specs=[pl.BlockSpec(memory_space=pl.ANY), pl.BlockSpec(memory_space=pl.ANY), pl.BlockSpec(memory_space=pltpu.VMEM)],
        out_specs=pl.BlockSpec(memory_space=pltpu.VMEM),
        scratch_shapes=[
            pltpu.VMEM(mo.shape, jnp.bfloat16),
            pltpu.VMEM((n_hh * k_loc, n_w * col_w), jnp.bfloat16),
            pltpu.VMEM((n_step, seq, col), jnp.float32),
            pltpu.VMEM((n_step, seq, col), jnp.float32),
            pltpu.VMEM((n_step, seq, col), jnp.float32),
            pltpu.VMEM((12, seq, col), jnp.float32),
            pltpu.SemaphoreType.DMA((4,)), pltpu.SemaphoreType.DMA((n_hh * n_w,)),
            pltpu.SemaphoreType.DMA((n_step,)), pltpu.SemaphoreType.DMA((n_step,)),
            pltpu.SemaphoreType.DMA((12,)), pltpu.SemaphoreType.DMA((12,)),
        ],
        compiler_params=pltpu.CompilerParams(collective_id=1, has_side_effects=True, vmem_limit_bytes=VMEM_LIMIT),
        cost_estimate=pl.CostEstimate(flops=40_000_000_000, bytes_accessed=16 * 2**20, transcendentals=0),
        name='down_project',
    )(mo, wb, resid)


def solution(mesh):
    batch_axes = ('dp', 'wy', 'wx')
    in_specs = (P(batch_axes), P(), P(None, 'wx', 'wy'), P(None, 'wx'), P(None, 'wx', None, 'wy'), P(None, 'wy', 'wx'), P(None, 'wy', 'wx'))
    out_specs = (P(batch_axes), P(None, batch_axes), P(None, batch_axes))
    n_wy, n_wx = mesh.shape['wy'], mesh.shape['wx']
    per = n_wy // n_wx
    perm = []
    for iy in range(n_wy):
        for ix in range(n_wx):
            perm.append((iy * n_wx + ix, ((iy % per) * n_wx + ix) * n_wx + iy // per))

    def device_step(x_tokens, gamma_ln, w_q, w_kv, w_gu, w_o, w_d):
        seq_len, d_model = x_tokens.shape[1], x_tokens.shape[2]
        head_dim = w_kv.shape[-1]
        d_loc = w_q.shape[1]
        f_loc = w_gu.shape[-1]
        n_layers = w_q.shape[0]
        cos_tab, sin_tab = rope_tables(seq_len, head_dim)
        iy = lax.axis_index('wy')
        weights_a, weights_b = [], []
        for layer_idx in range(n_layers):
            kv_half = lax.dynamic_index_in_dim(w_kv[layer_idx], lax.rem(iy, per), axis=1, keepdims=False)
            pack_a = jnp.concatenate([w_gu[layer_idx].reshape(d_loc, 2 * f_loc), w_q[layer_idx], kv_half], axis=1)
            pack_b = jnp.concatenate([w_d[layer_idx], w_o[layer_idx]], axis=0)
            pack_a = lax.ppermute(pack_a, ('wy', 'wx'), perm)
            pack_b = lax.ppermute(pack_b, ('wy', 'wx'), perm)
            full_a = lax.all_gather(pack_a, 'wy', axis=0, tiled=True)
            full_b = lax.all_gather(pack_b, 'wy', axis=0, tiled=True)
            weights_a.append(full_a.reshape(per, d_model, 2 * f_loc + 2 * head_dim))
            weights_b.append(full_b.reshape(per, n_wx, f_loc + head_dim, d_loc))
        resid = x_tokens[0]
        key_list = []
        value_list = []
        for layer_idx in range(n_layers):
            normed = layer_norm(resid, gamma_ln[layer_idx])
            h_all = gather_h(normed, n_wx)
            mo, k_rot, v_val = up_project(h_all, weights_a[layer_idx], cos_tab, sin_tab, f_loc, head_dim)
            resid = down_project(mo, weights_b[layer_idx], resid, n_wx)
            key_list.append(k_rot[None])
            value_list.append(v_val[None])
        return resid[None], jnp.stack(key_list), jnp.stack(value_list)

    return jax.shard_map(device_step, mesh=mesh, in_specs=in_specs, out_specs=out_specs, check_vma=False)
```

time: 815 us -> 492 us (0.60)
  waiting for transfers between devices: 586 us -> 99.4 us
  Pallas kernels: 0 us -> 327 us
  matrix products: 113 us -> 0 us
  local copies, waits for them, and re-layouts: 47.5 us -> 9.09 us
  other arithmetic: 30.9 us -> 9.39 us
  starting transfers between devices: 18.4 us -> 32.4 us
    pallas_call x0 -> x6, Pallas kernels: none -> 327 us  [the longest x2 162 us: down_project(): pl.pallas_call(functools.partial(down_kernel, n_wx), out_shape=jax.ShapeD...]
    reduce_scatter x2 -> x0, waiting for transfers between devices: 164 us -> none  [device_step(): mixed = lax.psum_scatter(total, 'wx', scatter_dimension=0, tiled=True)]
    all_gather x2, waiting for transfers between devices: 150 us -> 1.23 us  [device_step(): full_a = lax.all_gather(pack_a, 'wy', axis=0, tiled=True)]
    dot_general x12 -> x0, matrix products: 113 us -> none  [the longest x4 57.1 us: device_step(): jnp.dot(h_all, wa[hh], preferred_element_type=jnp.float32)]
    all_gather x2 -> x0, waiting for transfers between devices: 89.9 us -> none  [device_step(): h_all = lax.all_gather(normed, 'wx', axis=0, tiled=True)]
    all_gather x2, waiting for transfers between devices: 97.5 us -> 27.9 us  [device_step(): full_b = lax.all_gather(pack_b, 'wy', axis=0, tiled=True)]
    ppermute x2, waiting for transfers between devices: 30.9 us -> 6.48 us  [device_step(): pack_b = lax.ppermute(pack_b, ('wy', 'wx'), perm)]
    transpose x4 -> x0, local copies, waits for them, and re-layouts: 18.2 us -> none  [device_step(): rhs = jnp.transpose(wb[hh], (1, 0, 2)).reshape(f_loc + head_dim, d_model)]
  transfers between devices with their start and end apart: 12 -> 8, of which waited for: 12 -> 5; matrix products, arithmetic and copies ran while one was open for 6% -> 2% of each run, Pallas kernels for 0% -> 50%
where the time goes in v2:
time: 492 us; the launch traced here: 491 us
  Pallas kernels  327 us (66%)
  waiting for transfers between devices  99.4 us (20%)
  starting transfers between devices  32.4 us (7%)
  between operations  14.1 us (3%)
  other arithmetic  9.39 us (2%)
  local copies, waits for them, and re-layouts  9.09 us (2%)
    pallas_call x2, Pallas kernels, down_project(): pl.pallas_call(functools.partial(down_kernel, n_wx), out_shape=jax.ShapeD...  162 us
    pallas_call x2, Pallas kernels, gather_h(): pl.pallas_call(functools.partial(gather_kernel, n_wx), out_shape=jax.Shap...  97 us
    pallas_call x2, Pallas kernels, up_project(): pl.pallas_call(functools.partial(up_kernel, n_wx, f_loc, head_dim), out_s...  67.6 us
    ppermute x2, waiting for transfers between devices, device_step(): pack_a = lax.ppermute(pack_a, ('wy', 'wx'), perm)  63.7 us
    all_gather x2, waiting for transfers between devices, device_step(): full_b = lax.all_gather(pack_b, 'wy', axis=0, tiled=True)  27.9 us
    ppermute x2, starting transfers between devices, device_step(): pack_b = lax.ppermute(pack_b, ('wy', 'wx'), perm)  18.2 us
    ppermute x2, starting transfers between devices, device_step(): pack_a = lax.ppermute(pack_a, ('wy', 'wx'), perm)  14.1 us
  transfers between devices with their start and end apart: 8, of which 5 were waited for; matrix products, arithmetic and copies ran while one was open for 2% of the time, Pallas kernels for 50%

profile of v2, /device:TPU:1, one launch (start us, length us, event | category | flops | bytes accessed | tf_op | source)
XLA Modules:
  0.0 491.3 jit_solution(5449377747984565091)
XLA Ops:
  7.2 0.0 all-gather.5.cloned.1.call-start
  7.2 1.2 fusion.14
  8.4 0.3 constant_dynamic-slice_fusion
  8.7 1.9 fusion.13
  10.7 0.0 copy-start.8
  10.7 0.1 copy.16
  10.8 0.1 pad_maximum_fusion
  10.8 4.7 collective-permute-start
  15.6 28.4 %collective-permute-done = bf16[256,1280]{1,0:T(8,128)(2,1)S(1)} collective-permute-done((bf16[256,1280]{1,0:T(8,128)(2,1)S(1)}, bf16[256,1280]{1,0:T(8,128)(2,1)S(1)}, u32[]{:S(2)}, u32[]{:S(2)}) %collective-permute-start) | collective-permute-done | bytes 655392 | tf_op jit(solution)/shard_map/ppermute | solution.py:410
  43.9 0.8 copy-done.2
  44.8 0.0 all-gather.5.cloned.1.call-update
  44.8 0.0 all-gather.7.cloned.1.call-start
  45.0 9.5 %collective-permute-start.1 = (bf16[640,256]{1,0:T(8,128)(2,1)S(1)}, bf16[640,256]{1,0:T(8,128)(2,1)S(1)}, u32[]{:S(2)}, u32[]{:S(2)}) collective-permute-start(bf16[640,256]{1,0:T(8,128)(2,1)S(1)} %pad_maximum_fusion.2), channel_id=1, source_target_pairs={{0,0},{1,8},{2,16},{3,24},{4,32},{5,40},{6,48},{7,56},{8,64},{9,72... | collective-permute-start | bytes 983048 | tf_op jit(solution)/shard_map/ppermute | solution.py:411
  54.5 6.5 %collective-permute-done.1 = bf16[640,256]{1,0:T(8,128)(2,1)S(1)} collective-permute-done((bf16[640,256]{1,0:T(8,128)(2,1)S(1)}, bf16[640,256]{1,0:T(8,128)(2,1)S(1)}, u32[]{:S(2)}, u32[]{:S(2)}) %collective-permute-start.1) | collective-permute-done | bytes 327712 | tf_op jit(solution)/shard_map/ppermute | solution.py:411
  61.0 0.7 copy-done.5
  61.7 0.0 all-gather.7.cloned.1.call-update
  61.7 0.0 all-gather.9.cloned.1.call-start
  61.8 0.1 copy.17
  61.9 0.1 pad_maximum_fusion.1
  61.9 9.4 %collective-permute-start.2 = (bf16[256,1280]{1,0:T(8,128)(2,1)S(1)}, bf16[256,1280]{1,0:T(8,128)(2,1)S(1)}, u32[]{:S(2)}, u32[]{:S(2)}) collective-permute-start(bf16[256,1280]{1,0:T(8,128)(2,1)S(1)} %pad_maximum_fusion.1), channel_id=1, source_target_pairs={{0,0},{1,8},{2,16},{3,24},{4,32},{5,40},{6,48},{7,56},{8,64},{9,72... | collective-permute-start | bytes 1966088 | tf_op jit(solution)/shard_map/ppermute | solution.py:410
  71.3 35.4 %collective-permute-done.2 = bf16[256,1280]{1,0:T(8,128)(2,1)S(1)} collective-permute-done((bf16[256,1280]{1,0:T(8,128)(2,1)S(1)}, bf16[256,1280]{1,0:T(8,128)(2,1)S(1)}, u32[]{:S(2)}, u32[]{:S(2)}) %collective-permute-start.2) | collective-permute-done | bytes 655392 | tf_op jit(solution)/shard_map/ppermute | solution.py:410
  106.7 0.8 copy-done.3
  107.5 0.0 all-gather.9.cloned.1.call-update
  107.5 0.0 all-gather.11.cloned.1.call-start
  107.6 8.7 %collective-permute-start.3 = (bf16[640,256]{1,0:T(8,128)(2,1)S(1)}, bf16[640,256]{1,0:T(8,128)(2,1)S(1)}, u32[]{:S(2)}, u32[]{:S(2)}) collective-permute-start(bf16[640,256]{1,0:T(8,128)(2,1)S(1)} %pad_maximum_fusion.3), channel_id=1, source_target_pairs={{0,0},{1,8},{2,16},{3,24},{4,32},{5,40},{6,48},{7,56},{8,64},{9,72... | collective-permute-start | bytes 983048 | tf_op jit(solution)/shard_map/ppermute | solution.py:411
  116.3 0.2 convert_reduce_fusion.1
  116.5 0.4 fusion.7
  117.0 1.4 fusion.9.h_ref
  118.3 55.5 %gather_h.2.hall_ref = bf16[8,256,2048]{2,1,0:T(8,128)(2,1)} custom-call(bf16[256,2048]{1,0:T(8,128)(2,1)} %fusion.9.h_ref), custom_call_target="tpu_custom_call" | custom-call | flops 20000000000 | bytes 16777216 | tf_op jit(solution)/shard_map/gather_h/pallas_call | solution.py:141
  173.8 0.5 fusion.12
  174.4 0.8 pad_maximum_fusion.4
  175.2 0.7 copy-done.6
  175.9 0.0 all-gather.11.cloned.1.call-update
  176.0 1.2 all-gather.5.cloned.1.call-done
  177.2 33.8 %up_project.2 = (bf16[2048,1280]{1,0:T(8,128)(2,1)}, bf16[256,128]{1,0:T(8,128)(2,1)}, bf16[256,128]{1,0:T(8,128)(2,1)}) custom-call(bf16[8,256,2048]{2,1,0:T(8,128)(2,1)} %gather_h.2.hall_ref, bf16[2,2048,1280]{2,1,0:T(8,128)(2,1)} %bitcast.53, f32[256,128]{1,0:T(8,128)} %get-tuple-element.32.cos_ref, f32[256,128]{1,0:T(8,128)} %get-tuple-element.33.sin_ref), custom_call_target="tpu_custom_call" | custom-call | flops 22000001024 | bytes 25165824 | tf_op jit(solution)/shard_map/up_project/pallas_call | solution.py:236
  211.0 27.8 %all-gather.7.cloned.1.call-done = bf16[10240,256]{1,0:T(8,128)(2,1)} async-done(((bf16[640,256]{1,0:T(8,128)(2,1)}), bf16[10240,256]{1,0:T(8,128)(2,1)}) %all-gather.7.cloned.1.call-update) | async-done | bytes 5242896 | tf_op jit(solution)/shard_map/all_gather | solution.py:413
  238.8 82.0 %down_project.2.resid_ref = bf16[256,2048]{1,0:T(8,128)(2,1)} custom-call(bf16[2048,1280]{1,0:T(8,128)(2,1)} %get-tuple-element.9.mo_ref, bf16[2,8,640,256]{3,2,1,0:T(8,128)(2,1)} %bitcast.55, bf16[256,2048]{1,0:T(8,128)(2,1)} %bitcast.39), custom_call_target="tpu_custom_call" | custom-call | flops 40000000000 | bytes 16777216 | tf_op jit(solution)/shard_map/down_project/pallas_call | solution.py:364
  320.9 1.5 convert_reduce_fusion
  322.4 1.6 fusion.4
  324.1 1.4 fusion.6.h_ref
  325.4 41.4 %gather_h.3.hall_ref = bf16[8,256,2048]{2,1,0:T(8,128)(2,1)} custom-call(bf16[256,2048]{1,0:T(8,128)(2,1)} %fusion.6.h_ref), custom_call_target="tpu_custom_call" | custom-call | flops 20000000000 | bytes 16777216 | tf_op jit(solution)/shard_map/gather_h/pallas_call | solution.py:141
  366.9 0.0 all-gather.9.cloned.1.call-done
  366.9 33.8 %up_project.3 = (bf16[2048,1280]{1,0:T(8,128)(2,1)}, bf16[256,128]{1,0:T(8,128)(2,1)}, bf16[256,128]{1,0:T(8,128)(2,1)}) custom-call(bf16[8,256,2048]{2,1,0:T(8,128)(2,1)} %gather_h.3.hall_ref, bf16[2,2048,1280]{2,1,0:T(8,128)(2,1)} %bitcast.54, f32[256,128]{1,0:T(8,128)} %get-tuple-element.32.cos_ref, f32[256,128]{1,0:T(8,128)} %get-tuple-element.33.sin_ref), custom_call_target="tpu_custom_call" | custom-call | flops 22000001024 | bytes 25165824 | tf_op jit(solution)/shard_map/up_project/pallas_call | solution.py:236
  400.7 0.0 all-gather.11.cloned.1.call-done
  400.8 80.3 %down_project.3 = bf16[256,2048]{1,0:T(8,128)(2,1)} custom-call(bf16[2048,1280]{1,0:T(8,128)(2,1)} %get-tuple-element.10.mo_ref, bf16[2,8,640,256]{3,2,1,0:T(8,128)(2,1)} %bitcast.56, bf16[256,2048]{1,0:T(8,128)(2,1)} %down_project.2.resid_ref), custom_call_target="tpu_custom_call" | custom-call | flops 40000000000 | bytes 16777216 | tf_op jit(solution)/shard_map/down_project/pallas_call | solution.py:364
  481.1 0.7 pad_maximum_fusion.7
  481.8 0.7 pad_maximum_fusion.6
  482.5 2.3 copy.23
  (37 shorter events, 0.2 us)
Async XLA Ops:
  7.2 170.0 %all-gather.5.cloned.1.call-start = ((), (), s32[]{:S(2)}) async-start(), calls=%async_computation | async-start | bytes 11141120 | tf_op jit(solution)/shard_map/all_gather | solution.py:412
  7.2 3.5 copy-start.7
  10.7 34.2 %copy-start.8 = (bf16[2,128,256]{2,1,0:T(8,128)(2,1)S(1)}, bf16[2,128,256]{2,1,0:T(8,128)(2,1)}, u32[]{:S(2)}) copy-start(bf16[2,128,256]{2,1,0:T(8,128)(2,1)} %param.12) | copy-start | bytes 393220
  10.7 34.2 %copy-start.4 = (bf16[2,512,256]{2,1,0:T(8,128)(2,1)S(1)}, bf16[2,512,256]{2,1,0:T(8,128)(2,1)}, u32[]{:S(2)}) copy-start(bf16[2,512,256]{2,1,0:T(8,128)(2,1)} %param.13) | copy-start | bytes 1572868
  10.8 33.1 %collective-permute-start = (bf16[256,1280]{1,0:T(8,128)(2,1)S(1)}, bf16[256,1280]{1,0:T(8,128)(2,1)S(1)}, u32[]{:S(2)}, u32[]{:S(2)}) collective-permute-start(bf16[256,1280]{1,0:T(8,128)(2,1)S(1)} %pad_maximum_fusion), channel_id=1, source_target_pairs={{0,0},{1,8},{2,16},{3,24},{4,32},{5,40},{6,48},{7,56},{8,64},{9,72... | collective-permute-start | bytes 1966088 | tf_op jit(solution)/shard_map/ppermute | solution.py:410
  43.9 0.8 copy-start.2
  44.8 194.0 %all-gather.7.cloned.1.call-start = ((), (), s32[]{:S(2)}) async-start(), calls=%async_computation.1 | async-start | bytes 5570560 | tf_op jit(solution)/shard_map/all_gather | solution.py:413
  45.0 16.0 %collective-permute-start.1 = (bf16[640,256]{1,0:T(8,128)(2,1)S(1)}, bf16[640,256]{1,0:T(8,128)(2,1)S(1)}, u32[]{:S(2)}, u32[]{:S(2)}) collective-permute-start(bf16[640,256]{1,0:T(8,128)(2,1)S(1)} %pad_maximum_fusion.2), channel_id=1, source_target_pairs={{0,0},{1,8},{2,16},{3,24},{4,32},{5,40},{6,48},{7,56},{8,64},{9,72... | collective-permute-start | bytes 983048 | tf_op jit(solution)/shard_map/ppermute | solution.py:411
  61.0 0.7 copy-start.5
  61.0 55.3 %copy-start = (bf16[1,256,2048]{2,1,0:T(8,128)(2,1)S(1)}, bf16[1,256,2048]{2,1,0:T(8,128)(2,1)}, u32[]{:S(2)}) copy-start(bf16[1,256,2048]{2,1,0:T(8,128)(2,1)} %param.7) | copy-start | bytes 3145732
  61.7 305.2 %all-gather.9.cloned.1.call-start = ((), (), s32[]{:S(2)}) async-start(), calls=%async_computation.2 | async-start | bytes 11141120 | tf_op jit(solution)/shard_map/all_gather | solution.py:412
  61.9 55.1 %copy-start.13 = (f32[2,2048]{1,0:T(2,128)S(1)}, f32[2,2048]{1,0:T(2,128)}, u32[]{:S(2)}) copy-start(f32[2,2048]{1,0:T(2,128)} %param.8) | copy-start | bytes 49156
  61.9 44.7 %collective-permute-start.2 = (bf16[256,1280]{1,0:T(8,128)(2,1)S(1)}, bf16[256,1280]{1,0:T(8,128)(2,1)S(1)}, u32[]{:S(2)}, u32[]{:S(2)}) collective-permute-start(bf16[256,1280]{1,0:T(8,128)(2,1)S(1)} %pad_maximum_fusion.1), channel_id=1, source_target_pairs={{0,0},{1,8},{2,16},{3,24},{4,32},{5,40},{6,48},{7,56},{8,64},{9,72... | collective-permute-start | bytes 1966088 | tf_op jit(solution)/shard_map/ppermute | solution.py:410
  106.7 0.8 copy-start.3
  107.5 293.2 %all-gather.11.cloned.1.call-start = ((), (), s32[]{:S(2)}) async-start(), calls=%async_computation.3 | async-start | bytes 5570560 | tf_op jit(solution)/shard_map/all_gather | solution.py:413
  107.6 67.6 %collective-permute-start.3 = (bf16[640,256]{1,0:T(8,128)(2,1)S(1)}, bf16[640,256]{1,0:T(8,128)(2,1)S(1)}, u32[]{:S(2)}, u32[]{:S(2)}) collective-permute-start(bf16[640,256]{1,0:T(8,128)(2,1)S(1)} %pad_maximum_fusion.3), channel_id=1, source_target_pairs={{0,0},{1,8},{2,16},{3,24},{4,32},{5,40},{6,48},{7,56},{8,64},{9,72... | collective-permute-start | bytes 983048 | tf_op jit(solution)/shard_map/ppermute | solution.py:411
  175.2 0.7 copy-start.6
  320.8 3.2 copy-start.1
  400.8 80.4 %copy-start.10 = (bf16[256,128]{1,0:T(8,128)(2,1)S(1)}, bf16[256,128]{1,0:T(8,128)(2,1)}, u32[]{:S(2)}) copy-start(bf16[256,128]{1,0:T(8,128)(2,1)} %get-tuple-element.13) | copy-start | bytes 196612
  400.8 80.4 %copy-start.12 = (bf16[256,128]{1,0:T(8,128)(2,1)S(1)}, bf16[256,128]{1,0:T(8,128)(2,1)}, u32[]{:S(2)}) copy-start(bf16[256,128]{1,0:T(8,128)(2,1)} %get-tuple-element.14) | copy-start | bytes 196612
  400.8 81.0 %copy-start.9 = (bf16[256,128]{1,0:T(8,128)(2,1)S(1)}, bf16[256,128]{1,0:T(8,128)(2,1)}, u32[]{:S(2)}) copy-start(bf16[256,128]{1,0:T(8,128)(2,1)} %get-tuple-element.11) | copy-start | bytes 196612
  400.8 81.0 %copy-start.11 = (bf16[256,128]{1,0:T(8,128)(2,1)S(1)}, bf16[256,128]{1,0:T(8,128)(2,1)}, u32[]{:S(2)}) copy-start(bf16[256,128]{1,0:T(8,128)(2,1)} %get-tuple-element.12) | copy-start | bytes 196612
Sparse Core Ops, SparseCore 0:
  44.9 132.1 all-gather.4
  179.3 59.4 all-gather.6
  241.0 80.0 all-gather.8
  323.0 55.5 all-gather.10

commit v3 on v2

v3 whole, which is shorter than its diff:
```python
import functools

import jax
import jax.numpy as jnp
from jax import lax
from jax.experimental import pallas as pl
from jax.experimental.pallas import tpu as pltpu
from jax.sharding import PartitionSpec as P

LN_EPS = 1e-6
ROPE_BASE = 10000.0
MESH = pl.DeviceIdType.MESH
VMEM_LIMIT = 60 * 1024 * 1024


def rope_tables(seq_len, head_dim):
    half_dim = head_dim // 2
    inv_freq = ROPE_BASE ** (-2.0 * jnp.arange(half_dim, dtype=jnp.float32) / head_dim)
    angles = jnp.arange(seq_len, dtype=jnp.float32)[:, None] * inv_freq[None, :]
    cos, sin = jnp.cos(angles), jnp.sin(angles)
    return jnp.concatenate([cos, cos], axis=1), jnp.concatenate([-sin, sin], axis=1)


def layer_norm(resid, g_scale):
    resid_f = resid.astype(jnp.float32)
    centered = resid_f - jnp.mean(resid_f, axis=-1, keepdims=True)
    variance = jnp.mean(centered * centered, axis=-1, keepdims=True)
    return (centered * lax.rsqrt(variance + LN_EPS) * g_scale).astype(jnp.bfloat16)


def ring_ids(n_wx):
    me = lax.axis_index('wx')
    chip, core = lax.div(me, 2), lax.rem(me, 2)
    n_chip = n_wx // 2

    def at(step, other=0):
        return lax.rem(chip + step, n_chip) * 2 + (lax.rem(core + other, 2))

    return me, chip, core, at


def entry_barrier(peers):
    barrier = pltpu.get_barrier_semaphore()
    for peer in peers:
        pl.semaphore_signal(barrier, inc=1, device_id={'wx': peer}, device_id_type=MESH)
    pl.semaphore_wait(barrier, len(peers))


def gather_copies(n_wx, hall, send_sem, recv_sem):
    me, chip, core, at = ring_ids(n_wx)
    half = hall.shape[1] // 2
    right, left, partner = at(1), at(3), at(0, 1)
    top, bottom, whole = pl.ds(0, half), pl.ds(half, half), pl.ds(0, 2 * half)

    def copy(num, block, rows, target):
        ref = hall.at[block, rows]
        return pltpu.make_async_remote_copy(
            src_ref=ref, dst_ref=ref, send_sem=send_sem.at[num], recv_sem=recv_sem.at[num],
            device_id={'wx': target}, device_id_type=MESH)

    return [
        copy(0, me, whole, partner),
        copy(1, me, top, right), copy(2, me, bottom, left),
        copy(3, me, bottom, right), copy(4, me, top, left),
        copy(5, left, top, right), copy(6, right, bottom, left),
        copy(7, left, whole, partner), copy(8, right, whole, partner),
        copy(9, at(2), top, partner), copy(10, at(2), bottom, partner),
    ]


def arrivals(n_wx, hall, send_sem, recv_sem):
    me, chip, core, at = ring_ids(n_wx)
    half = hall.shape[1] // 2
    top, bottom, whole = pl.ds(0, half), pl.ds(half, half), pl.ds(0, 2 * half)

    def copy(num, block, rows):
        ref = hall.at[block, rows]
        return pltpu.make_async_remote_copy(
            src_ref=ref, dst_ref=ref, send_sem=send_sem.at[num], recv_sem=recv_sem.at[num],
            device_id={'wx': at(0, 1)}, device_id_type=MESH)

    return [
        copy(0, at(0, 1), whole),
        copy(1, at(3), top), copy(2, at(1), bottom), copy(3, at(3), bottom), copy(4, at(1), top),
        copy(5, at(2), top), copy(6, at(2), bottom),
        copy(7, at(3, 1), whole), copy(8, at(1, 1), whole),
        copy(9, at(2, 1), top), copy(10, at(2, 1), bottom),
    ]


PLANE = 4


class PlaneGather:
    def __init__(self, buf, send_sem, recv_sem):
        self.buf, self.send_sem, self.recv_sem = buf, send_sem, recv_sem
        pos = lax.axis_index('wy')
        self.pos = (lax.div(pos, PLANE), lax.rem(pos, PLANE))

    def at(self, half, first, second):
        step_z, step_y = (second, first) if half == 0 else (first, second)
        z, y = self.pos
        return lax.rem(z + step_z + PLANE, PLANE) * PLANE + lax.rem(y + step_y + PLANE, PLANE)

    def copy(self, num, block, half, quarter, target):
        rows = self.buf.shape[1]
        size = rows // 2 if quarter is None else rows // 4
        start = half * (rows // 2) + (quarter or 0) * size
        ref = self.buf.at[block, pl.ds(start, size)]
        return pltpu.make_async_remote_copy(
            src_ref=ref, dst_ref=ref, send_sem=self.send_sem.at[num], recv_sem=self.recv_sem.at[num],
            device_id={'wy': target}, device_id_type=MESH)

    def one(self, half, sign, landing=False):
        num = half * 2 + (sign < 0)
        block = self.at(half, -sign if landing else 0, 0)
        return self.copy(num, block, half, None, self.at(half, sign, 0))

    def two(self, half, sign, landing=False):
        num = 4 + half * 2 + (sign < 0)
        block = self.at(half, -2 * sign if landing else -sign, 0)
        return self.copy(num, block, half, int(sign < 0), self.at(half, sign, 0))

    def three(self, half, off, sign, landing=False):
        num = 8 + (half * 4 + off % 4) * 2 + (sign < 0)
        block = self.at(half, off, -sign if landing else 0)
        return self.copy(num, block, half, None, self.at(half, 0, sign))

    def four(self, half, off, sign, landing=False):
        num = 24 + (half * 4 + off % 4) * 2 + (sign < 0)
        block = self.at(half, off, -2 * sign if landing else -sign)
        return self.copy(num, block, half, int(sign < 0), self.at(half, 0, sign))

    ways = [(half, sign) for half in range(2) for sign in (1, -1)]

    def start(self):
        for half, sign in self.ways:
            self.one(half, sign).start()
        for half, sign in self.ways:
            self.three(half, 0, sign).start()

    def stage_1(self):
        for half, sign in self.ways:
            self.one(half, sign, True).wait_recv()
            self.two(half, sign).start()
        for half, sign in self.ways:
            for way in (1, -1):
                self.three(half, -sign, way).start()

    def stage_2(self):
        for half, sign in self.ways:
            self.three(half, 0, sign, True).wait_recv()
            self.four(half, 0, sign).start()

    def stage_3(self):
        for half, sign in self.ways:
            self.two(half, sign, True).wait_recv()
        for half, sign in self.ways:
            self.three(half, 2, sign).start()

    def stage_4(self):
        for half, sign in self.ways:
            for off in (1, -1):
                self.three(half, off, sign, True).wait_recv()
                self.four(half, off, sign).start()

    def stage_5(self):
        for half, sign in self.ways:
            self.three(half, 2, sign, True).wait_recv()
            self.four(half, 2, sign).start()

    def finish(self):
        for half, sign in self.ways:
            for off in (0, 1, -1, 2):
                self.four(half, off, sign, True).wait_recv()

    def drain(self):
        for half, sign in self.ways:
            self.one(half, sign).wait_send()
            self.two(half, sign).wait_send()
            for off in (0, 1, -1, 2):
                self.three(half, off, sign).wait_send()
                self.four(half, off, sign).wait_send()


def up_step(hall, wa, mo, kv_out, xt, cos, sin, f_loc, head_dim):
    seq, d_model = hall.shape[1], hall.shape[2]
    n_w = wa.shape[0] // 2
    first = pl.multiple_of(xt * 2 * seq, 2 * seq)
    h = hall[pl.ds(xt * 2, 2)].reshape(2 * seq, d_model)
    width = f_loc + head_dim

    def project(hh, lo, hi):
        weight = wa[hh * n_w:(hh + 1) * n_w, :, lo:hi].reshape(d_model, hi - lo)
        return jnp.dot(h, weight, preferred_element_type=jnp.float32).astype(jnp.bfloat16)

    narrow = [project(hh, 2 * f_loc, 2 * (f_loc + head_dim)) for hh in range(2)]
    for hh in range(2):
        g_f = project(hh, 0, f_loc).astype(jnp.float32)
        u_f = project(hh, f_loc, 2 * f_loc).astype(jnp.float32)
        hidden = g_f * (1.0 / (1.0 + jnp.exp(-g_f))) * u_f
        mo[pl.ds(first, 2 * seq), hh * width:hh * width + f_loc] = hidden.astype(jnp.bfloat16)

    def rot(val):
        val_f = val.astype(jnp.float32)
        return (val_f * cos + pltpu.roll(val_f, head_dim // 2, 1) * sin).astype(jnp.bfloat16)

    allowed = lax.broadcasted_iota(jnp.int32, (seq, seq), 0) >= lax.broadcasted_iota(jnp.int32, (seq, seq), 1)
    for b in range(2):
        part = slice(b * seq, (b + 1) * seq)
        k_rot = rot(narrow[0][part, head_dim:])
        v_val = narrow[1][part, head_dim:]
        kv_out[b, 0] = k_rot
        kv_out[b, 1] = v_val
        for hh in range(2):
            q_rot = rot(narrow[hh][part, :head_dim])
            scores = lax.dot_general(q_rot, k_rot, (((1,), (1,)), ((), ())), preferred_element_type=jnp.float32) * head_dim ** -0.5
            scores = jnp.where(allowed, scores, -jnp.inf)
            top = jnp.max(scores, axis=-1, keepdims=True)
            expd = jnp.exp(scores - top)
            probs = (expd / jnp.sum(expd, axis=-1, keepdims=True)).astype(jnp.bfloat16)
            att = jnp.dot(probs, v_val, preferred_element_type=jnp.float32)
            mo[pl.ds(first + b * seq, seq), hh * width + f_loc:(hh + 1) * width] = att.astype(jnp.bfloat16)


def up_kernel(n_wx, f_loc, head_dim, gathers, *refs):
    if gathers:
        (h_ref, wa_ref, wb_ref, cos_ref, sin_ref, mo_ref, k_ref, v_ref, wb_out, hall, wa, mo, kv, send_sem, recv_sem, own_sem, w_sem, out_sem, kv_sem,
         wb, a_send, a_recv, b_send, b_recv, wb_sem) = refs
    else:
        h_ref, wa_ref, cos_ref, sin_ref, mo_ref, k_ref, v_ref, hall, wa, mo, kv, send_sem, recv_sem, own_sem, w_sem, out_sem, kv_sem = refs
    me, chip, core, at = ring_ids(n_wx)
    n_chip = n_wx // 2
    seq = hall.shape[1]
    sends = gather_copies(n_wx, hall, send_sem, recv_sem)
    lands = arrivals(n_wx, hall, send_sem, recv_sem)
    own_load = pltpu.make_async_copy(h_ref, hall.at[me], own_sem)
    own_load.start()
    if gathers:
        here = lax.axis_index('wy')
        gather_a = PlaneGather(wa, a_send, a_recv)
        gather_b = PlaneGather(wb, b_send, b_recv)
        a_load = pltpu.make_async_copy(wa_ref, wa.at[here], w_sem.at[0])
        b_load = pltpu.make_async_copy(wb_ref, wb.at[here], w_sem.at[1])
        a_load.start()
        b_load.start()
    else:
        half_w = wa.shape[0] // 2
        w_loads = [pltpu.make_async_copy(wa_ref.at[pl.ds(hh * half_w, half_w)], wa.at[pl.ds(hh * half_w, half_w)], w_sem.at[hh]) for hh in range(2)]
        for load in w_loads:
            load.start()
    barrier = pltpu.get_barrier_semaphore()
    peers = [{'wx': at(1)}, {'wx': at(3)}, {'wx': at(0, 1)}]
    if gathers:
        peers += [{'wy': gather_a.at(0, 1, 0)}, {'wy': gather_a.at(0, -1, 0)}, {'wy': gather_a.at(1, 1, 0)}, {'wy': gather_a.at(1, -1, 0)}]
    for peer in peers:
        pl.semaphore_signal(barrier, inc=1, device_id=peer, device_id_type=MESH)
    pl.semaphore_wait(barrier, len(peers))
    own_load.wait()
    for num in range(5):
        sends[num].start()
    if gathers:
        a_load.wait()
        gather_a.start()
        gather_a.stage_1()
        lands[1].wait_recv()
        sends[5].start()
        lands[2].wait_recv()
        sends[6].start()
        gather_a.stage_2()
        gather_a.stage_3()
        lands[3].wait_recv()
        sends[7].start()
        lands[4].wait_recv()
        sends[8].start()
        lands[0].wait_recv()
        gather_a.stage_4()
        lands[5].wait_recv()
        sends[9].start()
        lands[6].wait_recv()
        sends[10].start()
        gather_a.stage_5()
        b_load.wait()
        gather_b.start()
        for num in range(7, 11):
            lands[num].wait_recv()
        gather_a.finish()
    else:
        for load in w_loads:
            load.wait()

    def out_copy(xt):
        rows = pl.ds(pl.multiple_of(xt * 2 * seq, 2 * seq), 2 * seq)
        return pltpu.make_async_copy(mo.at[rows], mo_ref.at[rows], out_sem.at[xt])

    def body(step, carry):
        off = jnp.where(step == 0, 0, jnp.where(step == 1, 3, jnp.where(step == 2, 1, 2)))
        xt = lax.rem(chip + off, n_chip)
        if gathers:
            @pl.when(step == 1)
            def _():
                gather_b.stage_1()

            @pl.when(step == 2)
            def _():
                gather_b.stage_2()
                gather_b.stage_3()

            @pl.when(step == 3)
            def _():
                gather_b.stage_4()
                gather_b.stage_5()
        else:
            @pl.when(step == 0)
            def _():
                lands[0].wait_recv()

            @pl.when(step == 1)
            def _():
                lands[1].wait_recv()
                sends[5].start()
                lands[2].wait_recv()
                sends[6].start()
                lands[3].wait_recv()
                sends[7].start()
                lands[4].wait_recv()
                sends[8].start()
                lands[7].wait_recv()

            @pl.when(step == 2)
            def _():
                lands[8].wait_recv()

            @pl.when(step == 3)
            def _():
                lands[5].wait_recv()
                sends[9].start()
                lands[6].wait_recv()
                sends[10].start()
                lands[9].wait_recv()
                lands[10].wait_recv()

        up_step(hall, wa, mo, kv.at[step], xt, cos_ref[...], sin_ref[...], f_loc, head_dim)
        out_copy(xt).start()
        return carry

    lax.fori_loop(0, n_chip, body, 0)
    caches = [pltpu.make_async_copy(kv.at[0, core, num], ref, kv_sem.at[num]) for num, ref in enumerate((k_ref, v_ref))]
    for cache in caches:
        cache.start()
    if gathers:
        gather_b.finish()
        wb_copy = pltpu.make_async_copy(wb, wb_out, wb_sem)
        wb_copy.start()
        wb_copy.wait()
        gather_a.drain()
        gather_b.drain()
    for num in range(11):
        sends[num].wait_send()
    for xt in range(n_chip):
        out_copy(xt).wait()
    for cache in caches:
        cache.wait()


def up_project(h, wa, wb, cos, sin, f_loc, head_dim, n_wx, gathers):
    seq, d_model = h.shape
    n_chip = n_wx // 2
    n_block = PLANE * PLANE
    width = 2 * (f_loc + head_dim)
    any_spec, vmem_spec = pl.BlockSpec(memory_space=pl.ANY), pl.BlockSpec(memory_space=pltpu.VMEM)
    out_shape = [
        jax.ShapeDtypeStruct((n_wx * seq, width), jnp.bfloat16),
        jax.ShapeDtypeStruct((seq, head_dim), jnp.bfloat16),
        jax.ShapeDtypeStruct((seq, head_dim), jnp.bfloat16),
    ]
    wa_shape = (n_block,) + wa.shape if gathers else wa.shape
    scratch = [
        pltpu.VMEM((n_wx, seq, d_model), jnp.bfloat16),
        pltpu.VMEM(wa_shape, jnp.bfloat16),
        pltpu.VMEM((n_wx * seq, width), jnp.bfloat16),
        pltpu.VMEM((n_chip, 2, 2, seq, head_dim), jnp.bfloat16),
        pltpu.SemaphoreType.DMA((11,)), pltpu.SemaphoreType.DMA((11,)),
        pltpu.SemaphoreType.DMA, pltpu.SemaphoreType.DMA((2,)),
        pltpu.SemaphoreType.DMA((n_chip,)), pltpu.SemaphoreType.DMA((2,)),
    ]
    args = [h, wa, cos, sin]
    in_specs = [any_spec, any_spec, vmem_spec, vmem_spec]
    if gathers:
        out_shape.append(jax.ShapeDtypeStruct((n_block,) + wb.shape, jnp.bfloat16))
        scratch += [
            pltpu.VMEM((n_block,) + wb.shape, jnp.bfloat16),
            pltpu.SemaphoreType.DMA((40,)), pltpu.SemaphoreType.DMA((40,)),
            pltpu.SemaphoreType.DMA((40,)), pltpu.SemaphoreType.DMA((40,)),
            pltpu.SemaphoreType.DMA,
        ]
        args.insert(2, wb)
        in_specs.insert(2, any_spec)
    return pl.pallas_call(
        functools.partial(up_kernel, n_wx, f_loc, head_dim, gathers),
        out_shape=tuple(out_shape),
        in_specs=in_specs,
        out_specs=[any_spec] * len(out_shape),
        scratch_shapes=scratch,
        compiler_params=pltpu.CompilerParams(collective_id=0 if gathers else 2, has_side_effects=True, vmem_limit_bytes=VMEM_LIMIT),
        cost_estimate=pl.CostEstimate(flops=40_000_000_000, bytes_accessed=24 * 2**20, transcendentals=0),
        name='up_gather' if gathers else 'up_project',
    )(*args)


N_COL = 4


def down_kernel(n_wx, normed, mo_ref, wb_ref, resid_ref, gamma_ref, *refs):
    if normed:
        out_ref, h_ref = refs[:2]
    else:
        out_ref = refs[0]
    (mo, wb, given, taken, acc, landed, mo_sem, wb_sem, pair_send, pair_recv, ring_send, ring_recv) = refs[1 + normed:]
    me, chip, core, at = ring_ids(n_wx)
    n_chip = n_wx // 2
    right, left, partner = at(1), at(3), at(0, 1)
    seq = resid_ref.shape[0]
    n_block, k_loc, col_w = wb_ref.shape
    n_w = n_wx
    n_hh = n_block // n_w
    col = wb.shape[1] // N_COL

    def step_of(i):
        phase, j = lax.div(i, 4), lax.rem(i, 4)
        odd, slot = lax.rem(j, 2), lax.div(j, 2)
        off = jnp.where(phase == 0, 2, jnp.where(phase == 3, 0, 1 + 2 * odd))
        q = jnp.where(phase == 3, j, jnp.where(phase == 1, (1 - odd) * 2 + slot, odd * 2 + slot))
        return lax.rem(chip + off, n_chip), q, odd

    def mo_load(off):
        rows = pl.ds(pl.multiple_of(lax.rem(chip + off, n_chip) * 2 * seq, 2 * seq), 2 * seq)
        return pltpu.make_async_copy(mo_ref.at[rows], mo.at[rows], mo_sem.at[off])

    def wb_load(hh, w):
        return pltpu.make_async_copy(
            wb_ref.at[hh * n_w + w], wb.at[pl.ds(hh * k_loc, k_loc), pl.ds(w * col_w, col_w)], wb_sem.at[hh * n_w + w])

    def pair_copy(i):
        return pltpu.make_async_remote_copy(
            src_ref=given.at[i], dst_ref=taken.at[i], send_sem=pair_send.at[i], recv_sem=pair_recv.at[i],
            device_id={'wx': partner}, device_id_type=MESH)

    def ring_copy(k, odd):
        return pltpu.make_async_remote_copy(
            src_ref=acc.at[k], dst_ref=landed.at[k], send_sem=ring_send.at[k], recv_sem=ring_recv.at[k],
            device_id={'wx': jnp.where(odd == 0, right, left)}, device_id_type=MESH)

    mo_load(2).start()
    for hh in range(n_hh):
        for w in range(n_w):
            wb_load(hh, w).start()
    for off in (1, 3, 0):
        mo_load(off).start()
    entry_barrier([right, left, partner])
    mo_load(2).wait()
    for hh in range(n_hh):
        for w in range(n_w):
            wb_load(hh, w).wait()
    for off in (1, 3, 0):
        mo_load(off).wait()

    def dot_of(i, which):
        xt, q, _ = step_of(i)
        rows = pl.ds(pl.multiple_of((xt * 2 + which) * seq, seq), seq)
        cols = pl.ds(pl.multiple_of(q * col, col), col)
        return jnp.dot(mo[rows, :], wb[:, cols], preferred_element_type=jnp.float32)

    def body(i, carry):
        given[i] = dot_of(i, 1 - core)

        @pl.when(i > 0)
        def _():
            pair_copy(i - 1).wait_recv()
            acc[i - 1] = acc[i - 1] + taken[i - 1]

        acc[i] = dot_of(i, core)
        pair_copy(i).start()

        @pl.when((i > 0) & (i <= 8))
        def _():
            ring_copy(i - 1, lax.rem(i - 1, 2)).start()

        return carry

    n_step = 4 * N_COL
    lax.fori_loop(0, n_step, body, 0)
    pair_copy(n_step - 1).wait_recv()
    acc[n_step - 1] = acc[n_step - 1] + taken[n_step - 1]
    for pair in range(2):
        for odd in range(2):
            k = 8 + pair * 2 + odd
            ring_copy(k - 8, odd).wait_recv()
            acc[k] = acc[k] + landed[k - 8]
        for q in (pair, pair + 2):
            cols = slice(q * col, (q + 1) * col)
            acc[12 + q] = acc[12 + q] + resid_ref[:, cols].astype(jnp.float32)
        for odd in range(2):
            ring_copy(8 + pair * 2 + odd, odd).start()
    for q, (raw, comb) in ((0, (5, 8)), (2, (4, 9)), (1, (7, 10)), (3, (6, 11))):
        ring_copy(raw, raw % 2).wait_recv()
        ring_copy(comb, comb % 2).wait_recv()
        cols = slice(q * col, (q + 1) * col)
        out_ref[:, cols] = (acc[12 + q] + (landed[raw] + landed[comb])).astype(jnp.bfloat16)
    if normed:
        resid_f = out_ref[...].astype(jnp.float32)
        centered = resid_f - jnp.mean(resid_f, axis=-1, keepdims=True)
        variance = jnp.mean(centered * centered, axis=-1, keepdims=True)
        h_ref[...] = (centered * lax.rsqrt(variance + LN_EPS) * gamma_ref[...]).astype(jnp.bfloat16)
    for i in range(n_step):
        pair_copy(i).wait_send()
    for k in range(12):
        ring_copy(k, k % 2).wait_send()


def down_project(mo, wb, resid, gamma, n_wx, normed):
    seq, d_model = resid.shape
    col = d_model // N_COL
    n_block, k_loc, col_w = wb.shape
    n_w = n_wx
    n_hh = n_block // n_w
    n_step = 4 * N_COL
    return pl.pallas_call(
        functools.partial(down_kernel, n_wx, normed),
        out_shape=(jax.ShapeDtypeStruct((seq, d_model), jnp.bfloat16),) * (1 + normed),
        in_specs=[pl.BlockSpec(memory_space=pl.ANY), pl.BlockSpec(memory_space=pl.ANY), pl.BlockSpec(memory_space=pltpu.VMEM),
                  pl.BlockSpec(memory_space=pltpu.VMEM)],
        out_specs=[pl.BlockSpec(memory_space=pltpu.VMEM)] * (1 + normed),
        scratch_shapes=[
            pltpu.VMEM(mo.shape, jnp.bfloat16),
            pltpu.VMEM((n_hh * k_loc, n_w * col_w), jnp.bfloat16),
            pltpu.VMEM((n_step, seq, col), jnp.float32),
            pltpu.VMEM((n_step, seq, col), jnp.float32),
            pltpu.VMEM((n_step, seq, col), jnp.float32),
            pltpu.VMEM((12, seq, col), jnp.float32),
            pltpu.SemaphoreType.DMA((4,)), pltpu.SemaphoreType.DMA((n_hh * n_w,)),
            pltpu.SemaphoreType.DMA((n_step,)), pltpu.SemaphoreType.DMA((n_step,)),
            pltpu.SemaphoreType.DMA((12,)), pltpu.SemaphoreType.DMA((12,)),
        ],
        compiler_params=pltpu.CompilerParams(collective_id=1 if normed else 3, has_side_effects=True, vmem_limit_bytes=VMEM_LIMIT),
        cost_estimate=pl.CostEstimate(flops=40_000_000_000, bytes_accessed=16 * 2**20, transcendentals=0),
        name='down_project',
    )(mo, wb, resid, gamma)


def solution(mesh):
    batch_axes = ('dp', 'wy', 'wx')
    in_specs = (P(batch_axes), P(), P(None, 'wx', 'wy'), P(None, 'wx'), P(None, 'wx', None, 'wy'), P(None, 'wy', 'wx'), P(None, 'wy', 'wx'))
    out_specs = (P(batch_axes), P(None, batch_axes), P(None, batch_axes))
    n_wy, n_wx = mesh.shape['wy'], mesh.shape['wx']
    per = n_wy // n_wx
    perm = []
    for iy in range(n_wy):
        for ix in range(n_wx):
            perm.append((iy * n_wx + ix, ((iy % per) * n_wx + ix) * n_wx + iy // per))

    def device_step(x_tokens, gamma_ln, w_q, w_kv, w_gu, w_o, w_d):
        seq_len, d_model = x_tokens.shape[1], x_tokens.shape[2]
        head_dim = w_kv.shape[-1]
        d_loc = w_q.shape[1]
        f_loc = w_gu.shape[-1]
        cos_tab, sin_tab = rope_tables(seq_len, head_dim)
        iy = lax.axis_index('wy')
        packs = []
        for layer_idx in range(2):
            kv_half = lax.dynamic_index_in_dim(w_kv[layer_idx], lax.rem(iy, per), axis=1, keepdims=False)
            pack_a = jnp.concatenate([w_gu[layer_idx].reshape(d_loc, 2 * f_loc), w_q[layer_idx], kv_half], axis=1)
            pack_b = jnp.concatenate([w_d[layer_idx], w_o[layer_idx]], axis=0)
            if layer_idx:
                pack_a, pack_b, packs[0][0], packs[0][1] = lax.optimization_barrier((pack_a, pack_b, packs[0][0], packs[0][1]))
            packs.append([lax.ppermute(pack, ('wy', 'wx'), perm) for pack in (pack_a, pack_b)])
        resid = x_tokens[0]
        normed = layer_norm(resid, gamma_ln[0])
        mo, k_0, v_0, wb_0 = up_project(normed, packs[0][0], packs[0][1], cos_tab, sin_tab, f_loc, head_dim, n_wx, True)
        pack_a, pack_b, mo, wb_0 = lax.optimization_barrier((packs[1][0], packs[1][1], mo, wb_0))
        wa_1 = lax.all_gather(pack_a, 'wy', axis=0, tiled=True).reshape((n_wy,) + pack_a.shape)
        wb_1 = lax.all_gather(pack_b, 'wy', axis=0, tiled=True).reshape((n_wy,) + pack_b.shape)
        resid, normed = down_project(mo, wb_0, resid, gamma_ln[1:], n_wx, True)
        mo, k_1, v_1 = up_project(normed, wa_1, None, cos_tab, sin_tab, f_loc, head_dim, n_wx, False)
        resid, = down_project(mo, wb_1, resid, gamma_ln[1:], n_wx, False)
        return resid[None], jnp.stack([k_0, k_1])[:, None], jnp.stack([v_0, v_1])[:, None]

    return jax.shard_map(device_step, mesh=mesh, in_specs=in_specs, out_specs=out_specs, check_vma=False)
```

time: 492 us -> 445 us (0.904)
  waiting for transfers between devices: 99.4 us -> 32.8 us
  Pallas kernels: 327 us -> 352 us
    ppermute x4, waiting for transfers between devices: 70.2 us -> 30.3 us  [device_step(): lax.ppermute(pack, ('wy', 'wx'), perm)]
    all_gather x4 -> x2, waiting for transfers between devices: 29.1 us -> 2.01 us  [the longest x1 1.99 us: device_step(): lax.all_gather(pack_b, 'wy', axis=0, tiled=True)]
    pallas_call x6 -> x4, Pallas kernels: 327 us -> 352 us  [the longest x2 177 us: up_project(): pl.pallas_call(functools.partial(up_kernel, n_wx, f_loc, head_dim, gather...]
  transfers between devices with their start and end apart: 8 -> 6, of which waited for: 5 -> 3; matrix products, arithmetic and copies ran while one was open for 2% -> 1% of each run, Pallas kernels for 50% -> 61%
where the time goes in v3:
time: 445 us; the launch traced here: 444 us
  Pallas kernels  352 us (79%)
  waiting for transfers between devices  32.8 us (7%)
  starting transfers between devices  32 us (7%)
  between operations  14.4 us (3%)
  local copies, waits for them, and re-layouts  8.09 us (2%)
  other arithmetic  4.85 us (1%)
    pallas_call x2, Pallas kernels, up_project(): pl.pallas_call(functools.partial(up_kernel, n_wx, f_loc, head_dim, gather...  177 us
    pallas_call x2, Pallas kernels, down_project(): pl.pallas_call(functools.partial(down_kernel, n_wx, normed), out_shape=(j...  175 us
    ppermute x4, starting transfers between devices, device_step(): lax.ppermute(pack, ('wy', 'wx'), perm)  31.7 us
    ppermute x4, waiting for transfers between devices, device_step(): lax.ppermute(pack, ('wy', 'wx'), perm)  30.3 us
  transfers between devices with their start and end apart: 6, of which 3 were waited for; matrix products, arithmetic and copies ran while one was open for 1% of the time, Pallas kernels for 61%

profile of v3, /device:TPU:1, one launch (start us, length us, event | category | flops | bytes accessed | tf_op | source)
XLA Modules:
  0.0 444.1 jit_solution(15929230263744065278)
XLA Ops:
  7.2 0.0 copy-start.4
  7.2 0.0 copy-start.1
  7.2 0.0 all-gather.3.cloned.1.call-start
  7.2 1.0 slice_bitcast_fusion.2
  8.2 1.1 slice_bitcast_fusion
  9.3 4.6 %collective-permute-start.1 = (bf16[640,256]{1,0:T(8,128)(2,1)S(1)}, bf16[640,256]{1,0:T(8,128)(2,1)}, u32[]{:S(2)}, u32[]{:S(2)}) collective-permute-start(bf16[640,256]{1,0:T(8,128)(2,1)S(1)} %pad_maximum_fusion.3), channel_id=1, source_target_pairs={{0,0},{1,8},{2,16},{3,24},{4,32},{5,40},{6,48},{7,56},{8,64},{9,72... | collective-permute-start | bytes 983048 | tf_op jit(solution)/shard_map/ppermute | solution.py:576
  13.9 0.9 slice_bitcast_fusion.3
  14.8 0.0 copy-done.4
  14.8 0.2 fusion.9
  15.0 0.3 constant_dynamic-slice_fusion
  15.3 0.0 copy-done.1
  15.3 0.0 copy-start
  15.3 0.7 fusion.8
  16.1 0.0 copy-start.9
  16.1 0.1 copy.21
  16.2 0.1 pad_maximum_fusion.1
  16.2 5.7 %collective-permute-start = (bf16[256,1280]{1,0:T(8,128)(2,1)S(1)}, bf16[256,1280]{1,0:T(8,128)(2,1)S(1)}, u32[]{:S(2)}, u32[]{:S(2)}) collective-permute-start(bf16[256,1280]{1,0:T(8,128)(2,1)S(1)} %pad_maximum_fusion.1), channel_id=1, source_target_pairs={{0,0},{1,8},{2,16},{3,24},{4,32},{5,40},{6,48},{7,56},{8,64},{9,72... | collective-permute-start | bytes 1966088 | tf_op jit(solution)/shard_map/ppermute | solution.py:576
  21.9 0.0 copy-done
  21.9 0.2 convert_reduce_fusion
  22.1 0.4 fusion.2
  22.6 0.0 copy-done.9
  22.6 0.6 fusion.10
  23.2 1.4 fusion.4.refs_0_
  24.6 0.1 copy.20
  24.7 0.5 fusion.7
  25.2 0.8 pad_maximum_fusion.4
  26.0 0.1 pad_maximum_fusion
  26.1 17.1 %collective-permute-done.1.refs_2_ = bf16[640,256]{1,0:T(8,128)(2,1)} collective-permute-done((bf16[640,256]{1,0:T(8,128)(2,1)S(1)}, bf16[640,256]{1,0:T(8,128)(2,1)}, u32[]{:S(2)}, u32[]{:S(2)}) %collective-permute-start.1) | collective-permute-done | bytes 327712 | tf_op jit(solution)/shard_map/ppermute | solution.py:576
  43.2 13.2 %collective-permute-done.refs_1_ = bf16[256,1280]{1,0:T(8,128)(2,1)S(1)} collective-permute-done((bf16[256,1280]{1,0:T(8,128)(2,1)S(1)}, bf16[256,1280]{1,0:T(8,128)(2,1)S(1)}, u32[]{:S(2)}, u32[]{:S(2)}) %collective-permute-start) | collective-permute-done | bytes 655392 | tf_op jit(solution)/shard_map/ppermute | solution.py:576
  56.3 14.7 %collective-permute-start.3 = (bf16[640,256]{1,0:T(8,128)(2,1)S(1)}, bf16[640,256]{1,0:T(8,128)(2,1)S(1)}, u32[]{:S(2)}, u32[]{:S(2)}) collective-permute-start(bf16[640,256]{1,0:T(8,128)(2,1)S(1)} %pad_maximum_fusion.2), channel_id=1, source_target_pairs={{0,0},{1,8},{2,16},{3,24},{4,32},{5,40},{6,48},{7,56},{8,64},{9,72... | collective-permute-start | bytes 983048 | tf_op jit(solution)/shard_map/ppermute | solution.py:576
  71.0 6.8 %collective-permute-start.2 = (bf16[256,1280]{1,0:T(8,128)(2,1)S(1)}, bf16[256,1280]{1,0:T(8,128)(2,1)S(1)}, u32[]{:S(2)}, u32[]{:S(2)}) collective-permute-start(bf16[256,1280]{1,0:T(8,128)(2,1)S(1)} %pad_maximum_fusion), channel_id=1, source_target_pairs={{0,0},{1,8},{2,16},{3,24},{4,32},{5,40},{6,48},{7,56},{8,64},{9,72... | collective-permute-start | bytes 1966088 | tf_op jit(solution)/shard_map/ppermute | solution.py:576
  77.8 123.0 %up_gather.1 = (bf16[2048,1280]{1,0:T(8,128)(2,1)}, bf16[256,128]{1,0:T(8,128)(2,1)}, bf16[256,128]{1,0:T(8,128)(2,1)}, bf16[16,640,256]{2,1,0:T(8,128)(2,1)}) custom-call(bf16[256,2048]{1,0:T(8,128)(2,1)} %fusion.4.refs_0_, bf16[256,1280]{1,0:T(8,128)(2,1)} %copy-done.10, bf16[640,256]{1,0:T(8,128)(2,1)} %collective-permute-done.1.refs_2_, ...), custom_call_target="tpu_custom_call" | custom-call | flops 40000000000 | bytes 25165824 | tf_op jit(solution)/shard_map/up_gather/pallas_call | solution.py:399
  200.8 0.0 collective-permute-done.3
  200.8 0.0 collective-permute-done.2
  200.8 0.0 copy-start.2
  200.8 0.9 copy-done.2
  201.7 0.0 all-gather.3.cloned.1.call-update
  201.7 0.2 all-gather.5.cloned.1.call-start
  202.0 0.0 copy-done.3
  202.0 0.5 all-gather.5.cloned.1.call-update
  202.5 93.6 %down_project.2 = (bf16[256,2048]{1,0:T(8,128)(2,1)}, bf16[256,2048]{1,0:T(8,128)(2,1)}) custom-call(bf16[2048,1280]{1,0:T(8,128)(2,1)} %get-tuple-element.26.mo_ref, bf16[16,640,256]{2,1,0:T(8,128)(2,1)} %get-tuple-element.27.wb_ref, bf16[256,2048]{1,0:T(8,128)(2,1)} %bitcast.44, f32[1,2048]{1,0:T(1,128)} %get-tuple-element.53.gamma_ref), custom_call_target="tpu_custom_call" | custom-call | flops 40000000000 | bytes 16777216 | tf_op jit(solution)/shard_map/down_project/pallas_call | solution.py:528
  296.1 0.0 all-gather.3.cloned.1.call-done
  296.2 53.8 %up_project.1 = (bf16[2048,1280]{1,0:T(8,128)(2,1)}, bf16[256,128]{1,0:T(8,128)(2,1)}, bf16[256,128]{1,0:T(8,128)(2,1)}) custom-call(bf16[256,2048]{1,0:T(8,128)(2,1)} %get-tuple-element.28.refs_0_, bf16[16,256,1280]{2,1,0:T(8,128)(2,1)} %bitcast.57, f32[256,128]{1,0:T(8,128)} %get-tuple-element.60.refs_3_.refs_2_, f32[256,128]{1,0:T(8,128)} %get-tuple-element.61.refs_4_.refs_3_), custom_call_target="tpu_custom_call" | custom-call | flops 40000000000 | bytes 25165824 | tf_op jit(solution)/shard_map/up_project/pallas_call | solution.py:399
  349.9 2.0 all-gather.5.cloned.1.call-done
  351.9 81.7 %down_project.3 = bf16[256,2048]{1,0:T(8,128)(2,1)} custom-call(bf16[2048,1280]{1,0:T(8,128)(2,1)} %get-tuple-element.30.mo_ref, bf16[16,640,256]{2,1,0:T(8,128)(2,1)} %bitcast.58, bf16[256,2048]{1,0:T(8,128)(2,1)} %get-tuple-element.32.resid_ref, f32[1,2048]{1,0:T(1,128)} %get-tuple-element.53.gamma_ref), custom_call_target="tpu_custom_call" | custom-call | flops 40000000000 | bytes 16777216 | tf_op jit(solution)/shard_map/down_project/pallas_call | solution.py:528
  433.6 0.7 maximum_bitcast_fusion
  434.3 0.7 maximum_bitcast_fusion.1
  435.0 2.3 copy.27
  (18 shorter events, 0.1 us)
Async XLA Ops:
  7.2 7.6 %copy-start.4 = (bf16[2,256,2,128]{3,2,1,0:T(2,128)(2,1)S(1)}, bf16[2,256,2,128]{3,2,1,0:T(2,128)(2,1)}, u32[]{:S(2)}) copy-start(bf16[2,256,2,128]{3,2,1,0:T(2,128)(2,1)} %param.10) | copy-start | bytes 786436
  7.2 8.1 %copy-start.1 = (bf16[2,256,2,512]{3,2,1,0:T(2,128)(2,1)S(1)}, bf16[2,256,2,512]{3,2,1,0:T(2,128)(2,1)}, u32[]{:S(2)}) copy-start(bf16[2,256,2,512]{3,2,1,0:T(2,128)(2,1)} %param.11) | copy-start | bytes 3145732
  7.2 289.0 %all-gather.3.cloned.1.call-start = ((), (), s32[]{:S(2)}) async-start(), calls=%async_computation | async-start | bytes 11141120 | tf_op jit(solution)/shard_map/all_gather | solution.py:581
  9.3 33.8 %collective-permute-start.1 = (bf16[640,256]{1,0:T(8,128)(2,1)S(1)}, bf16[640,256]{1,0:T(8,128)(2,1)}, u32[]{:S(2)}, u32[]{:S(2)}) collective-permute-start(bf16[640,256]{1,0:T(8,128)(2,1)S(1)} %pad_maximum_fusion.3), channel_id=1, source_target_pairs={{0,0},{1,8},{2,16},{3,24},{4,32},{5,40},{6,48},{7,56},{8,64},{9,72... | collective-permute-start | bytes 983048 | tf_op jit(solution)/shard_map/ppermute | solution.py:576
  15.3 6.6 %copy-start = (bf16[1,256,2048]{2,1,0:T(8,128)(2,1)S(1)}, bf16[1,256,2048]{2,1,0:T(8,128)(2,1)}, u32[]{:S(2)}) copy-start(bf16[1,256,2048]{2,1,0:T(8,128)(2,1)} %param.7) | copy-start | bytes 3145732
  16.1 6.5 %copy-start.9 = (f32[2,2048]{1,0:T(2,128)S(1)}, f32[2,2048]{1,0:T(2,128)}, u32[]{:S(2)}) copy-start(f32[2,2048]{1,0:T(2,128)} %param.8) | copy-start | bytes 49156
  16.2 40.1 %collective-permute-start = (bf16[256,1280]{1,0:T(8,128)(2,1)S(1)}, bf16[256,1280]{1,0:T(8,128)(2,1)S(1)}, u32[]{:S(2)}, u32[]{:S(2)}) collective-permute-start(bf16[256,1280]{1,0:T(8,128)(2,1)S(1)} %pad_maximum_fusion.1), channel_id=1, source_target_pairs={{0,0},{1,8},{2,16},{3,24},{4,32},{5,40},{6,48},{7,56},{8,64},{9,72... | collective-permute-start | bytes 1966088 | tf_op jit(solution)/shard_map/ppermute | solution.py:576
  56.3 21.5 %copy-start.10 = (bf16[256,1280]{1,0:T(8,128)(2,1)}, bf16[256,1280]{1,0:T(8,128)(2,1)S(1)}, u32[]{:S(2)}) copy-start(bf16[256,1280]{1,0:T(8,128)(2,1)S(1)} %collective-permute-done.refs_1_) | copy-start | bytes 1966084
  56.3 144.5 %collective-permute-start.3 = (bf16[640,256]{1,0:T(8,128)(2,1)S(1)}, bf16[640,256]{1,0:T(8,128)(2,1)S(1)}, u32[]{:S(2)}, u32[]{:S(2)}) collective-permute-start(bf16[640,256]{1,0:T(8,128)(2,1)S(1)} %pad_maximum_fusion.2), channel_id=1, source_target_pairs={{0,0},{1,8},{2,16},{3,24},{4,32},{5,40},{6,48},{7,56},{8,64},{9,72... | collective-permute-start | bytes 983048 | tf_op jit(solution)/shard_map/ppermute | solution.py:576
  71.0 129.8 %collective-permute-start.2 = (bf16[256,1280]{1,0:T(8,128)(2,1)S(1)}, bf16[256,1280]{1,0:T(8,128)(2,1)S(1)}, u32[]{:S(2)}, u32[]{:S(2)}) collective-permute-start(bf16[256,1280]{1,0:T(8,128)(2,1)S(1)} %pad_maximum_fusion), channel_id=1, source_target_pairs={{0,0},{1,8},{2,16},{3,24},{4,32},{5,40},{6,48},{7,56},{8,64},{9,72... | collective-permute-start | bytes 1966088 | tf_op jit(solution)/shard_map/ppermute | solution.py:576
  200.8 1.2 copy-start.3
  200.8 0.9 copy-start.2
  201.7 150.2 %all-gather.5.cloned.1.call-start = ((), (), s32[]{:S(2)}) async-start(), calls=%async_computation.1 | async-start | bytes 5570560 | tf_op jit(solution)/shard_map/all_gather | solution.py:582
  351.9 81.7 %copy-start.6 = (bf16[256,128]{1,0:T(8,128)(2,1)S(1)}, bf16[256,128]{1,0:T(8,128)(2,1)}, u32[]{:S(2)}) copy-start(bf16[256,128]{1,0:T(8,128)(2,1)} %get-tuple-element.33) | copy-start | bytes 196612
  351.9 81.7 %copy-start.8 = (bf16[256,128]{1,0:T(8,128)(2,1)S(1)}, bf16[256,128]{1,0:T(8,128)(2,1)}, u32[]{:S(2)}) copy-start(bf16[256,128]{1,0:T(8,128)(2,1)} %get-tuple-element.34) | copy-start | bytes 196612
  351.9 82.4 %copy-start.5 = (bf16[256,128]{1,0:T(8,128)(2,1)S(1)}, bf16[256,128]{1,0:T(8,128)(2,1)}, u32[]{:S(2)}) copy-start(bf16[256,128]{1,0:T(8,128)(2,1)} %get-tuple-element.35) | copy-start | bytes 196612
  351.9 82.4 %copy-start.7 = (bf16[256,128]{1,0:T(8,128)(2,1)S(1)}, bf16[256,128]{1,0:T(8,128)(2,1)}, u32[]{:S(2)}) copy-start(bf16[256,128]{1,0:T(8,128)(2,1)} %get-tuple-element.36) | copy-start | bytes 196612
Sparse Core Ops, SparseCore 0:
  201.9 92.2 all-gather.2
  296.3 55.6 all-gather.4

commit v4 on v0

v4 whole, which is shorter than its diff:
```python
import functools

import jax
import jax.numpy as jnp
from jax import lax
from jax.experimental import pallas as pl
from jax.experimental.pallas import tpu as pltpu
from jax.sharding import PartitionSpec as P

LN_EPS = 1e-6
ROPE_BASE = 10000.0
MESH = pl.DeviceIdType.MESH
VMEM_LIMIT = 67043328
PLANE = 4
SUB = 128
N_COL = 4
N_RING = 12


def rope_tables(seq_len, head_dim):
    half_dim = head_dim // 2
    inv_freq = ROPE_BASE ** (-2.0 * jnp.arange(half_dim, dtype=jnp.float32) / head_dim)
    angles = jnp.arange(seq_len, dtype=jnp.float32)[:, None] * inv_freq[None, :]
    cos, sin = jnp.cos(angles), jnp.sin(angles)
    return jnp.concatenate([cos, cos], axis=1), jnp.concatenate([-sin, sin], axis=1)


def remote(src, dst, send, recv, target):
    return pltpu.make_async_remote_copy(src_ref=src, dst_ref=dst, send_sem=send, recv_sem=recv, device_id=target, device_id_type=MESH)


class Ring:
    def __init__(self, n_wx):
        self.me = lax.axis_index('wx')
        self.chip, self.core = lax.div(self.me, 2), lax.rem(self.me, 2)
        self.n_chip = n_wx // 2
        self.right, self.left, self.far = self.at(1), self.at(self.n_chip - 1), self.at(2)
        self.pair = self.at(0, 1)

    def at(self, step, other=0):
        return lax.rem(self.chip + step, self.n_chip) * 2 + lax.rem(self.core + other, 2)


class ChipGather:
    def __init__(self, ring, hall, send_sem, recv_sem):
        half = hall.shape[1] // 2
        top, bottom, whole = pl.ds(0, half), pl.ds(half, half), pl.ds(0, 2 * half)
        me, left, right, far, pair = ring.me, ring.left, ring.right, ring.far, ring.pair
        moves = [
            (me, whole, pair, pair),
            (me, top, right, left), (me, bottom, left, right),
            (me, bottom, right, left), (me, top, left, right),
            (left, top, right, far), (right, bottom, left, far),
            (left, whole, pair, ring.at(ring.n_chip - 1, 1)), (right, whole, pair, ring.at(1, 1)),
            (far, top, pair, ring.at(2, 1)), (far, bottom, pair, ring.at(2, 1)),
        ]
        self.sends, self.lands = [], []
        for num, (block, rows, target, landed) in enumerate(moves):
            for kept, there in ((self.sends, block), (self.lands, landed)):
                ref = hall.at[there, rows]
                kept.append(remote(ref, ref, send_sem.at[num], recv_sem.at[num], {'wx': target}))
        self.first = 5

    def start(self):
        for copy in self.sends[:self.first]:
            copy.start()

    def relay(self, landed, sent):
        self.lands[landed].wait_recv()
        self.sends[sent].start()

    def near_halves(self):
        self.relay(1, 5)
        self.relay(2, 6)

    def near_rest(self):
        self.relay(3, 7)
        self.relay(4, 8)

    def far_halves(self):
        self.relay(5, 9)
        self.relay(6, 10)

    def wait(self, *nums):
        for num in nums:
            self.lands[num].wait_recv()

    def drain(self):
        for copy in self.sends:
            copy.wait_send()


class PlaneGather:
    ways = [(half, sign) for half in range(2) for sign in (1, -1)]

    def __init__(self, buf, send_sem, recv_sem):
        self.buf, self.send_sem, self.recv_sem = buf, send_sem, recv_sem
        self.here = lax.axis_index('wy')
        self.pos = (lax.div(self.here, PLANE), lax.rem(self.here, PLANE))

    def at(self, half, first, second=0):
        step_z, step_y = (second, first) if half == 0 else (first, second)
        z, y = self.pos
        return lax.rem(z + step_z + PLANE, PLANE) * PLANE + lax.rem(y + step_y + PLANE, PLANE)

    def neighbours(self):
        return [{'wy': self.at(half, sign)} for half, sign in self.ways]

    def place(self, block, start, size):
        return self.buf.at[lax.div(block, 2), lax.rem(block, 2), pl.ds(start, size)]

    def copy(self, kind, num, block, half, quarter, target):
        rows = self.buf.shape[2]
        size = rows // 2 if quarter is None else rows // PLANE
        ref = self.place(block, half * (rows // 2) + (quarter or 0) * size, size)
        slot = kind * PLANE + num
        return remote(ref, ref, self.send_sem.at[slot], self.recv_sem.at[slot], {'wy': target})

    def one(self, half, sign, landing=False):
        block = self.at(half, -sign if landing else 0)
        return self.copy(0, half * 2 + (sign < 0), block, half, None, self.at(half, sign))

    def two(self, half, sign, landing=False):
        block = self.at(half, -2 * sign if landing else -sign)
        return self.copy(1, half * 2 + (sign < 0), block, half, int(sign < 0), self.at(half, sign))

    def three(self, half, off, sign, landing=False):
        block = self.at(half, off, -sign if landing else 0)
        return self.copy(2, (half * PLANE + off % PLANE) * 2 + (sign < 0), block, half, None, self.at(half, 0, sign))

    def four(self, half, off, sign, landing=False):
        block = self.at(half, off, -2 * sign if landing else -sign)
        return self.copy(6, (half * PLANE + off % PLANE) * 2 + (sign < 0), block, half, int(sign < 0), self.at(half, 0, sign))

    def start(self):
        for half, sign in self.ways:
            self.one(half, sign).start()
        for half, sign in self.ways:
            self.three(half, 0, sign).start()

    def stage_1(self):
        for half, sign in self.ways:
            self.one(half, sign, True).wait_recv()
            self.two(half, sign).start()
        for half, sign in self.ways:
            for way in (1, -1):
                self.three(half, -sign, way).start()

    def fourth(self, off):
        for half, sign in self.ways:
            self.three(half, off, sign, True).wait_recv()
            self.four(half, off, sign).start()

    def stage_2(self):
        self.fourth(0)

    def stage_3(self):
        for half, sign in self.ways:
            self.two(half, sign, True).wait_recv()
        for half, sign in self.ways:
            self.three(half, 2, sign).start()

    def stage_4(self):
        self.fourth(1)
        self.fourth(-1)

    def stage_5(self):
        self.fourth(2)

    def each(self, call):
        for half, sign in self.ways:
            for off in (0, 1, -1, 2):
                call(half, off, sign)

    def finish(self):
        self.each(lambda half, off, sign: self.four(half, off, sign, True).wait_recv())

    def drain(self):
        for half, sign in self.ways:
            self.one(half, sign).wait_send()
            self.two(half, sign).wait_send()
        self.each(lambda half, off, sign: self.three(half, off, sign).wait_send())
        self.each(lambda half, off, sign: self.four(half, off, sign).wait_send())


class Exchange:
    def __init__(self, ring, layer, shards, at_a, at_b, send_sem, recv_sem):
        pos = lax.axis_index('wy')
        odd = lax.rem(pos, 2)
        other = pos + 1 - 2 * odd
        same = odd == ring.core
        half = ring.n_chip * 2
        self.ring, self.pos = ring, pos
        self.send_to = (jnp.where(same, other, pos), jnp.where(same, ring.core, 1 - ring.core))
        self.recv_from = (jnp.where(same, pos, other), jnp.where(same, 1 - ring.core, ring.core))
        self.head_to = {'wy': odd * half + (1 - ring.core) * ring.n_chip + ring.chip, 'wx': lax.div(pos, 2)}
        self.head_from = {
            'wy': 2 * ring.me + lax.div(pos, half),
            'wx': lax.rem(pos, ring.n_chip) * 2 + 1 - lax.div(lax.rem(pos, half), ring.n_chip)}
        self.layer, self.shards = layer, shards
        self.at_a, self.at_b = at_a, at_b
        self.send_sem, self.recv_sem = send_sem, recv_sem

    def peers(self):
        wy, core = self.recv_from
        return [{'wy': wy, 'wx': self.chip(k) * 2 + core} for k in range(self.ring.n_chip)] + [self.head_from]

    def chip(self, step):
        return lax.rem(self.ring.chip + step, self.ring.n_chip)

    def block(self, which, step, landing):
        chip = self.chip(step)
        wy, core = self.send_to
        origin = chip if landing else self.ring.chip
        gu, d = self.shards[:2]
        rows = SUB if which else gu.shape[2]
        src = d.at[self.layer, pl.ds(pl.multiple_of(chip * SUB, SUB), SUB)] if which else gu.at[self.layer, chip]
        place = self.at_b if which else self.at_a
        dst = place(self.pos if landing else wy, pl.multiple_of(origin * rows, rows), rows)
        base = which * self.ring.n_chip
        return remote(src, dst, self.send_sem.at[base + chip], self.recv_sem.at[base + origin], {'wy': wy, 'wx': chip * 2 + core})

    def heads(self, which, landing):
        gu, d, q, kv, o = self.shards
        unit = self.pos if landing else self.head_to['wy']
        if which:
            parts = [(o, self.at_b(unit, self.ring.n_chip * SUB, o.shape[1]))]
        else:
            ref = self.at_a(unit, self.ring.n_chip * gu.shape[2], q.shape[1])
            parts = [(src, ref.at[:, pl.ds(num * SUB, SUB)]) for num, src in enumerate((q, kv))]
        base = self.ring.n_chip * 2 + which * 2
        return [remote(src.at[self.layer], dst, self.send_sem.at[base + num], self.recv_sem.at[base + num], self.head_to) for num, (src, dst) in enumerate(parts)]

    def copies(self, which, landing=False):
        return [self.block(which, step, landing) for step in (1, 3, 2, 0)] + self.heads(which, landing)

    def start(self, which):
        for copy in self.copies(which):
            copy.start()

    def land(self, which):
        for copy in self.copies(which, True):
            copy.wait_recv()

    def drain(self, which):
        for copy in self.copies(which):
            copy.wait_send()


def up_step(hall, wa, mo, kv_out, xt, cos, sin, between):
    seq, d_model = hall.shape[1], hall.shape[2]
    n_jj, tile, head_dim = wa.shape[0], wa.shape[3], cos.shape[1]
    half_d = d_model // 2
    first = pl.multiple_of(xt * 2 * seq, 2 * seq)
    h = hall[pl.ds(xt * 2, 2)].reshape(2 * seq, d_model)

    def project(weight):
        return jnp.dot(h, weight, preferred_element_type=jnp.float32).astype(jnp.bfloat16)

    narrow = [project(wa[hh * n_jj // 2:(hh + 1) * n_jj // 2, :, half_d:, :].reshape(d_model, tile)) for hh in range(2)]
    for jj in range(0, n_jj, 2):
        if jj == n_jj // 2:
            between()
        weight = jnp.concatenate([wa[jj + k, :, :half_d, :].reshape(d_model, tile) for k in range(2)], axis=1)
        both = project(weight)
        for k in range(2):
            g_f, u_f = (both[:, k * tile + part * SUB:k * tile + (part + 1) * SUB].astype(jnp.float32) for part in range(2))
            hidden = g_f * (1.0 / (1.0 + jnp.exp(-g_f))) * u_f
            mo[pl.ds(first, 2 * seq), (jj + k) * SUB:(jj + k + 1) * SUB] = hidden.astype(jnp.bfloat16)

    def rot(val):
        val_f = val.astype(jnp.float32)
        return (val_f * cos + pltpu.roll(val_f, head_dim // 2, 1) * sin).astype(jnp.bfloat16)

    allowed = lax.broadcasted_iota(jnp.int32, (seq, seq), 0) >= lax.broadcasted_iota(jnp.int32, (seq, seq), 1)
    for b in range(2):
        part = slice(b * seq, (b + 1) * seq)
        k_rot = rot(narrow[0][part, head_dim:])
        v_val = narrow[1][part, head_dim:]
        kv_out[b, 0] = k_rot
        kv_out[b, 1] = v_val
        for hh in range(2):
            q_rot = rot(narrow[hh][part, :head_dim])
            scores = lax.dot_general(q_rot, k_rot, (((1,), (1,)), ((), ())), preferred_element_type=jnp.float32) * head_dim ** -0.5
            scores = jnp.where(allowed, scores, -jnp.inf)
            expd = jnp.exp(scores - jnp.max(scores, axis=-1, keepdims=True))
            probs = (expd / jnp.sum(expd, axis=-1, keepdims=True)).astype(jnp.bfloat16)
            att = jnp.dot(probs, v_val, preferred_element_type=jnp.float32)
            lo = n_jj * SUB + hh * head_dim
            mo[pl.ds(first + b * seq, seq), lo:lo + head_dim] = att.astype(jnp.bfloat16)


class Scatter:
    def __init__(self, ring, first, mo, wb, given, taken, acc, landed, pair_send, pair_recv, ring_send, ring_recv):
        self.ring, self.first = ring, first
        self.mo, self.wb, self.given, self.taken, self.acc, self.landed = mo, wb, given, taken, acc, landed
        self.pair_send, self.pair_recv, self.ring_send, self.ring_recv = pair_send, pair_recv, ring_send, ring_recv

    def piece(self, n):
        if self.first:
            return n
        return jnp.where(n < N_COL, n + N_COL, jnp.where(n < 2 * N_COL, n - N_COL, n))

    def pair_copy(self, n):
        k, slot = self.piece(n), lax.rem(n, N_COL)
        return remote(self.given.at[slot], self.taken.at[k], self.pair_send.at[k], self.pair_recv.at[k], {'wx': self.ring.pair})

    def ring_copy(self, k):
        target = jnp.where(lax.rem(k, 2) == 0, self.ring.right, self.ring.left)
        return remote(self.acc.at[k], self.landed.at[k], self.ring_send.at[k], self.ring_recv.at[k], {'wx': target})

    def products(self, k):
        seq, col = self.acc.shape[1:]
        n_jj, _, rows, tile = self.wb.shape
        phase, j = lax.div(k, N_COL), lax.rem(k, N_COL)
        odd, slot = lax.rem(j, 2), lax.div(j, 2)
        own = phase == 3
        off = jnp.where(phase == 0, 2, jnp.where(own, 0, 1 + 2 * odd))
        q = jnp.where(own, j, jnp.where(phase == 1, 1 - odd, odd) * 2 + slot)
        xt = lax.rem(self.ring.chip + off, self.ring.n_chip)

        def columns(side):
            parts = [self.wb[:, side, pl.ds(pl.multiple_of(q * SUB, SUB), SUB), :].reshape(n_jj * SUB, tile)]
            for hh in range(2):
                unit = hh * n_jj + side * N_COL + q
                parts.append(self.wb[lax.div(unit, 2), lax.rem(unit, 2), N_COL * SUB:, :])
            return jnp.concatenate(parts, axis=0)

        weight = jnp.concatenate([columns(1), columns(0)], axis=1)

        def product(core):
            return jnp.dot(self.mo[pl.ds(pl.multiple_of((xt * 2 + core) * seq, seq), seq), :], weight, preferred_element_type=jnp.float32)

        return product

    def combine(self, n):
        k = self.piece(n)
        self.pair_copy(n).wait_recv()
        self.acc[k] = self.acc[k] + self.taken[k]

    def send(self, n):
        k = self.piece(n)

        @pl.when(k < 2 * N_COL)
        def _():
            self.ring_copy(k).start()

    def run(self, lo, hi):
        def body(n, carry):
            product = self.products(self.piece(n))

            @pl.when(n >= N_COL)
            def _():
                self.pair_copy(n - N_COL).wait_send()

            self.given[lax.rem(n, N_COL)] = product(1 - self.ring.core)

            @pl.when(n > lo)
            def _():
                self.combine(n - 1)

            self.acc[self.piece(n)] = product(self.ring.core)
            self.pair_copy(n).start()

            @pl.when(n > lo)
            def _():
                self.send(n - 1)

            return carry

        lax.fori_loop(lo, hi, body, 0)

        @pl.when(hi > lo)
        def _():
            self.combine(hi - 1)
            self.send(hi - 1)

    def finish(self, resid_ref, out_ref, beside):
        col = self.acc.shape[2]
        own = 3 * N_COL
        for pair in range(2):
            for odd in range(2):
                k = 2 * (N_COL + pair) + odd
                self.ring_copy(k - 2 * N_COL).wait_recv()
                self.acc[k] = self.acc[k] + self.landed[k - 2 * N_COL]
            for q in (pair, pair + 2):
                self.acc[own + q] = self.acc[own + q] + resid_ref[:, q * col:(q + 1) * col].astype(jnp.float32)
            for odd in range(2):
                self.ring_copy(2 * (N_COL + pair) + odd).start()
            beside[pair]()
        for pair in range(2):
            for q, raw, comb in ((pair, 5, 8), (pair + 2, 4, 9)):
                raw, comb = raw + 2 * pair, comb + 2 * pair
                self.ring_copy(raw).wait_recv()
                self.ring_copy(comb).wait_recv()
                out_ref[:, q * col:(q + 1) * col] = (self.acc[own + q] + (self.landed[raw] + self.landed[comb])).astype(jnp.bfloat16)
            beside[2 + pair]()
        for n in range(own, own + N_COL):
            self.pair_copy(n).wait_send()
        for k in range(N_RING):
            self.ring_copy(k).wait_send()


def layer_kernel(n_wx, first, *refs):
    if first:
        (resid_ref, gamma_ref, cos_ref, sin_ref, gu_ref, d_ref, q_ref, kv_ref, o_ref, out_ref, k_ref, v_ref, next_a, next_b,
         next_send, next_recv, x0_send, x0_recv, x1_send, x1_recv, a_send, a_recv, *rest) = refs
    else:
        resid_ref, gamma_ref, cos_ref, sin_ref, wa_ref, b_ref, out_ref, k_ref, v_ref, w_sem, *rest = refs
    hall, wa, wb, mo, kv, h_send, h_recv, b_send, b_recv, kv_sem, *parts = rest
    ring = Ring(n_wx)
    gather_h = ChipGather(ring, hall, h_send, h_recv)
    gather_b = PlaneGather(wb, b_send, b_recv)
    scatter = Scatter(ring, first, mo, wb, *parts)
    peers = [{'wx': ring.right}, {'wx': ring.left}, {'wx': ring.pair}] + gather_b.neighbours()
    if first:
        shards = gu_ref, d_ref, q_ref, kv_ref, o_ref
        gather_a = PlaneGather(wa, a_send, a_recv)
        gather_n = PlaneGather(next_a, next_send, next_recv)
        swap_0 = Exchange(ring, 0, shards, gather_a.place, gather_b.place, x0_send, x0_recv)
        swap_1 = Exchange(ring, 1, shards, gather_n.place, lambda unit, start, size: next_b.at[pl.ds(start, size)], x1_send, x1_recv)
        peers += swap_0.peers()
    else:
        here = gather_b.here
        b_load = pltpu.make_async_copy(b_ref, wb.at[lax.div(here, 2), lax.rem(here, 2)], w_sem.at[0])
        a_load = pltpu.make_async_copy(wa_ref, wa, w_sem.at[1])
        b_load.start()
        a_load.start()
    barrier = pltpu.get_barrier_semaphore()
    for peer in peers:
        pl.semaphore_signal(barrier, inc=1, device_id=peer, device_id_type=MESH)

    resid_f = resid_ref[...].astype(jnp.float32)
    centered = resid_f - jnp.mean(resid_f, axis=-1, keepdims=True)
    variance = jnp.mean(centered * centered, axis=-1, keepdims=True)
    normed = (centered * lax.rsqrt(variance + LN_EPS) * gamma_ref[...]).astype(jnp.bfloat16)
    tile = normed.shape[1] // n_wx
    for w in range(n_wx):
        lo = ((1 - w % 2) * ring.n_chip + w // 2) * tile
        hall[ring.me, :, lo:lo + tile] = normed[:, w * tile:(w + 1) * tile]

    pl.semaphore_wait(barrier, len(peers))
    if first:
        swap_0.start(0)
        gather_h.start()
        swap_0.land(0)
        gather_a.start()
        swap_0.start(1)
        gather_a.stage_1()
        gather_h.near_halves()
        gather_a.stage_2()
        gather_a.stage_3()
        gather_h.near_rest()
        swap_1.start(0)
        swap_1.start(1)
        gather_a.stage_4()
        gather_h.far_halves()
        gather_a.stage_5()
        swap_0.land(1)
        gather_b.start()
        gather_h.wait(0, 7, 8, 9, 10)
        gather_a.finish()
    else:
        b_load.wait()
        gather_h.start()
        gather_b.start()
        a_load.wait()

    def body(step, carry):
        turn = lax.rem(step + 1, PLANE) if first else step
        off = jnp.where(turn == 0, 0, jnp.where(turn == 1, 3, jnp.where(turn == 2, 1, 2)))

        def when(num, *calls):
            @pl.when(step == num)
            def _():
                for call in calls:
                    call()

        if first:
            when(1, gather_b.stage_1)
            when(2, gather_b.stage_3)
            when(3, gather_n.stage_1)
        else:
            when(0, lambda: gather_h.wait(0))
            when(1, gather_b.stage_1, gather_h.near_halves, gather_b.stage_2, gather_b.stage_3, gather_h.near_rest, lambda: gather_h.wait(7))
            when(2, gather_b.stage_4, gather_b.stage_5, lambda: gather_h.wait(8))
            when(3, gather_h.far_halves, lambda: gather_h.wait(9, 10))

        def between():
            if first:
                when(1, gather_b.stage_2)
                when(2, gather_b.stage_4)

        mine = jnp.where(turn == 0, 0, 1)
        up_step(hall, wa, mo, kv.at[mine], lax.rem(ring.chip + off, ring.n_chip), cos_ref[...], sin_ref[...], between)
        if first:
            when(2, gather_b.stage_5, gather_b.finish, lambda: swap_1.land(0), gather_n.start)
        else:
            when(2, gather_b.finish)
        split = 2 * N_COL if first else N_COL
        last = step == 3
        scatter.run(jnp.where(last, split, 0), jnp.where(last, 4 * N_COL, jnp.where(step == 2, split, 0)))
        return carry

    lax.fori_loop(0, ring.n_chip, body, 0)
    caches = [pltpu.make_async_copy(kv.at[0, ring.core, num], ref, kv_sem.at[num]) for num, ref in enumerate((k_ref, v_ref))]
    for cache in caches:
        cache.start()
    if first:
        scatter.finish(resid_ref, out_ref, (gather_n.stage_2, gather_n.stage_3, gather_n.stage_4, gather_n.stage_5))
        gather_n.finish()
        swap_1.land(1)
        for swap in (swap_0, swap_1):
            swap.drain(0)
            swap.drain(1)
        gather_a.drain()
        gather_n.drain()
    else:
        scatter.finish(resid_ref, out_ref, [lambda: None] * 4)
    gather_b.drain()
    gather_h.drain()
    for cache in caches:
        cache.wait()


def layer(resid, gamma, cos, sin, weights, n_wx, first):
    seq, d_model = resid.shape
    head_dim = cos.shape[1]
    n_unit = PLANE * PLANE
    col = d_model // N_COL
    any_spec, vmem_spec = pl.BlockSpec(memory_space=pl.ANY), pl.BlockSpec(memory_space=pltpu.VMEM)
    tile = d_model // n_wx
    unit_b = (PLANE * SUB + head_dim, tile)
    wa_shape = (n_unit // 2, 2, (PLANE + 1) * tile, tile)
    wb_shape = (n_unit // 2, 2) + unit_b
    piece = (seq, col)
    n_piece = 4 * N_COL
    dma = pltpu.SemaphoreType.DMA
    out_shape = [jax.ShapeDtypeStruct(shape, jnp.bfloat16) for shape in (resid.shape, (seq, head_dim), (seq, head_dim))]
    n_plane, n_swap, n_hop = dma((40,)), dma((11,)), dma((11,))
    if first:
        out_shape += [jax.ShapeDtypeStruct(shape, jnp.bfloat16) for shape in (wa_shape, unit_b)]
        scratch = [n_plane, n_plane, n_swap, n_swap, n_swap, n_swap, n_plane, n_plane]
    else:
        scratch = [dma((2,))]
    scratch += [
        pltpu.VMEM((n_wx, seq, d_model), jnp.bfloat16),
        pltpu.VMEM(wa_shape, jnp.bfloat16),
        pltpu.VMEM(wb_shape, jnp.bfloat16),
        pltpu.VMEM((n_wx * seq, n_unit // 2 * SUB + 2 * head_dim), jnp.bfloat16),
        pltpu.VMEM((2, 2, 2, seq, head_dim), jnp.bfloat16),
        n_hop, n_hop, n_plane, n_plane, dma((2,)),
        pltpu.VMEM((N_COL,) + piece, jnp.float32),
        pltpu.VMEM((n_piece,) + piece, jnp.float32),
        pltpu.VMEM((n_piece,) + piece, jnp.float32),
        pltpu.VMEM((N_RING,) + piece, jnp.float32),
        dma((n_piece,)), dma((n_piece,)), dma((N_RING,)), dma((N_RING,)),
    ]
    return pl.pallas_call(
        functools.partial(layer_kernel, n_wx, first),
        out_shape=tuple(out_shape),
        in_specs=[vmem_spec] * 4 + [any_spec] * len(weights),
        out_specs=[vmem_spec] + [any_spec] * (len(out_shape) - 1),
        scratch_shapes=scratch,
        compiler_params=pltpu.CompilerParams(collective_id=int(first), has_side_effects=True, vmem_limit_bytes=VMEM_LIMIT),
        name='layer_0' if first else 'layer_1',
    )(resid, gamma, cos, sin, *weights)


def solution(mesh):
    batch_axes = ('dp', 'wy', 'wx')
    in_specs = (P(batch_axes), P(), P(None, 'wx', 'wy'), P(None, 'wx'), P(None, 'wx', None, 'wy'), P(None, 'wy', 'wx'), P(None, 'wy', 'wx'))
    out_specs = (P(batch_axes), P(None, batch_axes), P(None, batch_axes))
    n_wx = mesh.shape['wx']

    def device_step(x_tokens, gamma_ln, w_q, w_kv, w_gu, w_o, w_d):
        n_layers, d_loc = w_q.shape[:2]
        cos_tab, sin_tab = rope_tables(x_tokens.shape[1], w_kv.shape[-1])
        kv_half = lax.dynamic_index_in_dim(w_kv, lax.rem(lax.axis_index('wy'), 2), axis=2, keepdims=False)
        gu = jnp.transpose(w_gu.reshape(n_layers, d_loc, 2, n_wx // 2, SUB), (0, 3, 1, 2, 4)).reshape(n_layers, n_wx // 2, d_loc, 2 * SUB)
        resid, k_0, v_0, wa, unit_b = layer(x_tokens[0], gamma_ln[:1], cos_tab, sin_tab, (gu, w_d, w_q, kv_half, w_o), n_wx, True)
        resid, k_1, v_1 = layer(resid, gamma_ln[1:], cos_tab, sin_tab, (wa, unit_b), n_wx, False)
        return resid[None], jnp.stack([k_0, k_1])[:, None], jnp.stack([v_0, v_1])[:, None]

    return jax.shard_map(device_step, mesh=mesh, in_specs=in_specs, out_specs=out_specs, check_vma=False)
```

time: 1680 us -> 346 us (0.21)
  waiting for transfers between devices: 1500 us -> 0 us
  Pallas kernels: 0 us -> 331 us
  matrix products: 135 us -> 0 us
    all_gather x18 -> x0, waiting for transfers between devices: 1500 us -> none  [the longest x2 586 us: device_step(): lax.all_gather(lax.all_gather(w_gu[layer_idx], 'wy', axis=2, tiled=True),...]
    pallas_call x0 -> x2, Pallas kernels: none -> 331 us  [layer(): pl.pallas_call(functools.partial(layer_kernel, n_wx, first), out_shape=tu...]
    dot_general x12 -> x0, matrix products: 132 us -> none  [the longest x2 61.3 us: decoder_layer(): jnp.einsum('bsd,dcf->bscf', normed, w_gu, preferred_element_type=jnp.floa...]
  transfers between devices with their start and end apart: 18 -> 0, of which waited for: 18 -> 0; matrix products, arithmetic and copies ran while one was open for 8% -> 0% of each run, Pallas kernels for 0% -> 0%
where the time goes in v4:
time: 346 us; the launch traced here: 345 us
  Pallas kernels  331 us (96%)
  local copies, waits for them, and re-layouts  9.04 us (3%)
  other arithmetic  4.43 us (1%)
    pallas_call x2, Pallas kernels, layer(): pl.pallas_call(functools.partial(layer_kernel, n_wx, first), out_shape=tu...  331 us

profile of v4, /device:TPU:1, one launch (start us, length us, event | category | flops | bytes accessed | tf_op | source)
XLA Modules:
  0.0 345.1 jit_solution(3930142724303236467)
XLA Ops:
  0.7 1.4 fusion.3
  2.1 1.2 constant_dynamic-slice_fusion
  3.3 0.7 copy.21
  4.0 0.5 fusion.2
  4.5 0.8 pad_maximum_fusion
  5.3 1.9 bitcast_bitcast_fusion
  7.3 1.5 reshape.18.refs_4_
  8.7 209.4 %layer_0.1 = (bf16[256,2048]{1,0:T(8,128)(2,1)}, bf16[256,128]{1,0:T(8,128)(2,1)}, bf16[256,128]{1,0:T(8,128)(2,1)}, bf16[8,2,1280,256]{3,2,1,0:T(8,128)(2,1)}, bf16[640,256]{1,0:T(8,128)(2,1)}) custom-call(bf16[256,2048]{1,0:T(8,128)(2,1)} %bitcast.24, f32[1,2048]{1,0:T(1,128)} %get-tuple-element.26.refs_1_, f32[256,128]{1,0:T(8,128)} %get-tuple-element.30.refs_2_, ...), custom_call_target="tpu_custom_call" | custom-call | tf_op jit(solution)/shard_map/layer_0/pallas_call | solution.py:559
  218.1 121.6 %layer_1.1 = (bf16[256,2048]{1,0:T(8,128)(2,1)}, bf16[256,128]{1,0:T(8,128)(2,1)}, bf16[256,128]{1,0:T(8,128)(2,1)}) custom-call(bf16[256,2048]{1,0:T(8,128)(2,1)} %get-tuple-element.11.refs_0_, f32[1,2048]{1,0:T(1,128)} %get-tuple-element.25.refs_1_, f32[256,128]{1,0:T(8,128)} %get-tuple-element.30.refs_2_, f32[256,128]{1,0:T(8,128)} %get-tuple-element.31.refs_3_, ...), custom_call_target="tpu_custom_call" | custom-call | tf_op jit(solution)/shard_map/layer_1/pallas_call | solution.py:559
  339.7 1.5 maximum_bitcast_fusion
  341.3 1.5 maximum_bitcast_fusion.1
  342.8 2.3 copy.23
  (1 shorter events, 0.0 us)

commit v5 on v4

--- a/solution.py
+++ b/solution.py
@@ -51,7 +51,8 @@
             (me, top, right, left), (me, bottom, left, right),
             (me, bottom, right, left), (me, top, left, right),
             (left, top, right, far), (right, bottom, left, far),
-            (left, whole, pair, ring.at(ring.n_chip - 1, 1)), (right, whole, pair, ring.at(1, 1)),
+            (left, top, pair, ring.at(ring.n_chip - 1, 1)), (right, bottom, pair, ring.at(1, 1)),
+            (left, bottom, pair, ring.at(ring.n_chip - 1, 1)), (right, top, pair, ring.at(1, 1)),
             (far, top, pair, ring.at(2, 1)), (far, bottom, pair, ring.at(2, 1)),
         ]
         self.sends, self.lands = [], []
@@ -65,21 +66,22 @@
         for copy in self.sends[:self.first]:
             copy.start()
 
-    def relay(self, landed, sent):
+    def relay(self, landed, *sent):
         self.lands[landed].wait_recv()
-        self.sends[sent].start()
+        for num in sent:
+            self.sends[num].start()
 
     def near_halves(self):
-        self.relay(1, 5)
-        self.relay(2, 6)
+        self.relay(1, 5, 7)
+        self.relay(2, 6, 8)
 
     def near_rest(self):
-        self.relay(3, 7)
-        self.relay(4, 8)
+        self.relay(3, 9)
+        self.relay(4, 10)
 
     def far_halves(self):
-        self.relay(5, 9)
-        self.relay(6, 10)
+        self.relay(5, 11)
+        self.relay(6, 12)
 
     def wait(self, *nums):
         for num in nums:
@@ -247,17 +249,23 @@
             copy.wait_send()
 
 
-def up_step(hall, wa, mo, kv_out, xt, cos, sin, between):
-    seq, d_model = hall.shape[1], hall.shape[2]
-    n_jj, tile, head_dim = wa.shape[0], wa.shape[3], cos.shape[1]
+def up_step(hall, wa, mo, narrow, chunks, between):
+    d_model = hall.shape[2]
+    half = hall.shape[1] // 2
+    n_jj, tile = wa.shape[0], wa.shape[3]
     half_d = d_model // 2
-    first = pl.multiple_of(xt * 2 * seq, 2 * seq)
-    h = hall[pl.ds(xt * 2, 2)].reshape(2 * seq, d_model)
+    rows = [(prompt, pl.ds(pl.multiple_of(start, half), half)) for prompt, start in chunks]
+    h = jnp.concatenate([hall[prompt, part] for prompt, part in rows], axis=0)
 
     def project(weight):
         return jnp.dot(h, weight, preferred_element_type=jnp.float32).astype(jnp.bfloat16)
 
-    narrow = [project(wa[hh * n_jj // 2:(hh + 1) * n_jj // 2, :, half_d:, :].reshape(d_model, tile)) for hh in range(2)]
+    def keep(value, ref, lo):
+        for num, (prompt, part) in enumerate(rows):
+            ref[prompt, part, lo:lo + value.shape[1]] = value[num * half:(num + 1) * half]
+
+    for hh in range(2):
+        keep(project(wa[hh * n_jj // 2:(hh + 1) * n_jj // 2, :, half_d:, :].reshape(d_model, tile)), narrow, hh * tile)
     for jj in range(0, n_jj, 2):
         if jj == n_jj // 2:
             between()
@@ -266,7 +274,12 @@
         for k in range(2):
             g_f, u_f = (both[:, k * tile + part * SUB:k * tile + (part + 1) * SUB].astype(jnp.float32) for part in range(2))
             hidden = g_f * (1.0 / (1.0 + jnp.exp(-g_f))) * u_f
-            mo[pl.ds(first, 2 * seq), (jj + k) * SUB:(jj + k + 1) * SUB] = hidden.astype(jnp.bfloat16)
+            keep(hidden.astype(jnp.bfloat16), mo, (jj + k) * SUB)
+
+
+def attend(narrow, mo, kv_out, xt, cos, sin):
+    seq, head_dim = cos.shape
+    tile = 2 * head_dim
 
     def rot(val):
         val_f = val.astype(jnp.float32)
@@ -274,20 +287,20 @@
 
     allowed = lax.broadcasted_iota(jnp.int32, (seq, seq), 0) >= lax.broadcasted_iota(jnp.int32, (seq, seq), 1)
     for b in range(2):
-        part = slice(b * seq, (b + 1) * seq)
-        k_rot = rot(narrow[0][part, head_dim:])
-        v_val = narrow[1][part, head_dim:]
+        prompt = xt * 2 + b
+        k_rot = rot(narrow[prompt, :, head_dim:tile])
+        v_val = narrow[prompt, :, tile + head_dim:]
         kv_out[b, 0] = k_rot
         kv_out[b, 1] = v_val
         for hh in range(2):
-            q_rot = rot(narrow[hh][part, :head_dim])
+            q_rot = rot(narrow[prompt, :, hh * tile:hh * tile + head_dim])
             scores = lax.dot_general(q_rot, k_rot, (((1,), (1,)), ((), ())), preferred_element_type=jnp.float32) * head_dim ** -0.5
             scores = jnp.where(allowed, scores, -jnp.inf)
             expd = jnp.exp(scores - jnp.max(scores, axis=-1, keepdims=True))
             probs = (expd / jnp.sum(expd, axis=-1, keepdims=True)).astype(jnp.bfloat16)
             att = jnp.dot(probs, v_val, preferred_element_type=jnp.float32)
-            lo = n_jj * SUB + hh * head_dim
-            mo[pl.ds(first + b * seq, seq), lo:lo + head_dim] = att.astype(jnp.bfloat16)
+            lo = mo.shape[2] - (2 - hh) * head_dim
+            mo[prompt, :, lo:lo + head_dim] = att.astype(jnp.bfloat16)
 
 
 class Scatter:
@@ -310,8 +323,7 @@
         return remote(self.acc.at[k], self.landed.at[k], self.ring_send.at[k], self.ring_recv.at[k], {'wx': target})
 
     def products(self, k):
-        seq, col = self.acc.shape[1:]
-        n_jj, _, rows, tile = self.wb.shape
+        n_jj, tile = self.wb.shape[0], self.wb.shape[3]
         phase, j = lax.div(k, N_COL), lax.rem(k, N_COL)
         odd, slot = lax.rem(j, 2), lax.div(j, 2)
         own = phase == 3
@@ -329,7 +341,7 @@
         weight = jnp.concatenate([columns(1), columns(0)], axis=1)
 
         def product(core):
-            return jnp.dot(self.mo[pl.ds(pl.multiple_of((xt * 2 + core) * seq, seq), seq), :], weight, preferred_element_type=jnp.float32)
+            return jnp.dot(self.mo[xt * 2 + core], weight, preferred_element_type=jnp.float32)
 
         return product
 
@@ -389,12 +401,14 @@
                 self.ring_copy(2 * (N_COL + pair) + odd).start()
             beside[pair]()
         for pair in range(2):
+            for k in (N_COL + 2 * pair, N_COL + 2 * pair + 1):
+                self.ring_copy(k).wait_recv()
+            beside[2 + pair]()
+        for pair in range(2):
             for q, raw, comb in ((pair, 5, 8), (pair + 2, 4, 9)):
                 raw, comb = raw + 2 * pair, comb + 2 * pair
-                self.ring_copy(raw).wait_recv()
                 self.ring_copy(comb).wait_recv()
                 out_ref[:, q * col:(q + 1) * col] = (self.acc[own + q] + (self.landed[raw] + self.landed[comb])).astype(jnp.bfloat16)
-            beside[2 + pair]()
         for n in range(own, own + N_COL):
             self.pair_copy(n).wait_send()
         for k in range(N_RING):
@@ -403,11 +417,11 @@
 
 def layer_kernel(n_wx, first, *refs):
     if first:
-        (resid_ref, gamma_ref, cos_ref, sin_ref, gu_ref, d_ref, q_ref, kv_ref, o_ref, out_ref, k_ref, v_ref, next_a, next_b,
+        (resid_ref, gamma_ref, cos_ref, sin_ref, gu_ref, d_ref, q_ref, kv_ref, o_ref, out_ref, k_out, v_out, next_a, next_b,
          next_send, next_recv, x0_send, x0_recv, x1_send, x1_recv, a_send, a_recv, *rest) = refs
     else:
-        resid_ref, gamma_ref, cos_ref, sin_ref, wa_ref, b_ref, out_ref, k_ref, v_ref, w_sem, *rest = refs
-    hall, wa, wb, mo, kv, h_send, h_recv, b_send, b_recv, kv_sem, *parts = rest
+        resid_ref, gamma_ref, cos_ref, sin_ref, wa_ref, b_ref, k_ref, v_ref, out_ref, k_out, v_out, w_sem, old_sem, *rest = refs
+    hall, wa, wb, mo, narrow, kv, h_send, h_recv, b_send, b_recv, kv_sem, *parts = rest
     ring = Ring(n_wx)
     gather_h = ChipGather(ring, hall, h_send, h_recv)
     gather_b = PlaneGather(wb, b_send, b_recv)
@@ -424,8 +438,9 @@
         here = gather_b.here
         b_load = pltpu.make_async_copy(b_ref, wb.at[lax.div(here, 2), lax.rem(here, 2)], w_sem.at[0])
         a_load = pltpu.make_async_copy(wa_ref, wa, w_sem.at[1])
-        b_load.start()
-        a_load.start()
+        old_loads = [pltpu.make_async_copy(ref, kv.at[2, 0, num], old_sem.at[num]) for num, ref in enumerate((k_ref, v_ref))]
+        for load in (b_load, a_load, *old_loads):
+            load.start()
     barrier = pltpu.get_barrier_semaphore()
     for peer in peers:
         pl.semaphore_signal(barrier, inc=1, device_id=peer, device_id_type=MESH)
@@ -433,7 +448,7 @@
     resid_f = resid_ref[...].astype(jnp.float32)
     centered = resid_f - jnp.mean(resid_f, axis=-1, keepdims=True)
     variance = jnp.mean(centered * centered, axis=-1, keepdims=True)
-    normed = (centered * lax.rsqrt(variance + LN_EPS) * gamma_ref[...]).astype(jnp.bfloat16)
+    normed = (centered * lax.rsqrt(variance + LN_EPS) * gamma_ref[1 - first:2 - first, :]).astype(jnp.bfloat16)
     tile = normed.shape[1] // n_wx
     for w in range(n_wx):
         lo = ((1 - w % 2) * ring.n_chip + w // 2) * tile
@@ -458,17 +473,19 @@
         gather_a.stage_5()
         swap_0.land(1)
         gather_b.start()
-        gather_h.wait(0, 7, 8, 9, 10)
+        gather_h.wait(0, 7, 8, 9, 10, 11, 12)
         gather_a.finish()
     else:
+        gather_h.start()
         b_load.wait()
-        gather_h.start()
         gather_b.start()
         a_load.wait()
 
+    seq = hall.shape[1]
+    half = seq // 2
+
     def body(step, carry):
         turn = lax.rem(step + 1, PLANE) if first else step
-        off = jnp.where(turn == 0, 0, jnp.where(turn == 1, 3, jnp.where(turn == 2, 1, 2)))
 
         def when(num, *calls):
             @pl.when(step == num)
@@ -479,20 +496,41 @@
         if first:
             when(1, gather_b.stage_1)
             when(2, gather_b.stage_3)
-            when(3, gather_n.stage_1)
         else:
             when(0, lambda: gather_h.wait(0))
-            when(1, gather_b.stage_1, gather_h.near_halves, gather_b.stage_2, gather_b.stage_3, gather_h.near_rest, lambda: gather_h.wait(7))
-            when(2, gather_b.stage_4, gather_b.stage_5, lambda: gather_h.wait(8))
-            when(3, gather_h.far_halves, lambda: gather_h.wait(9, 10))
+            when(1, gather_b.stage_1, gather_h.near_halves, gather_b.stage_2, lambda: gather_h.wait(7, 8))
+            when(2, gather_b.stage_3, gather_h.near_rest, gather_b.stage_4, lambda: gather_h.wait(9, 10))
+            when(3, gather_h.far_halves, lambda: gather_h.wait(11, 12))
 
         def between():
             if first:
                 when(1, gather_b.stage_2)
                 when(2, gather_b.stage_4)
-
-        mine = jnp.where(turn == 0, 0, 1)
-        up_step(hall, wa, mo, kv.at[mine], lax.rem(ring.chip + off, ring.n_chip), cos_ref[...], sin_ref[...], between)
+                when(3, gather_n.stage_1)
+            else:
+                when(2, gather_b.stage_5)
+
+        near = (turn == 1) | (turn == 2)
+        lone = jnp.where(turn == 0, ring.chip, lax.rem(ring.chip + 2, ring.n_chip))
+        one = jnp.where(near, lax.div(ring.left, 2), lone)
+        two = jnp.where(near, lax.div(ring.right, 2), lone)
+        start = jnp.where(turn == 2, half, 0)
+        up_step(hall, wa, mo, narrow, [(one * 2 + b, start) for b in range(2)] + [(two * 2 + b, half - start) for b in range(2)], between)
+
+        def attention(num, carry):
+            place = lax.rem(num + 1, PLANE) if first else num
+            off = jnp.where(place == 0, 0, jnp.where(place == 1, 3, jnp.where(place == 2, 1, 2)))
+            attend(narrow, mo, kv.at[jnp.where(place == 0, 0, 1)], lax.rem(ring.chip + off, ring.n_chip), cos_ref[...], sin_ref[...])
+            return carry
+
+        early = 0 if first else 1
+        lo = jnp.where(step == 3, 3, jnp.where(step == 2, 2 - early, 0))
+        if first:
+            hi = jnp.where(step == 0, 0, step + 1)
+            lo = jnp.where(step == 2, 2, lo)
+        else:
+            lo, hi = jnp.where(step == 1, 1, lo), jnp.where(step < 2, 1, step + 1)
+        lax.fori_loop(lo, hi, attention, 0)
         if first:
             when(2, gather_b.stage_5, gather_b.finish, lambda: swap_1.land(0), gather_n.start)
         else:
@@ -503,7 +541,14 @@
         return carry
 
     lax.fori_loop(0, ring.n_chip, body, 0)
-    caches = [pltpu.make_async_copy(kv.at[0, ring.core, num], ref, kv_sem.at[num]) for num, ref in enumerate((k_ref, v_ref))]
+    if first:
+        caches = [(kv.at[0, ring.core, num], ref) for num, ref in enumerate((k_out, v_out))]
+    else:
+        for load in old_loads:
+            load.wait()
+        caches = [(kv.at[0, ring.core, num], ref.at[1]) for num, ref in enumerate((k_out, v_out))]
+        caches += [(kv.at[2, 0, num], ref.at[0]) for num, ref in enumerate((k_out, v_out))]
+    caches = [pltpu.make_async_copy(src, dst, kv_sem.at[num]) for num, (src, dst) in enumerate(caches)]
     for cache in caches:
         cache.start()
     if first:
@@ -536,20 +581,22 @@
     piece = (seq, col)
     n_piece = 4 * N_COL
     dma = pltpu.SemaphoreType.DMA
-    out_shape = [jax.ShapeDtypeStruct(shape, jnp.bfloat16) for shape in (resid.shape, (seq, head_dim), (seq, head_dim))]
-    n_plane, n_swap, n_hop = dma((40,)), dma((11,)), dma((11,))
+    cache = (seq, head_dim) if first else (2, seq, head_dim)
+    out_shape = [jax.ShapeDtypeStruct(shape, jnp.bfloat16) for shape in (resid.shape, cache, cache)]
+    n_plane, n_swap, n_hop = dma((40,)), dma((11,)), dma((13,))
     if first:
         out_shape += [jax.ShapeDtypeStruct(shape, jnp.bfloat16) for shape in (wa_shape, unit_b)]
         scratch = [n_plane, n_plane, n_swap, n_swap, n_swap, n_swap, n_plane, n_plane]
     else:
-        scratch = [dma((2,))]
+        scratch = [dma((2,)), dma((2,))]
     scratch += [
         pltpu.VMEM((n_wx, seq, d_model), jnp.bfloat16),
         pltpu.VMEM(wa_shape, jnp.bfloat16),
         pltpu.VMEM(wb_shape, jnp.bfloat16),
-        pltpu.VMEM((n_wx * seq, n_unit // 2 * SUB + 2 * head_dim), jnp.bfloat16),
-        pltpu.VMEM((2, 2, 2, seq, head_dim), jnp.bfloat16),
-        n_hop, n_hop, n_plane, n_plane, dma((2,)),
+        pltpu.VMEM((n_wx, seq, n_unit // 2 * SUB + 2 * head_dim), jnp.bfloat16),
+        pltpu.VMEM((n_wx, seq, 4 * head_dim), jnp.bfloat16),
+        pltpu.VMEM((3, 2, 2, seq, head_dim), jnp.bfloat16),
+        n_hop, n_hop, n_plane, n_plane, dma((4,)),
         pltpu.VMEM((N_COL,) + piece, jnp.float32),
         pltpu.VMEM((n_piece,) + piece, jnp.float32),
         pltpu.VMEM((n_piece,) + piece, jnp.float32),
@@ -578,8 +625,8 @@
         cos_tab, sin_tab = rope_tables(x_tokens.shape[1], w_kv.shape[-1])
         kv_half = lax.dynamic_index_in_dim(w_kv, lax.rem(lax.axis_index('wy'), 2), axis=2, keepdims=False)
         gu = jnp.transpose(w_gu.reshape(n_layers, d_loc, 2, n_wx // 2, SUB), (0, 3, 1, 2, 4)).reshape(n_layers, n_wx // 2, d_loc, 2 * SUB)
-        resid, k_0, v_0, wa, unit_b = layer(x_tokens[0], gamma_ln[:1], cos_tab, sin_tab, (gu, w_d, w_q, kv_half, w_o), n_wx, True)
-        resid, k_1, v_1 = layer(resid, gamma_ln[1:], cos_tab, sin_tab, (wa, unit_b), n_wx, False)
-        return resid[None], jnp.stack([k_0, k_1])[:, None], jnp.stack([v_0, v_1])[:, None]
+        resid, k_0, v_0, wa, unit_b = layer(x_tokens[0], gamma_ln, cos_tab, sin_tab, (gu, w_d, w_q, kv_half, w_o), n_wx, True)
+        resid, k_all, v_all = layer(resid, gamma_ln, cos_tab, sin_tab, (wa, unit_b, k_0, v_0), n_wx, False)
+        return resid[None], k_all[:, None], v_all[:, None]
 
     return jax.shard_map(device_step, mesh=mesh, in_specs=in_specs, out_specs=out_specs, check_vma=False)

time: 346 us -> 334 us (0.965)
  Pallas kernels: 331 us -> 321 us
    pallas_call x2, Pallas kernels: 331 us -> 321 us  [layer(): pl.pallas_call(functools.partial(layer_kernel, n_wx, first), out_shape=tu...]
where the time goes in v5:
time: 334 us
  Pallas kernels  321 us (96%)
  local copies, waits for them, and re-layouts  10.8 us (3%)
    pallas_call x2, Pallas kernels, layer(): pl.pallas_call(functools.partial(layer_kernel, n_wx, first), out_shape=tu...  321 us

profile of v5, /device:TPU:1, one launch (start us, length us, event | category | flops | bytes accessed | tf_op | source)
XLA Modules:
  0.0 333.8 jit_solution(8928461443017708370)
XLA Ops:
  0.7 1.2 constant_dynamic-slice_fusion
  1.9 0.7 copy.21
  2.5 0.5 fusion.2
  3.1 0.8 pad_maximum_fusion
  3.9 1.9 bitcast_bitcast_fusion
  5.8 1.5 reshape.18.refs_4_
  7.3 203.5 %layer_0.1 = (bf16[256,2048]{1,0:T(8,128)(2,1)}, bf16[256,128]{1,0:T(8,128)(2,1)}, bf16[256,128]{1,0:T(8,128)(2,1)}, bf16[8,2,1280,256]{3,2,1,0:T(8,128)(2,1)}, bf16[640,256]{1,0:T(8,128)(2,1)}) custom-call(bf16[256,2048]{1,0:T(8,128)(2,1)} %bitcast.18, f32[2,2048]{1,0:T(2,128)} %refs_1_.3, f32[256,128]{1,0:T(8,128)} %get-tuple-element.28.refs_2_, ...), custom_call_target="tpu_custom_call" | custom-call | tf_op jit(solution)/shard_map/layer_0/pallas_call | solution.py:606
  210.8 117.6 %layer_1.1 = (bf16[256,2048]{1,0:T(8,128)(2,1)}, bf16[2,256,128]{2,1,0:T(8,128)(2,1)}, bf16[2,256,128]{2,1,0:T(8,128)(2,1)}) custom-call(bf16[256,2048]{1,0:T(8,128)(2,1)} %get-tuple-element.11.refs_0_, f32[2,2048]{1,0:T(2,128)} %refs_1_.3, f32[256,128]{1,0:T(8,128)} %get-tuple-element.28.refs_2_, f32[256,128]{1,0:T(8,128)} %get-tuple-element.29.refs_3_, ...), custom_call_target="tpu_custom_call" | custom-call | tf_op jit(solution)/shard_map/layer_1/pallas_call | solution.py:606
  328.4 2.3 copy.25
  330.7 1.6 copy.26
  332.3 1.6 copy.27
  (1 shorter events, 0.0 us)

commit v6 on v5

--- a/solution.py
+++ b/solution.py
@@ -12,7 +12,7 @@
 MESH = pl.DeviceIdType.MESH
 VMEM_LIMIT = 67043328
 PLANE = 4
-SUB = 128
+SUB = 64
 N_COL = 4
 N_RING = 12
 
@@ -109,10 +109,10 @@
         return [{'wy': self.at(half, sign)} for half, sign in self.ways]
 
     def place(self, block, start, size):
-        return self.buf.at[lax.div(block, 2), lax.rem(block, 2), pl.ds(start, size)]
+        return self.buf.at[block, pl.ds(start, size)]
 
     def copy(self, kind, num, block, half, quarter, target):
-        rows = self.buf.shape[2]
+        rows = self.buf.shape[1]
         size = rows // 2 if quarter is None else rows // PLANE
         ref = self.place(block, half * (rows // 2) + (quarter or 0) * size, size)
         slot = kind * PLANE + num
@@ -187,62 +187,61 @@
 
 class Exchange:
     def __init__(self, ring, layer, shards, at_a, at_b, send_sem, recv_sem):
-        pos = lax.axis_index('wy')
-        odd = lax.rem(pos, 2)
-        other = pos + 1 - 2 * odd
-        same = odd == ring.core
-        half = ring.n_chip * 2
-        self.ring, self.pos = ring, pos
-        self.send_to = (jnp.where(same, other, pos), jnp.where(same, ring.core, 1 - ring.core))
-        self.recv_from = (jnp.where(same, pos, other), jnp.where(same, 1 - ring.core, ring.core))
-        self.head_to = {'wy': odd * half + (1 - ring.core) * ring.n_chip + ring.chip, 'wx': lax.div(pos, 2)}
-        self.head_from = {
-            'wy': 2 * ring.me + lax.div(pos, half),
-            'wx': lax.rem(pos, ring.n_chip) * 2 + 1 - lax.div(lax.rem(pos, half), ring.n_chip)}
+        self.me, self.n_wx = ring.me, ring.n_chip * 2
+        self.pos = pos = lax.axis_index('wy')
+        self.head_to = {'wy': lax.rem(pos, 2) * self.n_wx + self.turn(self.me), 'wx': lax.div(pos, 2)}
+        self.head_from = {'wy': 2 * self.me + lax.div(pos, self.n_wx), 'wx': self.turn(lax.rem(pos, self.n_wx))}
         self.layer, self.shards = layer, shards
         self.at_a, self.at_b = at_a, at_b
         self.send_sem, self.recv_sem = send_sem, recv_sem
 
+    def turn(self, w):
+        return lax.rem(w + self.n_wx // 2, self.n_wx)
+
+    def others(self):
+        return [lax.rem(self.me + step, self.n_wx) for step in (4, 5, 3, 2, 6, 7, 1)]
+
     def peers(self):
-        wy, core = self.recv_from
-        return [{'wy': wy, 'wx': self.chip(k) * 2 + core} for k in range(self.ring.n_chip)] + [self.head_from]
-
-    def chip(self, step):
-        return lax.rem(self.ring.chip + step, self.ring.n_chip)
-
-    def block(self, which, step, landing):
-        chip = self.chip(step)
-        wy, core = self.send_to
-        origin = chip if landing else self.ring.chip
+        return [{'wx': other} for other in self.others()] + [self.head_from]
+
+    def block(self, which, to, origin):
         gu, d = self.shards[:2]
-        rows = SUB if which else gu.shape[2]
-        src = d.at[self.layer, pl.ds(pl.multiple_of(chip * SUB, SUB), SUB)] if which else gu.at[self.layer, chip]
-        place = self.at_b if which else self.at_a
-        dst = place(self.pos if landing else wy, pl.multiple_of(origin * rows, rows), rows)
-        base = which * self.ring.n_chip
-        return remote(src, dst, self.send_sem.at[base + chip], self.recv_sem.at[base + origin], {'wy': wy, 'wx': chip * 2 + core})
-
-    def heads(self, which, landing):
+        if which:
+            src, place, rows = d.at[self.layer, pl.ds(pl.multiple_of(to * SUB, SUB), SUB)], self.at_b, SUB
+        else:
+            src, place, rows = gu.at[self.layer, to], self.at_a, gu.shape[2]
+        return src, place(self.pos, pl.multiple_of(origin * rows, rows), rows)
+
+    def kept(self, which):
+        return pltpu.make_async_copy(*self.block(which, self.me, self.me), self.send_sem.at[which * self.n_wx + self.me])
+
+    def copies(self, which, landing=False):
+        base = which * self.n_wx
+        found = []
+        for other in self.others():
+            origin = other if landing else self.me
+            src, dst = self.block(which, other, origin)
+            found.append(remote(src, dst, self.send_sem.at[base + other], self.recv_sem.at[base + origin], {'wx': other}))
         gu, d, q, kv, o = self.shards
         unit = self.pos if landing else self.head_to['wy']
+        base = self.n_wx * 2 + which * 2
         if which:
-            parts = [(o, self.at_b(unit, self.ring.n_chip * SUB, o.shape[1]))]
+            parts = [(o, self.at_b(unit, self.n_wx * SUB, o.shape[1]))]
         else:
-            ref = self.at_a(unit, self.ring.n_chip * gu.shape[2], q.shape[1])
-            parts = [(src, ref.at[:, pl.ds(num * SUB, SUB)]) for num, src in enumerate((q, kv))]
-        base = self.ring.n_chip * 2 + which * 2
-        return [remote(src.at[self.layer], dst, self.send_sem.at[base + num], self.recv_sem.at[base + num], self.head_to) for num, (src, dst) in enumerate(parts)]
-
-    def copies(self, which, landing=False):
-        return [self.block(which, step, landing) for step in (1, 3, 2, 0)] + self.heads(which, landing)
+            parts = [(src, self.at_a(unit, (self.n_wx + num) * q.shape[1], q.shape[1])) for num, src in enumerate((q, kv))]
+        for num, (src, dst) in enumerate(parts):
+            found.append(remote(src.at[self.layer], dst, self.send_sem.at[base + num], self.recv_sem.at[base + num], self.head_to))
+        return found
 
     def start(self, which):
+        self.kept(which).start()
         for copy in self.copies(which):
             copy.start()
 
     def land(self, which):
         for copy in self.copies(which, True):
             copy.wait_recv()
+        self.kept(which).wait()
 
     def drain(self, which):
         for copy in self.copies(which):
@@ -252,10 +251,11 @@
 def up_step(hall, wa, mo, narrow, chunks, between):
     d_model = hall.shape[2]
     half = hall.shape[1] // 2
-    n_jj, tile = wa.shape[0], wa.shape[3]
-    half_d = d_model // 2
+    n_unit, tile = wa.shape[0], wa.shape[2]
+    n_w = n_unit // 2
     rows = [(prompt, pl.ds(pl.multiple_of(start, half), half)) for prompt, start in chunks]
     h = jnp.concatenate([hall[prompt, part] for prompt, part in rows], axis=0)
+    low = lax.broadcasted_iota(jnp.int32, (h.shape[0], tile), 1) < SUB
 
     def project(weight):
         return jnp.dot(h, weight, preferred_element_type=jnp.float32).astype(jnp.bfloat16)
@@ -265,16 +265,22 @@
             ref[prompt, part, lo:lo + value.shape[1]] = value[num * half:(num + 1) * half]
 
     for hh in range(2):
-        keep(project(wa[hh * n_jj // 2:(hh + 1) * n_jj // 2, :, half_d:, :].reshape(d_model, tile)), narrow, hh * tile)
-    for jj in range(0, n_jj, 2):
-        if jj == n_jj // 2:
+        sides = []
+        for num in range(2):
+            lo = d_model + num * d_model // n_w
+            parts = [wa[hh * n_w + k:hh * n_w + k + n_w // 2, lo:lo + d_model // n_w, :].reshape(d_model // 2, tile) for k in (n_w // 2, 0)]
+            sides.append(jnp.concatenate(parts, axis=0))
+        keep(project(jnp.concatenate(sides, axis=1)), narrow, hh * 2 * tile)
+    for first in range(0, n_unit, PLANE):
+        if first == n_w:
             between()
-        weight = jnp.concatenate([wa[jj + k, :, :half_d, :].reshape(d_model, tile) for k in range(2)], axis=1)
-        both = project(weight)
-        for k in range(2):
-            g_f, u_f = (both[:, k * tile + part * SUB:k * tile + (part + 1) * SUB].astype(jnp.float32) for part in range(2))
+        both = project(jnp.concatenate([wa[first + k, :d_model, :] for k in range(PLANE)], axis=1))
+        for k in range(0, PLANE, 2):
+            one, two = (both[:, part * tile:(part + 1) * tile].astype(jnp.float32) for part in (k, k + 1))
+            g_f = jnp.where(low, one, pltpu.roll(two, SUB, 1))
+            u_f = jnp.where(low, pltpu.roll(one, SUB, 1), two)
             hidden = g_f * (1.0 / (1.0 + jnp.exp(-g_f))) * u_f
-            keep(hidden.astype(jnp.bfloat16), mo, (jj + k) * SUB)
+            keep(hidden.astype(jnp.bfloat16), mo, (first + k) * SUB)
 
 
 def attend(narrow, mo, kv_out, xt, cos, sin):
@@ -323,7 +329,8 @@
         return remote(self.acc.at[k], self.landed.at[k], self.ring_send.at[k], self.ring_recv.at[k], {'wx': target})
 
     def products(self, k):
-        n_jj, tile = self.wb.shape[0], self.wb.shape[3]
+        n_unit, rows, tile = self.wb.shape
+        n_w = n_unit // 2
         phase, j = lax.div(k, N_COL), lax.rem(k, N_COL)
         odd, slot = lax.rem(j, 2), lax.div(j, 2)
         own = phase == 3
@@ -331,14 +338,13 @@
         q = jnp.where(own, j, jnp.where(phase == 1, 1 - odd, odd) * 2 + slot)
         xt = lax.rem(self.ring.chip + off, self.ring.n_chip)
 
-        def columns(side):
-            parts = [self.wb[:, side, pl.ds(pl.multiple_of(q * SUB, SUB), SUB), :].reshape(n_jj * SUB, tile)]
+        def columns(w):
+            parts = [self.wb[:, pl.ds(pl.multiple_of(w * SUB, SUB), SUB), :].reshape(n_unit * SUB, tile)]
             for hh in range(2):
-                unit = hh * n_jj + side * N_COL + q
-                parts.append(self.wb[lax.div(unit, 2), lax.rem(unit, 2), N_COL * SUB:, :])
+                parts.append(self.wb[hh * n_w + lax.rem(w + n_w // 2, n_w), n_w * SUB:, :])
             return jnp.concatenate(parts, axis=0)
 
-        weight = jnp.concatenate([columns(1), columns(0)], axis=1)
+        weight = jnp.concatenate([columns(2 * q), columns(2 * q + 1)], axis=1)
 
         def product(core):
             return jnp.dot(self.mo[xt * 2 + core], weight, preferred_element_type=jnp.float32)
@@ -436,7 +442,7 @@
         peers += swap_0.peers()
     else:
         here = gather_b.here
-        b_load = pltpu.make_async_copy(b_ref, wb.at[lax.div(here, 2), lax.rem(here, 2)], w_sem.at[0])
+        b_load = pltpu.make_async_copy(b_ref, wb.at[here], w_sem.at[0])
         a_load = pltpu.make_async_copy(wa_ref, wa, w_sem.at[1])
         old_loads = [pltpu.make_async_copy(ref, kv.at[2, 0, num], old_sem.at[num]) for num, ref in enumerate((k_ref, v_ref))]
         for load in (b_load, a_load, *old_loads):
@@ -449,11 +455,7 @@
     centered = resid_f - jnp.mean(resid_f, axis=-1, keepdims=True)
     variance = jnp.mean(centered * centered, axis=-1, keepdims=True)
     normed = (centered * lax.rsqrt(variance + LN_EPS) * gamma_ref[1 - first:2 - first, :]).astype(jnp.bfloat16)
-    tile = normed.shape[1] // n_wx
-    for w in range(n_wx):
-        lo = ((1 - w % 2) * ring.n_chip + w // 2) * tile
-        hall[ring.me, :, lo:lo + tile] = normed[:, w * tile:(w + 1) * tile]
-
+    hall[ring.me] = normed
     pl.semaphore_wait(barrier, len(peers))
     if first:
         swap_0.start(0)
@@ -575,15 +577,15 @@
     col = d_model // N_COL
     any_spec, vmem_spec = pl.BlockSpec(memory_space=pl.ANY), pl.BlockSpec(memory_space=pltpu.VMEM)
     tile = d_model // n_wx
-    unit_b = (PLANE * SUB + head_dim, tile)
-    wa_shape = (n_unit // 2, 2, (PLANE + 1) * tile, tile)
-    wb_shape = (n_unit // 2, 2) + unit_b
+    unit_b = (n_wx * SUB + head_dim, tile)
+    wa_shape = (n_unit, d_model + 2 * tile, 2 * SUB)
+    wb_shape = (n_unit,) + unit_b
     piece = (seq, col)
     n_piece = 4 * N_COL
     dma = pltpu.SemaphoreType.DMA
     cache = (seq, head_dim) if first else (2, seq, head_dim)
     out_shape = [jax.ShapeDtypeStruct(shape, jnp.bfloat16) for shape in (resid.shape, cache, cache)]
-    n_plane, n_swap, n_hop = dma((40,)), dma((11,)), dma((13,))
+    n_plane, n_swap, n_hop = dma((40,)), dma((19,)), dma((13,))
     if first:
         out_shape += [jax.ShapeDtypeStruct(shape, jnp.bfloat16) for shape in (wa_shape, unit_b)]
         scratch = [n_plane, n_plane, n_swap, n_swap, n_swap, n_swap, n_plane, n_plane]
@@ -593,7 +595,7 @@
         pltpu.VMEM((n_wx, seq, d_model), jnp.bfloat16),
         pltpu.VMEM(wa_shape, jnp.bfloat16),
         pltpu.VMEM(wb_shape, jnp.bfloat16),
-        pltpu.VMEM((n_wx, seq, n_unit // 2 * SUB + 2 * head_dim), jnp.bfloat16),
+        pltpu.VMEM((n_wx, seq, n_unit * SUB + 2 * head_dim), jnp.bfloat16),
         pltpu.VMEM((n_wx, seq, 4 * head_dim), jnp.bfloat16),
         pltpu.VMEM((3, 2, 2, seq, head_dim), jnp.bfloat16),
         n_hop, n_hop, n_plane, n_plane, dma((4,)),
@@ -614,6 +616,32 @@
     )(resid, gamma, cos, sin, *weights)
 
 
+def settle_kernel(*refs):
+    n = len(refs) // 3
+    srcs, dsts, held, sem = refs[:n], refs[n:2 * n], refs[2 * n:3 * n], refs[-1]
+    loads = [pltpu.make_async_copy(src, mid, sem.at[num]) for num, (src, mid) in enumerate(zip(srcs, held))]
+    stores = [pltpu.make_async_copy(mid, dst, sem.at[n + num]) for num, (mid, dst) in enumerate(zip(held, dsts))]
+    for load in loads:
+        load.start()
+    for load, store in zip(loads, stores):
+        load.wait()
+        store.start()
+    for store in stores:
+        store.wait()
+
+
+def settle(arrays):
+    n = len(arrays)
+    return pl.pallas_call(
+        settle_kernel,
+        out_shape=tuple(jax.ShapeDtypeStruct(a.shape, a.dtype) for a in arrays),
+        in_specs=[pl.BlockSpec(memory_space=pl.ANY)] * n,
+        out_specs=[pl.BlockSpec(memory_space=pl.ANY)] * n,
+        scratch_shapes=[pltpu.VMEM(a.shape, a.dtype) for a in arrays] + [pltpu.SemaphoreType.DMA((2 * n,))],
+        name='settle',
+    )(*arrays)
+
+
 def solution(mesh):
     batch_axes = ('dp', 'wy', 'wx')
     in_specs = (P(batch_axes), P(), P(None, 'wx', 'wy'), P(None, 'wx'), P(None, 'wx', None, 'wy'), P(None, 'wy', 'wx'), P(None, 'wy', 'wx'))
@@ -624,9 +652,9 @@
         n_layers, d_loc = w_q.shape[:2]
         cos_tab, sin_tab = rope_tables(x_tokens.shape[1], w_kv.shape[-1])
         kv_half = lax.dynamic_index_in_dim(w_kv, lax.rem(lax.axis_index('wy'), 2), axis=2, keepdims=False)
-        gu = jnp.transpose(w_gu.reshape(n_layers, d_loc, 2, n_wx // 2, SUB), (0, 3, 1, 2, 4)).reshape(n_layers, n_wx // 2, d_loc, 2 * SUB)
+        gu = jnp.transpose(w_gu.reshape(n_layers, d_loc, 2, n_wx, SUB), (0, 3, 1, 2, 4)).reshape(n_layers, n_wx, d_loc, 2 * SUB)
         resid, k_0, v_0, wa, unit_b = layer(x_tokens[0], gamma_ln, cos_tab, sin_tab, (gu, w_d, w_q, kv_half, w_o), n_wx, True)
-        resid, k_all, v_all = layer(resid, gamma_ln, cos_tab, sin_tab, (wa, unit_b, k_0, v_0), n_wx, False)
+        resid, k_all, v_all = settle(layer(resid, gamma_ln, cos_tab, sin_tab, (wa, unit_b, k_0, v_0), n_wx, False))
         return resid[None], k_all[:, None], v_all[:, None]
 
     return jax.shard_map(device_step, mesh=mesh, in_specs=in_specs, out_specs=out_specs, check_vma=False)

time: 334 us -> 325 us (0.973)
  local copies, waits for them, and re-layouts: 10.8 us -> 5.73 us
  Pallas kernels: 321 us -> 317 us
    pallas_call x2, Pallas kernels: 321 us -> 315 us  [layer(): pl.pallas_call(functools.partial(layer_kernel, n_wx, first), out_shape=tu...]
where the time goes in v6:
time: 325 us
  Pallas kernels  317 us (98%)
  local copies, waits for them, and re-layouts  5.73 us (2%)
    pallas_call x2, Pallas kernels, layer(): pl.pallas_call(functools.partial(layer_kernel, n_wx, first), out_shape=tu...  315 us

profile of v6, /device:TPU:1, one launch (start us, length us, event | category | flops | bytes accessed | tf_op | source)
XLA Modules:
  0.0 325.0 jit_solution(4120390766205357391)
XLA Ops:
  0.7 1.2 constant_dynamic-slice_fusion
  1.9 0.7 copy.21
  2.6 0.5 fusion.2
  3.1 0.8 pad_maximum_fusion
  3.9 2.4 copy.13
  6.3 0.1 copy.14
  6.4 1.3 copy.16.refs_4_
  7.7 195.2 %layer_0.1 = (bf16[256,2048]{1,0:T(8,128)(2,1)}, bf16[256,128]{1,0:T(8,128)(2,1)}, bf16[256,128]{1,0:T(8,128)(2,1)}, bf16[16,2560,128]{2,1,0:T(8,128)(2,1)}, bf16[640,256]{1,0:T(8,128)(2,1)}) custom-call(bf16[256,2048]{1,0:T(8,128)(2,1)} %bitcast.17, f32[2,2048]{1,0:T(2,128)} %refs_1_.3, f32[256,128]{1,0:T(8,128)} %get-tuple-element.34.refs_2_, ...), custom_call_target="tpu_custom_call" | custom-call | tf_op jit(solution)/shard_map/layer_0/pallas_call | solution.py:608
  202.9 119.6 %layer_1.1 = (bf16[256,2048]{1,0:T(8,128)(2,1)}, bf16[2,256,128]{2,1,0:T(8,128)(2,1)}, bf16[2,256,128]{2,1,0:T(8,128)(2,1)}) custom-call(bf16[256,2048]{1,0:T(8,128)(2,1)} %get-tuple-element.14.refs_0_, f32[2,2048]{1,0:T(2,128)} %refs_1_.3, f32[256,128]{1,0:T(8,128)} %get-tuple-element.34.refs_2_, f32[256,128]{1,0:T(8,128)} %get-tuple-element.35.refs_3_, ...), custom_call_target="tpu_custom_call" | custom-call | tf_op jit(solution)/shard_map/layer_1/pallas_call | solution.py:608
  322.5 2.3 settle.1
  (1 shorter events, 0.0 us)

commit v7 on v6

--- a/solution.py
+++ b/solution.py
@@ -227,8 +227,13 @@
         base = self.n_wx * 2 + which * 2
         if which:
             parts = [(o, self.at_b(unit, self.n_wx * SUB, o.shape[1]))]
+            if self.layer == 0:
+                both = self.at_b(unit, self.n_wx * SUB + o.shape[1], q.shape[1])
+                parts += [(src, both.at[:, pl.ds(num * q.shape[2], q.shape[2])]) for num, src in enumerate((q, kv))]
+        elif self.layer:
+            parts = [(src, self.at_a(unit, (self.n_wx + num) * q.shape[1], q.shape[1])) for num, src in enumerate((q, kv))]
         else:
-            parts = [(src, self.at_a(unit, (self.n_wx + num) * q.shape[1], q.shape[1])) for num, src in enumerate((q, kv))]
+            parts = []
         for num, (src, dst) in enumerate(parts):
             found.append(remote(src.at[self.layer], dst, self.send_sem.at[base + num], self.recv_sem.at[base + num], self.head_to))
         return found
@@ -248,7 +253,7 @@
             copy.wait_send()
 
 
-def up_step(hall, wa, mo, narrow, chunks, between):
+def up_step(hall, wa, mo, chunks, between):
     d_model = hall.shape[2]
     half = hall.shape[1] // 2
     n_unit, tile = wa.shape[0], wa.shape[2]
@@ -264,13 +269,6 @@
         for num, (prompt, part) in enumerate(rows):
             ref[prompt, part, lo:lo + value.shape[1]] = value[num * half:(num + 1) * half]
 
-    for hh in range(2):
-        sides = []
-        for num in range(2):
-            lo = d_model + num * d_model // n_w
-            parts = [wa[hh * n_w + k:hh * n_w + k + n_w // 2, lo:lo + d_model // n_w, :].reshape(d_model // 2, tile) for k in (n_w // 2, 0)]
-            sides.append(jnp.concatenate(parts, axis=0))
-        keep(project(jnp.concatenate(sides, axis=1)), narrow, hh * 2 * tile)
     for first in range(0, n_unit, PLANE):
         if first == n_w:
             between()
@@ -281,6 +279,29 @@
             u_f = jnp.where(low, pltpu.roll(one, SUB, 1), two)
             hidden = g_f * (1.0 / (1.0 + jnp.exp(-g_f))) * u_f
             keep(hidden.astype(jnp.bfloat16), mo, (first + k) * SUB)
+
+
+def head_weight(first, wa, wb, hh, d_model):
+    n_w = wa.shape[0] // 2
+    rows = d_model // n_w
+    turned = [hh * n_w + k for k in (n_w // 2, 0)]
+
+    def piece(ref, lo):
+        return jnp.concatenate([ref[unit:unit + n_w // 2, lo:lo + rows, :].reshape(d_model // 2, ref.shape[2]) for unit in turned], axis=0)
+
+    if first:
+        return piece(wb, wb.shape[1] - rows)
+    return jnp.concatenate([piece(wa, d_model + num * rows) for num in range(2)], axis=1)
+
+
+def head_step(first, hall, wa, wb, narrow, chunks):
+    half, d_model = hall.shape[1] // 2, hall.shape[2]
+    rows = [(prompt, pl.ds(pl.multiple_of(start, half), half)) for prompt, start in chunks]
+    h = jnp.concatenate([hall[prompt, part] for prompt, part in rows], axis=0)
+    for hh in range(2):
+        value = jnp.dot(h, head_weight(first, wa, wb, hh, d_model), preferred_element_type=jnp.float32).astype(jnp.bfloat16)
+        for num, (prompt, part) in enumerate(rows):
+            narrow[prompt, part, hh * value.shape[1]:(hh + 1) * value.shape[1]] = value[num * half:(num + 1) * half]
 
 
 def attend(narrow, mo, kv_out, xt, cos, sin):
@@ -341,7 +362,7 @@
         def columns(w):
             parts = [self.wb[:, pl.ds(pl.multiple_of(w * SUB, SUB), SUB), :].reshape(n_unit * SUB, tile)]
             for hh in range(2):
-                parts.append(self.wb[hh * n_w + lax.rem(w + n_w // 2, n_w), n_w * SUB:, :])
+                parts.append(self.wb[hh * n_w + lax.rem(w + n_w // 2, n_w), n_w * SUB:n_w * SUB + 2 * SUB, :])
             return jnp.concatenate(parts, axis=0)
 
         weight = jnp.concatenate([columns(2 * q), columns(2 * q + 1)], axis=1)
@@ -486,63 +507,76 @@
     seq = hall.shape[1]
     half = seq // 2
 
-    def body(step, carry):
-        turn = lax.rem(step + 1, PLANE) if first else step
-
+    def whole(xt):
+        return [(xt * 2 + b, start) for start in (0, half) for b in range(2)]
+
+    def attend_to(off):
+        xt = lax.rem(ring.chip + off, ring.n_chip)
+        attend(narrow, mo, kv.at[jnp.where(off == 0, 0, 1)], xt, cos_ref[...], sin_ref[...])
+
+    def at_step(step):
         def when(num, *calls):
             @pl.when(step == num)
             def _():
                 for call in calls:
                     call()
 
-        if first:
-            when(1, gather_b.stage_1)
-            when(2, gather_b.stage_3)
-        else:
-            when(0, lambda: gather_h.wait(0))
-            when(1, gather_b.stage_1, gather_h.near_halves, gather_b.stage_2, lambda: gather_h.wait(7, 8))
-            when(2, gather_b.stage_3, gather_h.near_rest, gather_b.stage_4, lambda: gather_h.wait(9, 10))
-            when(3, gather_h.far_halves, lambda: gather_h.wait(11, 12))
-
-        def between():
-            if first:
-                when(1, gather_b.stage_2)
-                when(2, gather_b.stage_4)
-                when(3, gather_n.stage_1)
-            else:
-                when(2, gather_b.stage_5)
-
-        near = (turn == 1) | (turn == 2)
-        lone = jnp.where(turn == 0, ring.chip, lax.rem(ring.chip + 2, ring.n_chip))
+        return when
+
+    def wide(step, carry):
+        when = at_step(step)
+        when(1, gather_b.stage_1)
+        when(2, gather_b.stage_3)
+        when(3, gather_b.stage_4)
+        up_step(hall, wa, mo, whole(step), lambda: when(1, gather_b.stage_2))
+        return carry
+
+    def heads(num, carry):
+        when = at_step(num)
+        when(1, gather_n.stage_1)
+        when(3, gather_n.stage_2)
+        off = jnp.where(num == 0, 2, jnp.where(num == 1, 3, jnp.where(num == 2, 1, 0)))
+        head_step(first, hall, wa, wb, narrow, whole(lax.rem(ring.chip + off, ring.n_chip)))
+        attend_to(off)
+        lo = jnp.where(num == 3, 2 * N_COL, jnp.where(num == 2, N_COL, 0))
+        scatter.run(lo, jnp.where(num == 3, 4 * N_COL, jnp.where(num == 1, 0, lo + N_COL)))
+        return carry
+
+    def body(step, carry):
+        when = at_step(step)
+        when(0, lambda: gather_h.wait(0))
+        when(1, gather_b.stage_1, gather_h.near_halves, gather_b.stage_2, lambda: gather_h.wait(7, 8))
+        when(2, gather_b.stage_3, gather_h.near_rest, gather_b.stage_4, lambda: gather_h.wait(9, 10))
+        when(3, gather_h.far_halves, lambda: gather_h.wait(11, 12))
+        near = (step == 1) | (step == 2)
+        lone = jnp.where(step == 0, ring.chip, lax.rem(ring.chip + 2, ring.n_chip))
         one = jnp.where(near, lax.div(ring.left, 2), lone)
         two = jnp.where(near, lax.div(ring.right, 2), lone)
-        start = jnp.where(turn == 2, half, 0)
-        up_step(hall, wa, mo, narrow, [(one * 2 + b, start) for b in range(2)] + [(two * 2 + b, half - start) for b in range(2)], between)
+        start = jnp.where(step == 2, half, 0)
+        chunks = [(one * 2 + b, start) for b in range(2)] + [(two * 2 + b, half - start) for b in range(2)]
+        head_step(first, hall, wa, wb, narrow, chunks)
+        up_step(hall, wa, mo, chunks, lambda: when(2, gather_b.stage_5))
 
         def attention(num, carry):
-            place = lax.rem(num + 1, PLANE) if first else num
-            off = jnp.where(place == 0, 0, jnp.where(place == 1, 3, jnp.where(place == 2, 1, 2)))
-            attend(narrow, mo, kv.at[jnp.where(place == 0, 0, 1)], lax.rem(ring.chip + off, ring.n_chip), cos_ref[...], sin_ref[...])
+            attend_to(jnp.where(num == 0, 0, jnp.where(num == 1, 3, jnp.where(num == 2, 1, 2))))
             return carry
 
-        early = 0 if first else 1
-        lo = jnp.where(step == 3, 3, jnp.where(step == 2, 2 - early, 0))
-        if first:
-            hi = jnp.where(step == 0, 0, step + 1)
-            lo = jnp.where(step == 2, 2, lo)
-        else:
-            lo, hi = jnp.where(step == 1, 1, lo), jnp.where(step < 2, 1, step + 1)
-        lax.fori_loop(lo, hi, attention, 0)
-        if first:
-            when(2, gather_b.stage_5, gather_b.finish, lambda: swap_1.land(0), gather_n.start)
-        else:
-            when(2, gather_b.finish)
-        split = 2 * N_COL if first else N_COL
+        lo = jnp.where(step == 3, 3, jnp.where(step == 0, 0, 1))
+        lax.fori_loop(lo, jnp.where(step < 2, 1, step + 1), attention, 0)
+        when(2, gather_b.finish)
         last = step == 3
-        scatter.run(jnp.where(last, split, 0), jnp.where(last, 4 * N_COL, jnp.where(step == 2, split, 0)))
+        scatter.run(jnp.where(last, N_COL, 0), jnp.where(last, 4 * N_COL, jnp.where(step == 2, N_COL, 0)))
         return carry
 
-    lax.fori_loop(0, ring.n_chip, body, 0)
+    if first:
+        lax.fori_loop(0, ring.n_chip, wide, 0)
+        gather_b.stage_5()
+        gather_b.finish()
+        swap_1.land(0)
+        gather_n.start()
+        lax.fori_loop(0, ring.n_chip, heads, 0)
+    else:
+        lax.fori_loop(0, ring.n_chip, body, 0)
     if first:
         caches = [(kv.at[0, ring.core, num], ref) for num, ref in enumerate((k_out, v_out))]
     else:
@@ -554,7 +588,7 @@
     for cache in caches:
         cache.start()
     if first:
-        scatter.finish(resid_ref, out_ref, (gather_n.stage_2, gather_n.stage_3, gather_n.stage_4, gather_n.stage_5))
+        scatter.finish(resid_ref, out_ref, (lambda: None, gather_n.stage_3, gather_n.stage_4, gather_n.stage_5))
         gather_n.finish()
         swap_1.land(1)
         for swap in (swap_0, swap_1):
@@ -578,16 +612,17 @@
     any_spec, vmem_spec = pl.BlockSpec(memory_space=pl.ANY), pl.BlockSpec(memory_space=pltpu.VMEM)
     tile = d_model // n_wx
     unit_b = (n_wx * SUB + head_dim, tile)
-    wa_shape = (n_unit, d_model + 2 * tile, 2 * SUB)
-    wb_shape = (n_unit,) + unit_b
+    next_shape = (n_unit, d_model + 2 * tile, 2 * SUB)
+    wa_shape = (n_unit, d_model, 2 * SUB) if first else next_shape
+    wb_shape = (n_unit, unit_b[0] + (tile if first else 0), tile)
     piece = (seq, col)
     n_piece = 4 * N_COL
     dma = pltpu.SemaphoreType.DMA
     cache = (seq, head_dim) if first else (2, seq, head_dim)
     out_shape = [jax.ShapeDtypeStruct(shape, jnp.bfloat16) for shape in (resid.shape, cache, cache)]
-    n_plane, n_swap, n_hop = dma((40,)), dma((19,)), dma((13,))
-    if first:
-        out_shape += [jax.ShapeDtypeStruct(shape, jnp.bfloat16) for shape in (wa_shape, unit_b)]
+    n_plane, n_swap, n_hop = dma((40,)), dma((21,)), dma((13,))
+    if first:
+        out_shape += [jax.ShapeDtypeStruct(shape, jnp.bfloat16) for shape in (next_shape, unit_b)]
         scratch = [n_plane, n_plane, n_swap, n_swap, n_swap, n_swap, n_plane, n_plane]
     else:
         scratch = [dma((2,)), dma((2,))]

time: 325 us -> 324 us (level)
  no operation moved by 1% of the time
where the time goes in v7:
time: 324 us
  Pallas kernels  316 us (98%)
  local copies, waits for them, and re-layouts  5.73 us (2%)
    pallas_call x2, Pallas kernels, layer(): pl.pallas_call(functools.partial(layer_kernel, n_wx, first), out_shape=tu...  314 us

profile of v7, /device:TPU:1, one launch (start us, length us, event | category | flops | bytes accessed | tf_op | source)
XLA Modules:
  0.0 324.2 jit_solution(12403723070083473529)
XLA Ops:
  0.7 1.2 constant_dynamic-slice_fusion
  1.9 0.7 copy.21
  2.6 0.5 fusion.2
  3.1 0.8 pad_maximum_fusion
  3.9 2.4 copy.13
  6.3 0.1 copy.14
  6.4 1.3 copy.16.refs_4_
  7.7 196.3 %layer_0.1 = (bf16[256,2048]{1,0:T(8,128)(2,1)}, bf16[256,128]{1,0:T(8,128)(2,1)}, bf16[256,128]{1,0:T(8,128)(2,1)}, bf16[16,2560,128]{2,1,0:T(8,128)(2,1)}, bf16[640,256]{1,0:T(8,128)(2,1)}) custom-call(bf16[256,2048]{1,0:T(8,128)(2,1)} %bitcast.17, f32[2,2048]{1,0:T(2,128)} %refs_1_.3, f32[256,128]{1,0:T(8,128)} %get-tuple-element.34.refs_2_, ...), custom_call_target="tpu_custom_call" | custom-call | tf_op jit(solution)/shard_map/layer_0/pallas_call | solution.py:643
  204.1 117.6 %layer_1.1 = (bf16[256,2048]{1,0:T(8,128)(2,1)}, bf16[2,256,128]{2,1,0:T(8,128)(2,1)}, bf16[2,256,128]{2,1,0:T(8,128)(2,1)}) custom-call(bf16[256,2048]{1,0:T(8,128)(2,1)} %get-tuple-element.14.refs_0_, f32[2,2048]{1,0:T(2,128)} %refs_1_.3, f32[256,128]{1,0:T(8,128)} %get-tuple-element.34.refs_2_, f32[256,128]{1,0:T(8,128)} %get-tuple-element.35.refs_3_, ...), custom_call_target="tpu_custom_call" | custom-call | tf_op jit(solution)/shard_map/layer_1/pallas_call | solution.py:643
  321.7 2.3 settle.1
  (1 shorter events, 0.0 us)

commit v8 on v7

--- a/solution.py
+++ b/solution.py
@@ -489,8 +489,6 @@
         gather_a.stage_2()
         gather_a.stage_3()
         gather_h.near_rest()
-        swap_1.start(0)
-        swap_1.start(1)
         gather_a.stage_4()
         gather_h.far_halves()
         gather_a.stage_5()
@@ -526,7 +524,7 @@
     def wide(step, carry):
         when = at_step(step)
         when(1, gather_b.stage_1)
-        when(2, gather_b.stage_3)
+        when(2, gather_b.stage_3, lambda: swap_1.start(0), lambda: swap_1.start(1))
         when(3, gather_b.stage_4)
         up_step(hall, wa, mo, whole(step), lambda: when(1, gather_b.stage_2))
         return carry

time: 324 us -> 324 us (level)
  no operation moved by 1% of the time
where the time goes in v8:
time: 324 us
  Pallas kernels  316 us (98%)
  local copies, waits for them, and re-layouts  5.73 us (2%)
    pallas_call x2, Pallas kernels, layer(): pl.pallas_call(functools.partial(layer_kernel, n_wx, first), out_shape=tu...  313 us

profile of v8, /device:TPU:1, one launch (start us, length us, event | category | flops | bytes accessed | tf_op | source)
XLA Modules:
  0.0 323.7 jit_solution(9957934650332348184)
XLA Ops:
  0.7 1.2 constant_dynamic-slice_fusion
  1.9 0.7 copy.21
  2.6 0.5 fusion.2
  3.1 0.8 pad_maximum_fusion
  3.9 2.4 copy.13
  6.3 0.1 copy.14
  6.4 1.3 copy.16.refs_4_
  7.7 194.1 %layer_0.1 = (bf16[256,2048]{1,0:T(8,128)(2,1)}, bf16[256,128]{1,0:T(8,128)(2,1)}, bf16[256,128]{1,0:T(8,128)(2,1)}, bf16[16,2560,128]{2,1,0:T(8,128)(2,1)}, bf16[640,256]{1,0:T(8,128)(2,1)}) custom-call(bf16[256,2048]{1,0:T(8,128)(2,1)} %bitcast.17, f32[2,2048]{1,0:T(2,128)} %refs_1_.3, f32[256,128]{1,0:T(8,128)} %get-tuple-element.34.refs_2_, ...), custom_call_target="tpu_custom_call" | custom-call | tf_op jit(solution)/shard_map/layer_0/pallas_call | solution.py:641
  201.8 119.4 %layer_1.1 = (bf16[256,2048]{1,0:T(8,128)(2,1)}, bf16[2,256,128]{2,1,0:T(8,128)(2,1)}, bf16[2,256,128]{2,1,0:T(8,128)(2,1)}) custom-call(bf16[256,2048]{1,0:T(8,128)(2,1)} %get-tuple-element.14.refs_0_, f32[2,2048]{1,0:T(2,128)} %refs_1_.3, f32[256,128]{1,0:T(8,128)} %get-tuple-element.34.refs_2_, f32[256,128]{1,0:T(8,128)} %get-tuple-element.35.refs_3_, ...), custom_call_target="tpu_custom_call" | custom-call | tf_op jit(solution)/shard_map/layer_1/pallas_call | solution.py:641
  321.2 2.3 settle.1
  (1 shorter events, 0.0 us)
